TPU v7x, 8 devices: a whole 2x2x1 slice. The times are simulated.
8 devices in a mesh: dp: 2 (over z, y), cp: 4 (over x, core).
Axes of the slice: x: 2, y: 2, z: 1, core: 2. Of those that a mesh axis runs over, the one named last changes fastest.
Arguments:
- hidden: bfloat16 [64, 32, 1024], P('dp'), parts along dimension 0
- memory: bfloat16 [64, 1500, 1024], P('dp', 'cp'), parts along dimension 0
- ln_gain: bfloat16 [1024], replicated
- ln_bias: bfloat16 [1024], replicated
- w_q: bfloat16 [1024, 1024], replicated
- b_q: bfloat16 [1024], replicated
- w_k: bfloat16 [1024, 1024], replicated
- w_v: bfloat16 [1024, 1024], replicated
- b_v: bfloat16 [1024], replicated
- w_o: bfloat16 [1024, 1024], replicated
- b_o: bfloat16 [1024], replicated
- grad_y: bfloat16 [64, 32, 1024], P('dp'), parts along dimension 0
Outputs:
- output 1: bfloat16 [64, 32, 1024], P('dp'), parts along dimension 0
- output 2: bfloat16 [64, 32, 1024], P('dp'), parts along dimension 0
- output 3: bfloat16 [64, 1500, 1024], P('dp', 'cp'), parts along dimension 0
- output 4: float32 [2048], P('dp'), parts along dimension 0
- output 5: float32 [2048], P('dp'), parts along dimension 0
- output 6: float32 [2048, 1024], P('dp'), parts along dimension 0
- output 7: float32 [2048], P('dp'), parts along dimension 0
- output 8: float32 [2048, 1024], P('dp'), parts along dimension 0
- output 9: float32 [2048, 1024], P('dp'), parts along dimension 0
- output 10: float32 [2048], P('dp'), parts along dimension 0
- output 11: float32 [2048, 1024], P('dp'), parts along dimension 0
- output 12: float32 [2048], P('dp'), parts along dimension 0
There are 2 independent parts. A program takes and returns all parts, laid end to end along the dimension named above; an argument that names none is the same for every part.
All inputs are finite; a program needn't handle non-finite values.
Results may differ from a plain program's by a relative error of at most 0.00976617.
Values are sent between devices in bfloat16 or wider.
A program may use at most 1 GiB of HBM per device.

v0:
```python
import jax
import jax.numpy as jnp
from jax import lax
from jax.sharding import PartitionSpec as P

EPS = 1e-5
HEAD = 64


def solution(mesh):
    act_spec = P("dp", None, None)
    mem_spec = P("dp", "cp", None)
    vec_out = P("dp")
    mat_out = P("dp", None)
    in_specs = (act_spec, mem_spec, P(), P(), P(), P(), P(), P(), P(), P(), P(), act_spec)
    out_specs = (act_spec, act_spec, mem_spec, vec_out, vec_out, mat_out, vec_out, mat_out, mat_out, vec_out, mat_out, vec_out)

    def device_step(hidden, memory, ln_gain, ln_bias, w_q, b_q, w_k, w_v, b_v, w_o, b_o, grad_y):
        n_batch, n_tokens, n_width = hidden.shape
        n_frames = memory.shape[1]
        n_heads = n_width // HEAD
        logit_scale = HEAD ** -0.5
        hidden_f32 = hidden.astype(jnp.float32)
        centered = hidden_f32 - jnp.mean(hidden_f32, axis=-1, keepdims=True)
        inv_std = lax.rsqrt(jnp.mean(centered * centered, axis=-1, keepdims=True) + EPS)
        x_hat = centered * inv_std
        gain_f32 = ln_gain.astype(jnp.float32)
        x_norm = (x_hat * gain_f32 + ln_bias.astype(jnp.float32)).astype(jnp.bfloat16)
        q_proj = (jnp.einsum("btd,de->bte", x_norm, w_q, preferred_element_type=jnp.float32) + b_q.astype(jnp.float32)).astype(jnp.bfloat16)
        k_proj = jnp.einsum("bfd,de->bfe", memory, w_k, preferred_element_type=jnp.float32).astype(jnp.bfloat16)
        v_proj = (jnp.einsum("bfd,de->bfe", memory, w_v, preferred_element_type=jnp.float32) + b_v.astype(jnp.float32)).astype(jnp.bfloat16)
        q_heads = q_proj.reshape(n_batch, n_tokens, n_heads, HEAD)
        k_heads = k_proj.reshape(n_batch, n_frames, n_heads, HEAD)
        v_heads = v_proj.reshape(n_batch, n_frames, n_heads, HEAD)
        logits = jnp.einsum("bthe,bfhe->bhtf", q_heads, k_heads, preferred_element_type=jnp.float32) * logit_scale
        row_max = lax.pmax(jnp.max(logits, axis=-1, keepdims=True), "cp")
        exp_logits = jnp.exp(logits - row_max)
        row_total = lax.psum(jnp.sum(exp_logits, axis=-1, keepdims=True), "cp")
        attn_probs = exp_logits / row_total
        probs_low = attn_probs.astype(jnp.bfloat16)
        attn_sum = lax.psum(jnp.einsum("bhtf,bfhe->bthe", probs_low, v_heads, preferred_element_type=jnp.float32), "cp")
        attn_out = attn_sum.reshape(n_batch, n_tokens, n_width).astype(jnp.bfloat16)
        out_y = (hidden_f32 + jnp.einsum("btd,de->bte", attn_out, w_o, preferred_element_type=jnp.float32) + b_o.astype(jnp.float32)).astype(jnp.bfloat16)

        grad_wo = jnp.einsum("btd,bte->de", attn_out, grad_y, preferred_element_type=jnp.float32)
        grad_bo = jnp.sum(grad_y, axis=(0, 1), dtype=jnp.float32)
        d_attn = jnp.einsum("bte,de->btd", grad_y, w_o, preferred_element_type=jnp.float32).astype(jnp.bfloat16)
        d_heads = d_attn.reshape(n_batch, n_tokens, n_heads, HEAD)
        d_probs = jnp.einsum("bthe,bfhe->bhtf", d_heads, v_heads, preferred_element_type=jnp.float32)
        row_dot = lax.psum(jnp.sum(attn_probs * d_probs, axis=-1, keepdims=True), "cp")
        d_logits = (attn_probs * (d_probs - row_dot) * logit_scale).astype(jnp.bfloat16)
        grad_q = lax.psum(jnp.einsum("bhtf,bfhe->bthe", d_logits, k_heads, preferred_element_type=jnp.float32), "cp").reshape(n_batch, n_tokens, n_width)
        grad_k = jnp.einsum("bhtf,bthe->bfhe", d_logits, q_heads, preferred_element_type=jnp.float32).reshape(n_batch, n_frames, n_width).astype(jnp.bfloat16)
        grad_v = jnp.einsum("bhtf,bthe->bfhe", probs_low, d_heads, preferred_element_type=jnp.float32).reshape(n_batch, n_frames, n_width)
        grad_bq = jnp.sum(grad_q, axis=(0, 1))
        grad_bv = lax.psum(jnp.sum(grad_v, axis=(0, 1)), "cp")
        dq_low = grad_q.astype(jnp.bfloat16)
        dv_low = grad_v.astype(jnp.bfloat16)
        grad_wq = jnp.einsum("btd,bte->de", x_norm, dq_low, preferred_element_type=jnp.float32)
        d_xnorm = jnp.einsum("bte,de->btd", dq_low, w_q, preferred_element_type=jnp.float32)
        grad_wk = lax.psum(jnp.einsum("bfd,bfe->de", memory, grad_k, preferred_element_type=jnp.float32), "cp")
        grad_wv = lax.psum(jnp.einsum("bfd,bfe->de", memory, dv_low, preferred_element_type=jnp.float32), "cp")
        grad_mem = (jnp.einsum("bfe,de->bfd", grad_k, w_k, preferred_element_type=jnp.float32) + jnp.einsum("bfe,de->bfd", dv_low, w_v, preferred_element_type=jnp.float32)).astype(jnp.bfloat16)
        grad_ln_gain = jnp.sum(d_xnorm * x_hat, axis=(0, 1))
        grad_ln_bias = jnp.sum(d_xnorm, axis=(0, 1))
        d_hat = d_xnorm * gain_f32
        d_hidden = inv_std * (d_hat - jnp.mean(d_hat, axis=-1, keepdims=True) - x_hat * jnp.mean(d_hat * x_hat, axis=-1, keepdims=True))
        grad_h = (grad_y.astype(jnp.float32) + d_hidden).astype(jnp.bfloat16)
        return (out_y, grad_h, grad_mem, grad_ln_gain, grad_ln_bias, grad_wq, grad_bq, grad_wk, grad_wv, grad_bv, grad_wo, grad_bo)

    return jax.shard_map(device_step, mesh=mesh, in_specs=in_specs, out_specs=out_specs, check_vma=False)
```

profile of v0, /device:TPU:0, one launch (start us, length us, event | category | flops | bytes accessed | tf_op | source)
XLA Modules:
  0.0 1075.2 jit_solution(9532861783910068044)
XLA Ops:
  7.2 0.0 copy-start
  7.2 0.0 all-reduce.8.cloned.1.call-start
  7.2 1.5 copy-done
  8.8 70.5 %fusion.9 = bf16[32,375,1024]{2,1,0:T(8,128)(2,1)} fusion(bf16[32,375,1024]{2,0,1:T(8,128)(2,1)} %param.13, bf16[1024,1024]{1,0:T(8,128)(2,1)S(1)} %copy-done), kind=kOutput, calls=%fused_computation.18 | convolution fusion | flops 25178112000 | bytes 51249152 | tf_op jit(solution)/shard_map/bfd,de->bfe/dot_general | solution.py:30
  79.3 0.0 copy-start.18
  79.3 0.0 copy-start.19
  79.3 0.0 copy-start.20
  79.3 32.3 %copy.46 = bf16[32,375,1024]{1,2,0:T(8,128)(2,1)} copy(bf16[32,375,1024]{2,1,0:T(8,128)(2,1)} %fusion.9) | data formatting | bytes 49152000 | tf_op jit(solution)/shard_map/convert_element_type | solution.py:30
  111.7 0.0 copy-start.13
  111.8 2.1 convert_reduce_fusion
  113.9 2.3 fusion.28
  116.2 0.6 copy-done.11
  116.8 3.7 add_convert_fusion.2
  120.6 6.3 reshape.72
  126.9 22.8 %multiply_reduce_fusion.1 = (f32[32,16,32]{2,1,0:T(8,128)}, f32[32,16,32,375]{3,2,1,0:T(8,128)}) fusion(bf16[32,375,16,64]{1,3,2,0:T(8,128)(2,1)} %bitcast.73, bf16[32,32,16,64]{3,2,1,0:T(8,128)(2,1)} %reshape.72), kind=kOutput, calls=%fused_computation.7 | convolution fusion | flops 798703616 | bytes 51314688 | tf_op jit(solution)/shard_map/bthe,bfhe->bhtf/dot_general | solution.py:35
  149.8 0.0 all-reduce.8.cloned.1.call-update
  149.8 0.0 all-reduce.10.cloned.1.call-start
  149.9 58.4 %add_convert_fusion.1 = bf16[32,375,1024]{2,1,0:T(8,128)(2,1)} fusion(f32[1024]{0:T(1024)S(1)} %convert_element_type.80, bf16[32,375,1024]{2,0,1:T(8,128)(2,1)} %param.13, bf16[1024,1024]{1,0:T(8,128)(2,1)} %param.19), kind=kOutput, calls=%fused_computation.3 | convolution fusion | flops 25190400000 | bytes 51253248 | tf_op jit(solution)/shard_map/bfd,de->bfe/dot_general | solution.py:31
  208.2 0.0 all-reduce.8.cloned.1.call-done
  208.3 15.3 %fusion.1 = f32[32,16,32]{2,1,0:T(8,128)} fusion(f32[32,16,32,375]{3,2,1,0:T(8,128)} %get-tuple-element.50, f32[32,16,32]{2,1,0:T(8,128)} %all-reduce.8.cloned.1.call-done), kind=kLoop, calls=%fused_computation.9 | loop fusion | flops 18415616 | bytes 24707072 | tf_op jit(solution)/shard_map/reduce_sum | solution.py:38
  223.5 0.0 all-reduce.10.cloned.1.call-update
  223.6 0.0 copy-start.22
  223.6 0.0 all-reduce.12.cloned.1.call-start
  223.6 5.9 fusion.60
  229.5 0.6 convert_element_type.91
  230.1 32.0 %copy.44 = bf16[32,375,1024]{1,2,0:T(8,128)(2,1)} copy(bf16[32,375,1024]{2,1,0:T(8,128)(2,1)} %add_convert_fusion.1) | data formatting | bytes 49152000 | tf_op jit(solution)/shard_map/convert_element_type | solution.py:31
  262.1 6.4 reshape.74
  268.5 20.8 %fusion.38 = f32[32,32,16,64]{3,1,2,0:T(8,128)} fusion(bf16[32,375,16,64]{1,3,2,0:T(8,128)(2,1)} %bitcast.79, f32[32,16,32,375]{3,2,1,0:T(8,128)} %get-tuple-element.50, f32[32,16,32]{2,1,0:T(8,128)} %all-reduce.10.cloned.1.call-done, f32[32,16,32]{2,1,0:T(8,128)S(1)} %copy-done.4), kind=kOutput, calls=%fused_computation.52 | convolution fusion | flops 811008000 | bytes 53477376 | tf_op jit(solution)/shard_map/bhtf,bfhe->bthe/dot_general | solution.py:41
  289.3 34.3 %bitcast_convert_fusion = (bf16[32,375,16,64]{1,3,2,0:T(8,128)(2,1)}, f32[32,16,64,375]{3,2,1,0:T(8,128)}) fusion(f32[32,16,32]{2,1,0:T(8,128)S(1)} %copy-done.8, f32[32,16,32]{2,1,0:T(8,128)S(1)} %copy-done.4, f32[32,16,32,375]{3,2,1,0:T(8,128)} %get-tuple-element.50, bf16[32,32,16,64]{3,2,1,0:T(8,128)(2,1)} %reshape.74), kind=kOutput, calls=%fused_computation.1 | convolution fusion | flops 823296000 | bytes 100532224 | tf_op jit(solution)/shard_map/bhtf,bthe->bfhe/dot_general | solution.py:54
  323.6 18.1 %bitcast_reduce_fusion = f32[16,64]{1,0:T(8,128)S(1)} fusion(f32[32,16,64,375]{3,2,1,0:T(8,128)} %get-tuple-element.54), kind=kLoop, calls=%fused_computation | loop fusion | flops 12286976 | bytes 49156096 | tf_op jit(solution)/shard_map/reduce_sum | solution.py:56
  341.7 0.1 reduce_sum.114
  341.8 150.1 %all-reduce.15 = (bf16[32,32,16,64]{3,1,2,0:T(8,128)(2,1)}, f32[1024]{0:T(1024)}) all-reduce(f32[32,32,16,64]{3,1,2,0:T(8,128)} %fusion.38, f32[1024]{0:T(1024)S(1)} %reduce_sum.114), channel_id=1, replica_groups=mesh['dp'=2,'cp'=4] {'cp'}, use_global_device_ids=true, to_apply=%region_6.0 | all-reduce | flops 1049600 | bytes 6299648 | tf_op jit(solution)/shard_map/psum | solution.py:41
  491.8 6.2 copy.48
  498.0 6.5 convert_element_type.90
  504.5 28.1 %multiply_reduce_fusion = (f32[32,16,32]{2,1,0:T(8,128)}, f32[32,16,32,375]{3,2,1,0:T(8,128)}) fusion(f32[32,16,32]{2,1,0:T(8,128)S(1)} %copy-done.8, f32[32,16,32]{2,1,0:T(8,128)S(1)} %copy-done.4, f32[32,16,32,375]{3,2,1,0:T(8,128)} %get-tuple-element.50, bf16[32,375,16,64]{1,3,2,0:T(8,128)(2,1)} %bitcast.80, bf16[32,32,16,64]{3,2,1,0:T(8,128)(2,1)} %reshape.74), kind=kOutput, calls=%fused_computation.5 | convolution fusion | flops 817135616 | bytes 76021760 | tf_op jit(solution)/shard_map/bthe,bfhe->bhtf/dot_general | solution.py:49
  532.6 0.0 all-reduce.12.cloned.1.call-update
  532.6 0.0 all-reduce.14.cloned.1.call-start
  532.7 0.0 copy-start.5
  532.7 0.0 copy-start.7
  532.7 50.0 %fusion.44 = f32[1024,1024]{0,1:T(8,128)} fusion(bf16[32,375,1024]{1,2,0:T(8,128)(2,1)} %bitcast.75, bf16[32,375,1024]{2,0,1:T(8,128)(2,1)} %param.13), kind=kOutput, calls=%fused_computation.55 | convolution fusion | flops 25165824000 | bytes 53346304 | tf_op jit(solution)/shard_map/bfd,bfe->de/dot_general | solution.py:62
  582.7 0.0 copy-start.2
  582.7 0.0 copy-start.17
  582.8 4.4 convolution_bitcast_fusion.1
  587.2 3.7 fusion.31
  590.9 22.3 %multiply_convert_fusion = bf16[32,16,32,375]{3,2,1,0:T(8,128)(2,1)} fusion(f32[32,16,32,375]{3,2,1,0:T(8,128)} %get-tuple-element.52, f32[32,16,32]{2,1,0:T(8,128)} %all-reduce.12.cloned.1.call-done, f32[32,16,32]{2,1,0:T(8,128)S(1)} %copy-done.8, f32[32,16,32]{2,1,0:T(8,128)S(1)} %copy-done.4, f32[32,16,32,375]{3,2,1,0:T(8,128)} %get-tuple-element.50), kind=kLoop, calls=%fused_computation.4 | loop fusion | flops 43008000 | bytes 61636608 | tf_op jit(solution)/shard_map/convert_element_type | solution.py:51
  613.2 21.7 %convolution_bitcast_fusion = f32[32,32,16,64]{3,1,2,0:T(8,128)} fusion(bf16[32,375,16,64]{1,3,2,0:T(8,128)(2,1)} %bitcast.74, bf16[32,16,32,375]{3,2,1,0:T(8,128)(2,1)} %multiply_convert_fusion), kind=kOutput, calls=%fused_computation.53 | convolution fusion | flops 786432000 | bytes 41058304 | tf_op jit(solution)/shard_map/bhtf,bfhe->bthe/dot_general | solution.py:52
  634.9 17.1 %convolution_convert_fusion = bf16[32,16,64,375]{3,2,1,0:T(8,128)(2,1)} fusion(bf16[32,16,32,375]{3,2,1,0:T(8,128)(2,1)} %multiply_convert_fusion, bf16[32,32,16,64]{3,2,1,0:T(8,128)(2,1)} %reshape.72), kind=kOutput, calls=%fused_computation.17 | convolution fusion | flops 798720000 | bytes 38961152 | tf_op jit(solution)/shard_map/bhtf,bthe->bfhe/dot_general | solution.py:53
  652.0 49.4 %fusion.41 = f32[1024,1024]{0,1:T(8,128)} fusion(bf16[32,375,1024]{1,2,0:T(8,128)(2,1)} %bitcast.77, bf16[32,375,1024]{2,0,1:T(8,128)(2,1)} %param.13), kind=kOutput, calls=%fused_computation.54 | convolution fusion | flops 25165824000 | bytes 53346304 | tf_op jit(solution)/shard_map/bfd,bfe->de/dot_general | solution.py:61
  701.4 35.1 %fusion.51 = f32[32,375,1024]{2,1,0:T(8,128)} fusion(bf16[32,375,1024]{1,2,0:T(8,128)(2,1)} %bitcast.78, bf16[1024,1024]{1,0:T(8,128)(2,1)S(1)} %copy-done), kind=kOutput, calls=%fused_computation.62 | convolution fusion | flops 25165824000 | bytes 75825152 | tf_op jit(solution)/shard_map/bfe,de->bfd/dot_general | solution.py:63
  736.5 0.0 all-reduce.14.cloned.1.call-update
  736.5 40.4 %add_convert_fusion = bf16[32,375,1024]{2,1,0:T(8,128)(2,1)} fusion(f32[32,375,1024]{2,1,0:T(8,128)} %fusion.51, bf16[32,375,1024]{1,2,0:T(8,128)(2,1)} %bitcast.76, bf16[1024,1024]{1,0:T(8,128)(2,1)} %param.19), kind=kOutput, calls=%fused_computation.2 | convolution fusion | flops 25190400000 | bytes 100401152 | tf_op jit(solution)/shard_map/bfe,de->bfd/dot_general | solution.py:63
  776.9 53.5 %copy.59 = bf16[32,375,1024]{2,0,1:T(8,128)(2,1)} copy(bf16[32,375,1024]{2,1,0:T(8,128)(2,1)} %add_convert_fusion) | data formatting | bytes 49152000
  830.4 189.0 %all-reduce.14.cloned.1.call-done = (f32[32,32,16,64]{3,1,2,0:T(8,128)}, f32[1024,1024]{0,1:T(8,128)}, f32[1024,1024]{0,1:T(8,128)}) async-done(((f32[32,32,16,64]{3,1,2,0:T(8,128)}, f32[1024,1024]{0,1:T(8,128)}, f32[1024,1024]{0,1:T(8,128)}), (f32[32,32,16,64]{3,1,2,0:T(8,128)}, f32[1024,1024]{0,1:T(8,128)}, f32[1024,1024]{0,1:T(8,128)})) %all-reduce.14.cloned.1.call-update) | async-done | bytes 12582928 | tf_op jit(solution)/shard_map/psum | solution.py:52
  1019.4 8.0 fusion.71
  1027.4 4.0 copy.50
  1031.3 6.7 convert_element_type.97
  1038.1 0.0 copy-start.3
  1038.1 0.0 copy-start.6
  1038.1 8.3 fusion.27
  1046.4 4.6 convolution_bitcast_fusion.2
  1051.0 0.7 reduce_sum.112
  1051.7 5.3 copy.60
  1057.0 5.3 copy.61
  1062.4 6.1 convert_reduce_fusion.1
  (45 shorter events, 0.1 us)
Async XLA Ops:
  7.2 1.6 copy-start
  7.2 201.1 %all-reduce.8.cloned.1.call-start = ((), (), s32[]{:S(2)}) async-start(), calls=%async_computation | async-start | bytes 524288 | tf_op jit(solution)/shard_map/pmax | solution.py:36
  79.3 32.4 %copy-start.18 = (bf16[1024]{0:T(1024)(128)(2,1)S(1)}, bf16[1024]{0:T(1024)(128)(2,1)}, u32[]{:S(2)}) copy-start(bf16[1024]{0:T(1024)(128)(2,1)} %param.17) | copy-start | bytes 6148
  79.3 32.4 %copy-start.19 = (bf16[1024]{0:T(1024)(128)(2,1)S(1)}, bf16[1024]{0:T(1024)(128)(2,1)}, u32[]{:S(2)}) copy-start(bf16[1024]{0:T(1024)(128)(2,1)} %param.15) | copy-start | bytes 6148
  79.3 32.4 %copy-start.20 = (bf16[1024]{0:T(1024)(128)(2,1)S(1)}, bf16[1024]{0:T(1024)(128)(2,1)}, u32[]{:S(2)}) copy-start(bf16[1024]{0:T(1024)(128)(2,1)} %param.14) | copy-start | bytes 6148
  111.7 5.1 copy-start.1
  111.7 5.1 copy-start.24
  111.7 4.5 copy-start.15
  111.7 4.4 copy-start.13
  113.9 2.3 copy-start.9
  116.2 0.6 copy-start.11
  126.9 22.9 %copy-start.21 = (bf16[1024]{0:T(1024)(128)(2,1)S(1)}, bf16[1024]{0:T(1024)(128)(2,1)}, u32[]{:S(2)}) copy-start(bf16[1024]{0:T(1024)(128)(2,1)} %param.20) | copy-start | bytes 6148
  149.8 118.8 %all-reduce.10.cloned.1.call-start = ((), (), s32[]{:S(2)}) async-start(), calls=%async_computation.1 | async-start | bytes 524288 | tf_op jit(solution)/shard_map/psum | solution.py:38
  223.6 6.0 copy-start.22
  223.6 367.4 %all-reduce.12.cloned.1.call-start = ((), (), s32[]{:S(2)}) async-start(), calls=%async_computation.2 | async-start | bytes 524288 | tf_op jit(solution)/shard_map/psum | solution.py:50
  262.1 6.4 copy-start.4
  268.5 20.8 %copy-start.8 = (f32[32,16,32]{2,1,0:T(8,128)S(1)}, f32[32,16,32]{2,1,0:T(8,128)}, u32[]{:S(2)}) copy-start(f32[32,16,32]{2,1,0:T(8,128)} %all-reduce.10.cloned.1.call-done) | copy-start | bytes 196612
  532.6 486.8 %all-reduce.14.cloned.1.call-start = ((), (), s32[]{:S(2)}) async-start(), calls=%async_computation.3 | async-start | bytes 33554432 | tf_op jit(solution)/shard_map/psum | solution.py:52
  532.7 50.0 %copy-start.5 = (bf16[32,32,1024]{2,1,0:T(8,128)(2,1)S(1)}, bf16[32,32,1024]{2,1,0:T(8,128)(2,1)}, u32[]{:S(2)}) copy-start(bf16[32,32,1024]{2,1,0:T(8,128)(2,1)} %convert_element_type.90) | copy-start | bytes 6291460
  532.7 50.0 %copy-start.7 = (bf16[32,32,1024]{2,1,0:T(8,128)(2,1)S(1)}, bf16[32,32,1024]{2,1,0:T(8,128)(2,1)}, u32[]{:S(2)}) copy-start(bf16[32,32,1024]{2,1,0:T(8,128)(2,1)} %param.23) | copy-start | bytes 6291460
  582.7 4.5 copy-start.2
  582.7 4.5 copy-start.17
  582.8 4.5 copy-start.23
  1031.3 6.7 copy-start.10
  1031.3 6.7 copy-start.12
  1031.3 6.7 copy-start.14
  1038.1 8.4 copy-start.3
  1038.1 8.3 copy-start.6
  1038.1 8.3 copy-start.16
Sparse Core Ops, SparseCore 0:
  149.9 29.5 all-reduce.7
  223.7 29.4 all-reduce.9
  532.7 26.7 all-reduce.11
  736.7 282.6 all-reduce.13
where the time goes:
time: 1090 us; the launch traced here: 1080 us
  matrix products  479 us (44%)
  waiting for transfers between devices  189 us (17%)
  local copies, waits for them, and re-layouts  168 us (15%)
  blocking collectives  150 us (14%)
  other arithmetic  74.7 us (7%)
  between operations  14.3 us (1%)
    psum x1, waiting for transfers between devices, device_step(): lax.psum(jnp.einsum('bhtf,bfhe->bthe', d_logits, k_heads, preferred_eleme...  189 us
    psum x1, blocking collectives, device_step(): lax.psum(jnp.einsum('bhtf,bfhe->bthe', probs_low, v_heads, preferred_elem...  150 us
    dot_general x1, matrix products, device_step(): jnp.einsum('bfd,de->bfe', memory, w_k, preferred_element_type=jnp.float32)  70.5 us
    unnamed x53, local copies, waits for them, and re-layouts  66.5 us
    dot_general x1, matrix products, device_step(): jnp.einsum('bfd,de->bfe', memory, w_v, preferred_element_type=jnp.float32)  58.4 us
    dot_general x1, matrix products, device_step(): jnp.einsum('bfd,bfe->de', memory, dv_low, preferred_element_type=jnp.floa...  50 us
    dot_general x1, matrix products, device_step(): jnp.einsum('bfd,bfe->de', memory, grad_k, preferred_element_type=jnp.floa...  49.4 us
    dot_general x1, matrix products, device_step(): jnp.einsum('bfe,de->bfd', dv_low, w_v, preferred_element_type=jnp.float32)  40.4 us
  transfers between devices with their start and end apart: 4, of which 1 were waited for; matrix products, arithmetic and copies ran while one was open for 24% of the time, Pallas kernels for 0%

commit v1 on v0

v1 whole, which is shorter than its diff:
```python
import functools
import math
import jax
import jax.numpy as jnp
from jax import lax
from jax.experimental import pallas as pl
from jax.experimental.pallas import tpu as pltpu
from jax.sharding import PartitionSpec as P

EPS = 1e-5
HEAD = 64
F, FP, D, T = 375, 384, 1024, 32
NB = 32
NP = NB // 2
STEPS = 2 * NP
W = 512
ROWS = 2 * FP
ACC = D + 8
BF, F32 = jnp.bfloat16, jnp.float32
LOG2 = 0.125 * math.log2(math.e)
MESH = pl.DeviceIdType.MESH
VMEM = pltpu.VMEM


def dotg(a, b, ca, cb):
    return lax.dot_general(a, b, (((ca,), (cb,)), ((), ())), preferred_element_type=F32)


def split_kernel(x_ref, o_ref, s_ref):
    x = x_ref[...].astype(F32).reshape(8 * F, 256)
    for t in range(2):
        s_ref[t] = x[:, 128 * t:128 * (t + 1)]
    for b in range(8):
        for t in range(2):
            y = s_ref[t, pl.ds(b, F, stride=8), :].astype(BF)
            o_ref[b, 0:F, 128 * t:128 * (t + 1)] = y
            o_ref[b, 368:FP, 128 * t:128 * (t + 1)] = jnp.concatenate([y[368:F], jnp.zeros((FP - F, 128), BF)], axis=0)


def split_frames(mt):
    return pl.pallas_call(
        split_kernel, grid=(NB // 8, D // 256), name="split_frames",
        out_shape=jax.ShapeDtypeStruct((NB, FP, D), BF),
        in_specs=[pl.BlockSpec((F, 8, 256), lambda b, c: (0, b, c))],
        out_specs=pl.BlockSpec((8, FP, 256), lambda b, c: (b, 0, c)),
        scratch_shapes=[VMEM((2, 8 * F, 128), F32)],
        compiler_params=pltpu.CompilerParams(vmem_limit_bytes=40 << 20),
    )(mt)


def join_kernel(x_ref, o_ref, s_ref):
    for b in range(8):
        x = x_ref[b, 0:F, :].astype(F32)
        for t in range(2):
            s_ref[t, pl.ds(b, F, stride=8), :] = x[:, 128 * t:128 * (t + 1)]
    y = jnp.concatenate([s_ref[0], s_ref[1]], axis=1)
    o_ref[...] = y.reshape(F, 8, 256).astype(BF)


def join_frames(x):
    return pl.pallas_call(
        join_kernel, grid=(NB // 8, D // 256), name="join_frames",
        out_shape=jax.ShapeDtypeStruct((F, NB, D), BF),
        in_specs=[pl.BlockSpec((8, FP, 256), lambda b, c: (b, 0, c))],
        out_specs=pl.BlockSpec((F, 8, 256), lambda b, c: (0, b, c)),
        scratch_shapes=[VMEM((2, 8 * F, 128), F32)],
        compiler_params=pltpu.CompilerParams(vmem_limit_bytes=40 << 20),
    )(x)


def dm_kernel(a_ref, b_ref, wk_ref, wv_ref, o_ref):
    x = jnp.concatenate([a_ref[0, 0], b_ref[0, 0]], axis=1)
    w = jnp.concatenate([wk_ref[:, :W], wv_ref[:, :W], wk_ref[:, W:], wv_ref[:, W:]], axis=1)
    o_ref[...] = dotg(x, w, 1, 1).astype(BF).reshape(2, FP, D)


def dm_product(dkv, w_k, w_v):
    full = pl.BlockSpec((D, D), lambda p: (0, 0))
    return pl.pallas_call(
        dm_kernel, grid=(NP,), name="dm_product",
        out_shape=jax.ShapeDtypeStruct((NB, FP, D), BF),
        in_specs=[pl.BlockSpec((1, 1, ROWS, D), lambda p: (0, p, 0, 0)), pl.BlockSpec((1, 1, ROWS, D), lambda p: (1, p, 0, 0)), full, full],
        out_specs=pl.BlockSpec((2, FP, D), lambda p: (p, 0, 0)),
        compiler_params=pltpu.CompilerParams(vmem_limit_bytes=56 << 20),
    )(dkv, dkv, w_k, w_v)


def block_mask():
    return lax.broadcasted_iota(jnp.int32, (128, 256), 0) // T == lax.broadcasted_iota(jnp.int32, (128, 256), 1) // HEAD


def block_diag(x, mask):
    return jnp.where(mask, jnp.concatenate([x] * 4, axis=0), jnp.zeros((), BF))


def attn_kernel(m_hbm, q, do, wk, wv, bv, od_hbm, dw_hbm, dkv_hbm,
                mbuf, kv, e_s, dp_s, mt, stats, coef, dkv, acc, od,
                m_sem, dkv_sem, od_sem, dw_sem, st_send, st_recv):
    me = lax.axis_index("cp")

    def m_copy(i):
        return pltpu.make_async_copy(m_hbm.at[pl.ds(2 * (i % NP), 2)], mbuf.at[i % 2], m_sem.at[i % 2])

    def stat_copy(i, k):
        return pltpu.make_async_remote_copy(
            src_ref=stats.at[i % 4, me], dst_ref=stats.at[i % 4, me],
            send_sem=st_send.at[i % 4, k - 1], recv_sem=st_recv.at[i % 4, me],
            device_id={"cp": (me + k) % 4}, device_id_type=MESH)

    def stat_wait(i, k):
        src = (me + k) % 4
        pltpu.make_async_remote_copy(
            src_ref=stats.at[i % 4, src], dst_ref=stats.at[i % 4, src],
            send_sem=st_send.at[i % 4, k - 1], recv_sem=st_recv.at[i % 4, src],
            device_id={"cp": src}, device_id_type=MESH).wait_recv()

    def dkv_copy(i):
        return pltpu.make_async_copy(dkv.at[i % 2], dkv_hbm.at[i // NP, i % NP], dkv_sem.at[i % 2])

    def od_copy(i):
        return pltpu.make_async_copy(
            od.at[i % 2], od_hbm.at[:, pl.ds(64 * (i % NP), 64), pl.ds(pl.multiple_of(W * (i // NP), W), W)], od_sem.at[i % 2])

    def operands(i, j, h):
        cols = pl.ds(pl.multiple_of(W * (i // NP) + 256 * h, 256), 256)
        rows = pl.ds(pl.multiple_of(64 * (i % NP) + T * j, T), T)
        mask = block_mask()
        return block_diag(q[rows, cols], mask), block_diag(do[rows, cols], mask), mask

    def stage_a(i):
        slot = i % 2
        m = mbuf[slot].reshape(ROWS, D)
        cols = pl.ds(pl.multiple_of(W * (i // NP), W), W)
        kv[slot, :, 0:W] = jnp.dot(m, wk[:, cols], preferred_element_type=F32).astype(BF)
        kv[slot, :, W:] = (jnp.dot(m, wv[:, cols], preferred_element_type=F32) + bv[:, cols]).astype(BF)
        mt[slot] = m.T
        real = lax.broadcasted_iota(jnp.int32, (FP, 128), 0) < F
        for j in range(2):
            rows = slice(FP * j, FP * (j + 1))
            for h in range(2):
                n = 2 * j + h
                qb, db, _ = operands(i, j, h)
                s = dotg(kv[slot, rows, 256 * h:256 * (h + 1)], qb, 1, 1)
                dp = dotg(kv[slot, rows, W + 256 * h:W + 256 * (h + 1)], db, 1, 1)
                s = jnp.where(real, s, -1e30)
                top = jnp.max(s, axis=0, keepdims=True)
                e = jnp.exp2((s - top) * LOG2)
                e_s[slot, n] = e
                dp_s[slot, n] = dp
                stats[i % 4, me, n:n + 1, :] = top
                stats[i % 4, me, 4 + n:5 + n, :] = jnp.sum(e, axis=0, keepdims=True)
                stats[i % 4, me, 8 + n:9 + n, :] = jnp.sum(e * dp, axis=0, keepdims=True)

    def combine(i):
        slot = i % 4
        tops = [stats[slot, d, 0:4, :] for d in range(4)]
        top = jnp.maximum(jnp.maximum(tops[0], tops[1]), jnp.maximum(tops[2], tops[3]))
        ws = [jnp.exp2((t - top) * LOG2) for t in tops]
        total = sum(stats[slot, d, 4:8, :] * ws[d] for d in range(4))
        dots = sum(stats[slot, d, 8:12, :] * ws[d] for d in range(4))
        coef[0:4, :] = jnp.exp2((stats[slot, me, 0:4, :] - top) * LOG2) / total
        coef[4:8, :] = dots / total

    def stage_b(i):
        slot = i % 2
        grp = i // NP
        for j in range(2):
            rows = slice(FP * j, FP * (j + 1))
            for h in range(2):
                n = 2 * j + h
                qb, db, mask = operands(i, j, h)
                ck, cv = slice(256 * h, 256 * (h + 1)), slice(W + 256 * h, W + 256 * (h + 1))
                p = e_s[slot, n] * coef[n:n + 1, :]
                pb = p.astype(BF)
                gb = (p * (dp_s[slot, n] - coef[4 + n:5 + n, :]) * 0.125).astype(BF)
                o = dotg(pb, kv[slot, rows, cv], 0, 0)
                dq = dotg(gb, kv[slot, rows, ck], 0, 0)
                for which, x in ((0, o), (1, dq)):
                    x = jnp.where(mask, x, 0.0)
                    x = (x[0:32] + x[32:64]) + (x[64:96] + x[96:128])
                    od[slot, which, T * j:T * (j + 1), ck] = x
                    if which == 1:
                        acc[grp, D:D + 1, ck] += jnp.sum(x, axis=0, keepdims=True)
                dk = jnp.dot(gb, qb, preferred_element_type=F32)
                dv = jnp.dot(pb, db, preferred_element_type=F32)
                dkv[slot, rows, ck] = dk.astype(BF)
                dkv[slot, rows, cv] = dv.astype(BF)
                acc[grp, D:D + 1, cv] += jnp.sum(dv, axis=0, keepdims=True)
        acc[grp, 0:D, :] += jnp.dot(mt[slot], dkv[slot], preferred_element_type=F32)

    def part_a(i):
        m_copy(i).wait()

        @pl.when(i + 1 < STEPS)
        def _():
            m_copy(i + 1).start()

        stage_a(i)
        for k in range(1, 4):
            stat_copy(i, k).start()

    def part_b(i):
        for k in range(1, 4):
            stat_wait(i, k)
            stat_copy(i, k).wait_send()

        @pl.when(i >= 2)
        def _():
            dkv_copy(i - 2).wait()
            od_copy(i - 2).wait()

        combine(i)
        stage_b(i)
        dkv_copy(i).start()
        od_copy(i).start()

    m_copy(0).start()
    for g in range(2):
        acc[g] = jnp.zeros((ACC, D), F32)
    barrier = pltpu.get_barrier_semaphore()
    for k in range(1, 4):
        pl.semaphore_signal(barrier, inc=1, device_id={"cp": (me + k) % 4}, device_id_type=MESH)
    pl.semaphore_wait(barrier, 3)
    part_a(jnp.int32(0))

    def step(i, carry):
        part_a(i)
        part_b(i - 1)
        return carry

    lax.fori_loop(1, STEPS, step, 0)
    part_b(jnp.int32(STEPS - 1))
    out = pltpu.make_async_copy(acc, dw_hbm, dw_sem)
    out.start()
    for i in (STEPS - 2, STEPS - 1):
        dkv_copy(i).wait()
        od_copy(i).wait()
    out.wait()


def attention(m_pad, q, do, w_k, w_v, b_v):
    vm = pl.BlockSpec(memory_space=VMEM)
    hbm = pl.BlockSpec(memory_space=pl.ANY)
    dma = pltpu.SemaphoreType.DMA
    return pl.pallas_call(
        attn_kernel, name="attention",
        out_shape=(jax.ShapeDtypeStruct((2, NB * T, D), F32), jax.ShapeDtypeStruct((2, ACC, D), F32),
                   jax.ShapeDtypeStruct((2, NP, ROWS, D), BF)),
        in_specs=[hbm, vm, vm, vm, vm, vm],
        out_specs=(hbm, hbm, hbm),
        scratch_shapes=[
            VMEM((2, 2, FP, D), BF), VMEM((2, ROWS, D), BF), VMEM((2, 4, FP, 128), F32), VMEM((2, 4, FP, 128), F32),
            VMEM((2, D, ROWS), BF), VMEM((4, 4, 16, 128), F32), VMEM((8, 128), F32), VMEM((2, ROWS, D), BF),
            VMEM((2, ACC, D), F32), VMEM((2, 2, 64, W), F32),
            dma((2,)), dma((2,)), dma((2,)), dma, dma((4, 3)), dma((4, 4))],
        compiler_params=pltpu.CompilerParams(vmem_limit_bytes=60 << 20, collective_id=0, has_side_effects=True),
    )(m_pad, q, do, w_k, w_v, b_v)


def solution(mesh):
    act_spec = P("dp", None, None)
    mem_spec = P("dp", "cp", None)
    vec_out = P("dp")
    mat_out = P("dp", None)
    in_specs = (act_spec, mem_spec, P(), P(), P(), P(), P(), P(), P(), P(), P(), act_spec)
    out_specs = (act_spec, act_spec, mem_spec, vec_out, vec_out, mat_out, vec_out, mat_out, mat_out, vec_out, mat_out, vec_out)

    def device_step(hidden, memory, ln_gain, ln_bias, w_q, b_q, w_k, w_v, b_v, w_o, b_o, grad_y):
        h = hidden.reshape(NB * T, D).astype(F32)
        dy = grad_y.reshape(NB * T, D)
        centered = h - jnp.mean(h, axis=-1, keepdims=True)
        inv_std = lax.rsqrt(jnp.mean(centered * centered, axis=-1, keepdims=True) + EPS)
        x_hat = centered * inv_std
        gain = ln_gain.astype(F32)
        x = (x_hat * gain + ln_bias.astype(F32)).astype(BF)
        q = (jnp.dot(x, w_q, preferred_element_type=F32) + b_q.astype(F32)).astype(BF)
        do = dotg(dy, w_o, 1, 1).astype(BF)
        m_pad = split_frames(memory.transpose(1, 0, 2))
        od, dw, dkv = attention(m_pad, q, do, w_k, w_v, b_v.astype(F32).reshape(1, D))
        od = lax.psum(od, "cp")
        dw = lax.psum(dw, "cp")
        grad_mem = join_frames(dm_product(dkv, w_k, w_v)).transpose(1, 0, 2)
        o = od[0].astype(BF)
        dq = od[1].astype(BF)
        out_y = (h + jnp.dot(o, w_o, preferred_element_type=F32) + b_o.astype(F32)).astype(BF)
        grad_wo = dotg(o, dy, 0, 0)
        grad_bo = jnp.sum(dy, axis=0, dtype=F32)
        grad_wk = jnp.concatenate([dw[0, :D, :W], dw[1, :D, :W]], axis=1)
        grad_wv = jnp.concatenate([dw[0, :D, W:], dw[1, :D, W:]], axis=1)
        grad_bq = jnp.concatenate([dw[0, D, :W], dw[1, D, :W]])
        grad_bv = jnp.concatenate([dw[0, D, W:], dw[1, D, W:]])
        grad_wq = dotg(x, dq, 0, 0)
        d_x = dotg(dq, w_q, 1, 1)
        grad_gain = jnp.sum(d_x * x_hat, axis=0)
        grad_bias = jnp.sum(d_x, axis=0)
        d_hat = d_x * gain
        d_h = inv_std * (d_hat - jnp.mean(d_hat, axis=-1, keepdims=True) - x_hat * jnp.mean(d_hat * x_hat, axis=-1, keepdims=True))
        grad_h = (dy.astype(F32) + d_h).astype(BF)
        return (out_y.reshape(NB, T, D), grad_h.reshape(NB, T, D), grad_mem, grad_gain, grad_bias, grad_wq, grad_bq,
                grad_wk, grad_wv, grad_bv, grad_wo, grad_bo)

    return jax.shard_map(device_step, mesh=mesh, in_specs=in_specs, out_specs=out_specs, check_vma=False)
```

time: 1090 us -> 620 us (0.57); the launches traced: 1080 us -> 619 us
  matrix products: 479 us -> 23.3 us
  Pallas kernels: 0 us -> 284 us
  waiting for transfers between devices: 189 us -> 0.02 us
  local copies, waits for them, and re-layouts: 168 us -> 5.43 us
  blocking collectives: 150 us -> 276 us
  other arithmetic: 74.7 us -> 15.7 us
    dot_general x18 -> x6, matrix products: 479 us -> 23.3 us  [the longest x4 15.9 us: dotg(): lax.dot_general(a, b, (((ca,), (cb,)), ((), ())), preferred_element_type=...]
    pallas_call x0 -> x4, Pallas kernels: none -> 284 us  [the longest x1 171 us: attention(): pl.pallas_call(attn_kernel, name='attention', out_shape=(jax.ShapeDtypeSt...]
    psum x3 -> x1, waiting for transfers between devices: 189 us -> 0.01 us  [device_step(): dw = lax.psum(dw, 'cp')]
    psum x1, blocking collectives: 150 us -> 276 us  [device_step(): od = lax.psum(od, 'cp')]
    convert_element_type x6 -> x0, local copies, waits for them, and re-layouts: 87.7 us -> none  [the longest x1 32.3 us: device_step(): jnp.einsum('bfd,de->bfe', memory, w_k, preferred_element_type=jnp.float32)]
    unnamed x53 -> x26, local copies, waits for them, and re-layouts: 66.5 us -> 0.07 us
    reduce_sum x5 -> x2, other arithmetic: 49.5 us -> 3.02 us  [the longest x1 2.06 us: device_step(): centered = h - jnp.mean(h, axis=-1, keepdims=True)]
    convert_element_type x6 -> x7, other arithmetic: 22.9 us -> 4.56 us  [the longest x1 2.91 us: device_step(): grad_h = (dy.astype(F32) + d_h).astype(BF)]
  transfers between devices with their start and end apart: 4 -> 1, of which waited for: 1 -> 0; matrix products, arithmetic and copies ran while one was open for 24% -> 3% of each run, Pallas kernels for 0% -> 14%
where the time goes in v1:
time: 620 us; the launch traced here: 619 us
  Pallas kernels  284 us (46%)
  blocking collectives  276 us (45%)
  matrix products  23.3 us (4%)
  other arithmetic  15.7 us (3%)
  between operations  14.2 us (2%)
    psum x1, blocking collectives, device_step(): od = lax.psum(od, 'cp')  276 us
    pallas_call x1, Pallas kernels, attention(): pl.pallas_call(attn_kernel, name='attention', out_shape=(jax.ShapeDtypeSt...  171 us
    pallas_call x1, Pallas kernels, dm_product(): pl.pallas_call(dm_kernel, grid=(NP,), name='dm_product', out_shape=jax.Sh...  59.8 us
    pallas_call x1, Pallas kernels, join_frames(): pl.pallas_call(join_kernel, grid=(NB // 8, D // 256), name='join_frames',...  27.5 us
    pallas_call x1, Pallas kernels, split_frames(): pl.pallas_call(split_kernel, grid=(NB // 8, D // 256), name='split_frames...  26.1 us
    dot_general x4, matrix products, dotg(): lax.dot_general(a, b, (((ca,), (cb,)), ((), ())), preferred_element_type=...  15.9 us
  transfers between devices with their start and end apart: 1, of which 0 were waited for; matrix products, arithmetic and copies ran while one was open for 3% of the time, Pallas kernels for 14%

profile of v1, /device:TPU:0, one launch (start us, length us, event | category | flops | bytes accessed | tf_op | source)
XLA Modules:
  0.0 619.2 jit_solution(5915794267629192680)
XLA Ops:
  7.2 0.0 copy-start
  7.2 0.0 copy-start.6
  7.2 0.0 copy-start.7
  7.2 0.0 copy-start.8
  7.2 0.0 all-reduce.3.cloned.1.call-start
  7.3 2.1 convert_reduce_fusion
  9.3 2.3 fusion.2
  11.6 0.1 div.15
  11.7 0.1 rsqrt.13
  11.8 0.0 copy-done.6
  11.8 0.0 copy-done.7
  11.8 0.0 copy-done.8
  11.9 0.0 copy-start.9
  11.9 0.0 copy-start.3
  11.9 0.0 copy-start.11
  11.9 26.1 %split_frames.1.m_hbm = bf16[32,384,1024]{2,1,0:T(8,128)(2,1)} custom-call(bf16[375,32,1024]{2,1,0:T(8,128)(2,1)} %bitcast.71), custom_call_target="tpu_custom_call" | custom-call | tf_op jit(solution)/shard_map/split_frames/pallas_call | solution.py:41
  38.0 0.0 copy-done.9
  38.0 0.6 reshape.114
  38.6 0.0 copy-done.3
  38.6 0.0 copy-done.11
  38.6 0.0 copy-start.1
  38.6 3.7 convolution_convert_fusion.do
  42.3 0.0 copy-done.1
  42.3 0.8 fusion.12
  43.1 0.0 copy-done
  43.1 3.7 add_convert_fusion.q
  46.8 171.0 %attention.1 = (f32[2,1024,1024]{2,1,0:T(8,128)}, f32[2,1032,1024]{2,1,0:T(8,128)}, bf16[2,16,768,1024]{3,2,1,0:T(8,128)(2,1)}) custom-call(bf16[32,384,1024]{2,1,0:T(8,128)(2,1)} %split_frames.1.m_hbm, bf16[1024,1024]{1,0:T(8,128)(2,1)} %add_convert_fusion.q, bf16[1024,1024]{1,0:T(8,128)(2,1)} %convolution_convert_fusion.do, bf16[1024,1024]{1,0:T(8,128)(2,1)} %wk_ref.1, ...), custom_call_target="tpu_custom_call" | custom-call | tf_op jit(solution)/shard_map/attention/pallas_call | solution.py:245
  217.8 0.0 all-reduce.3.cloned.1.call-update
  217.8 0.0 copy-start.10
  217.8 276.1 %all-reduce.4 = bf16[2,1024,1024]{2,1,0:T(8,128)(2,1)} all-reduce(f32[2,1024,1024]{2,1,0:T(8,128)} %get-tuple-element.15), channel_id=1, replica_groups=mesh['dp'=2,'cp'=4] {'cp'}, use_global_device_ids=true, to_apply=%region_2.0 | all-reduce | flops 2097152 | bytes 12582912 | tf_op jit(solution)/shard_map/psum | solution.py:280
  493.9 0.0 copy-done.10
  493.9 59.8 %dm_product.1.x_ref = bf16[32,384,1024]{2,1,0:T(8,128)(2,1)} custom-call(bf16[2,16,768,1024]{3,2,1,0:T(8,128)(2,1)} %get-tuple-element.16.a_ref.b_ref, bf16[2,16,768,1024]{3,2,1,0:T(8,128)(2,1)} %get-tuple-element.16.a_ref.b_ref, bf16[1024,1024]{1,0:T(8,128)(2,1)} %wk_ref.1, bf16[1024,1024]{1,0:T(8,128)(2,1)} %wv_ref.1), custom_call_target="tpu_custom_call" | custom-call | tf_op jit(solution)/shard_map/dm_product/pallas_call | solution.py:79
  553.7 0.0 copy-start.4
  553.7 0.0 copy-start.2
  553.7 0.0 copy-start.5
  553.7 27.5 %join_frames.1 = bf16[375,32,1024]{2,1,0:T(8,128)(2,1)} custom-call(bf16[32,384,1024]{2,1,0:T(8,128)(2,1)} %dm_product.1.x_ref), custom_call_target="tpu_custom_call" | custom-call | tf_op jit(solution)/shard_map/join_frames/pallas_call | solution.py:61
  581.3 0.0 copy-done.4
  581.3 1.0 convert_reduce_fusion.1
  582.2 0.0 copy-done.2
  582.2 0.0 copy-done.5
  582.2 3.4 fusion.18
  585.6 0.8 fusion.5
  586.4 4.4 fusion.27
  590.8 4.4 fusion.23
  595.3 0.0 copy-start.12
  595.3 2.9 fusion.17
  598.2 0.0 copy-done.12
  598.2 3.7 fusion.20
  601.9 0.0 all-reduce.3.cloned.1.call-done
  601.9 4.4 slice_bitcast_fusion.1
  606.4 4.6 pad_maximum_fusion
  611.0 0.8 fusion.30
  611.8 0.6 pad_maximum_fusion.2
  (7 shorter events, 0.0 us)
Async XLA Ops:
  7.2 35.9 %copy-start = (bf16[1024,1024]{1,0:T(8,128)(2,1)S(1)}, bf16[1024,1024]{1,0:T(8,128)(2,1)}, u32[]{:S(2)}) copy-start(bf16[1024,1024]{1,0:T(8,128)(2,1)} %param.16) | copy-start | bytes 6291460
  7.2 4.6 copy-start.6
  7.2 4.6 copy-start.7
  7.2 4.6 copy-start.8
  7.2 594.7 %all-reduce.3.cloned.1.call-start = ((), (), s32[]{:S(2)}) async-start(), calls=%async_computation | async-start | bytes 16908288 | tf_op jit(solution)/shard_map/psum | solution.py:281
  11.9 26.1 %copy-start.9 = (bf16[1024]{0:T(1024)(128)(2,1)S(1)}, bf16[1024]{0:T(1024)(128)(2,1)}, u32[]{:S(2)}) copy-start(bf16[1024]{0:T(1024)(128)(2,1)} %param.20) | copy-start | bytes 6148
  11.9 26.7 %copy-start.3 = (bf16[32,32,1024]{2,1,0:T(8,128)(2,1)S(1)}, bf16[32,32,1024]{2,1,0:T(8,128)(2,1)}, u32[]{:S(2)}) copy-start(bf16[32,32,1024]{2,1,0:T(8,128)(2,1)} %param.23) | copy-start | bytes 6291460
  11.9 26.7 %copy-start.11 = (bf16[1024,1024]{1,0:T(8,128)(2,1)S(1)}, bf16[1024,1024]{1,0:T(8,128)(2,1)}, u32[]{:S(2)}) copy-start(bf16[1024,1024]{1,0:T(8,128)(2,1)} %param.21) | copy-start | bytes 6291460
  38.6 3.7 copy-start.1
  217.8 276.1 %copy-start.10 = (bf16[1024]{0:T(1024)(128)(2,1)S(1)}, bf16[1024]{0:T(1024)(128)(2,1)}, u32[]{:S(2)}) copy-start(bf16[1024]{0:T(1024)(128)(2,1)} %param.22) | copy-start | bytes 6148
  553.7 27.5 %copy-start.4 = (bf16[32,32,1024]{2,1,0:T(8,128)(2,1)S(1)}, bf16[32,32,1024]{2,1,0:T(8,128)(2,1)}, u32[]{:S(2)}) copy-start(bf16[32,32,1024]{2,1,0:T(8,128)(2,1)} %param.23) | copy-start | bytes 6291460
  553.7 28.5 %copy-start.2 = (bf16[32,32,1024]{2,1,0:T(8,128)(2,1)S(1)}, bf16[32,32,1024]{2,1,0:T(8,128)(2,1)}, u32[]{:S(2)}) copy-start(bf16[32,32,1024]{2,1,0:T(8,128)(2,1)} %param.12) | copy-start | bytes 6291460
  553.7 28.5 %copy-start.5 = (bf16[2,1024,1024]{2,1,0:T(8,128)(2,1)S(1)}, bf16[2,1024,1024]{2,1,0:T(8,128)(2,1)}, u32[]{:S(2)}) copy-start(bf16[2,1024,1024]{2,1,0:T(8,128)(2,1)} %all-reduce.4) | copy-start | bytes 12582916
  595.3 2.9 copy-start.12
Sparse Core Ops, SparseCore 0:
  217.9 277.4 all-reduce.2

commit v2 on v1

--- a/solution.py
+++ b/solution.py
@@ -15,7 +15,6 @@
 STEPS = 2 * NP
 W = 512
 ROWS = 2 * FP
-ACC = D + 8
 BF, F32 = jnp.bfloat16, jnp.float32
 LOG2 = 0.125 * math.log2(math.e)
 MESH = pl.DeviceIdType.MESH
@@ -68,23 +67,6 @@
     )(x)
 
 
-def dm_kernel(a_ref, b_ref, wk_ref, wv_ref, o_ref):
-    x = jnp.concatenate([a_ref[0, 0], b_ref[0, 0]], axis=1)
-    w = jnp.concatenate([wk_ref[:, :W], wv_ref[:, :W], wk_ref[:, W:], wv_ref[:, W:]], axis=1)
-    o_ref[...] = dotg(x, w, 1, 1).astype(BF).reshape(2, FP, D)
-
-
-def dm_product(dkv, w_k, w_v):
-    full = pl.BlockSpec((D, D), lambda p: (0, 0))
-    return pl.pallas_call(
-        dm_kernel, grid=(NP,), name="dm_product",
-        out_shape=jax.ShapeDtypeStruct((NB, FP, D), BF),
-        in_specs=[pl.BlockSpec((1, 1, ROWS, D), lambda p: (0, p, 0, 0)), pl.BlockSpec((1, 1, ROWS, D), lambda p: (1, p, 0, 0)), full, full],
-        out_specs=pl.BlockSpec((2, FP, D), lambda p: (p, 0, 0)),
-        compiler_params=pltpu.CompilerParams(vmem_limit_bytes=56 << 20),
-    )(dkv, dkv, w_k, w_v)
-
-
 def block_mask():
     return lax.broadcasted_iota(jnp.int32, (128, 256), 0) // T == lax.broadcasted_iota(jnp.int32, (128, 256), 1) // HEAD
 
@@ -93,33 +75,184 @@
     return jnp.where(mask, jnp.concatenate([x] * 4, axis=0), jnp.zeros((), BF))
 
 
-def attn_kernel(m_hbm, q, do, wk, wv, bv, od_hbm, dw_hbm, dkv_hbm,
-                mbuf, kv, e_s, dp_s, mt, stats, coef, dkv, acc, od,
-                m_sem, dkv_sem, od_sem, dw_sem, st_send, st_recv):
+def when(cond):
+    if isinstance(cond, bool):
+        return (lambda f: f()) if cond else (lambda f: None)
+    return pl.when(cond)
+
+
+CH = 64
+NCH = D // 2 // CH
+
+
+def attn_kernel(m_hbm, q, do, wk, wv, bv, res_hbm, dw_hbm, bias_hbm, dm_hbm, dkv_hbm,
+                mbuf, kv, e_s, dp_s, mt, stats, coef, dkv, acc, bias, od, r1, keep, x2, r2, res, big1, big2,
+                m_sem, dkv_sem, dm_sem, out_sem, st_send, st_recv, s1_send, s1_recv, s2_send, s2_recv,
+                s3_send, s3_recv, s3s_send, s4_send, res_recv, e1_send, e1_recv, e2_send, e2_recv,
+                e3_send, e3_recv, e3s_send, e4_send, acc_recv, b_send, b_recv, free_sib, free_xn):
     me = lax.axis_index("cp")
+    cx, cc = me // 2, me % 2
+    sib, xn = 2 * cx + 1 - cc, 2 * (1 - cx) + cc
+
+    def remote(src, dst, ss, rs, dev):
+        return pltpu.make_async_remote_copy(src_ref=src, dst_ref=dst, send_sem=ss, recv_sem=rs,
+                                            device_id={"cp": dev}, device_id_type=MESH)
 
     def m_copy(i):
         return pltpu.make_async_copy(m_hbm.at[pl.ds(2 * (i % NP), 2)], mbuf.at[i % 2], m_sem.at[i % 2])
 
-    def stat_copy(i, k):
-        return pltpu.make_async_remote_copy(
-            src_ref=stats.at[i % 4, me], dst_ref=stats.at[i % 4, me],
-            send_sem=st_send.at[i % 4, k - 1], recv_sem=st_recv.at[i % 4, me],
-            device_id={"cp": (me + k) % 4}, device_id_type=MESH)
-
-    def stat_wait(i, k):
-        src = (me + k) % 4
-        pltpu.make_async_remote_copy(
-            src_ref=stats.at[i % 4, src], dst_ref=stats.at[i % 4, src],
-            send_sem=st_send.at[i % 4, k - 1], recv_sem=st_recv.at[i % 4, src],
-            device_id={"cp": src}, device_id_type=MESH).wait_recv()
-
     def dkv_copy(i):
         return pltpu.make_async_copy(dkv.at[i % 2], dkv_hbm.at[i // NP, i % NP], dkv_sem.at[i % 2])
 
-    def od_copy(i):
-        return pltpu.make_async_copy(
-            od.at[i % 2], od_hbm.at[:, pl.ds(64 * (i % NP), 64), pl.ds(pl.multiple_of(W * (i // NP), W), W)], od_sem.at[i % 2])
+    def stat_copy(i, src, k):
+        return remote(stats.at[i % 4, src], stats.at[i % 4, src], st_send.at[i % 4, k - 1], st_recv.at[i % 4, src], (me + k) % 4)
+
+    def s1(b):
+        return remote(od.at[b % 2, 1 - cc], r1.at[b % 4], s1_send.at[b % 4], s1_recv.at[b % 4], sib)
+
+    def s2(b):
+        return remote(x2.at[b % 4], r2.at[b % 8], s2_send.at[b % 8], s2_recv.at[b % 8], xn)
+
+    def res_at(b, x):
+        return res.at[cc, pl.ds(pl.multiple_of(64 * (b % NP) + T * x, T), T), pl.ds(pl.multiple_of(W * (b // NP), W), W)]
+
+    def s3(b, x):
+        return remote(res_at(b, x), res_at(b, x), s3_send.at[b % 8], s3_recv.at[b % 8], xn)
+
+    def s3s(b):
+        return remote(res_at(b, cx), res_at(b, cx), s3s_send.at[b % 4], res_recv, sib)
+
+    def s4(b):
+        return remote(res_at(b, 1 - cx), res_at(b, 1 - cx), s4_send.at[b % 4], res_recv, sib)
+
+    def od_pre(b, inside):
+        def on(k):
+            return (b >= k) if inside else (b - k < STEPS)
+
+        @when(on(7))
+        def _():
+            s4(b - 7).wait_send()
+
+        @when(on(5))
+        def _():
+            s3(b - 5, 1 - cx).wait_recv()
+            s4(b - 5).start()
+            s3(b - 5, cx).wait_send()
+            s3s(b - 5).wait_send()
+
+        @when(on(3))
+        def _():
+            s2(b - 3).wait_recv()
+            s2(b - 3).wait_send()
+            res_at(b - 3, cx)[...] = (keep[(b - 3) % 4] + r2[(b - 3) % 8]).astype(BF)
+
+        @when(on(2))
+        def _():
+            s1(b - 2).wait_send()
+
+        @when(on(1))
+        def _():
+            s1(b - 1).wait_recv()
+            for ref, x in ((keep, cx), (x2, 1 - cx)):
+                rows = pl.ds(pl.multiple_of(T * x, T), T)
+                ref[(b - 1) % 4] = od[(b - 1) % 2, cc, rows, :] + r1[(b - 1) % 4, rows, :]
+
+    def od_post(b, inside):
+        def on(k):
+            return (b >= k) if inside else (b - k < STEPS)
+
+        if inside:
+            s1(b).start()
+
+        @when(on(1))
+        def _():
+            s2(b - 1).start()
+
+        @when(on(3))
+        def _():
+            s3(b - 3, cx).start()
+            s3s(b - 3).start()
+
+    own = pl.ds(pl.multiple_of(W * cc, W), W)
+    other = pl.ds(pl.multiple_of(W * (1 - cc), W), W)
+
+    def rows_of(x, n):
+        return pl.ds(pl.multiple_of(x * (D // 2) + CH * n, CH), CH)
+
+    def e1(g):
+        return remote(acc.at[g, :, other], big1, e1_send.at[g], e1_recv.at[g], sib)
+
+    def e2(g, n):
+        return remote(acc.at[g, rows_of(1 - cx, n), own], big2.at[g, pl.ds(pl.multiple_of(CH * n, CH), CH)],
+                      e2_send.at[g, n], e2_recv.at[g, n], xn)
+
+    def e3(g, n, x):
+        ref = acc.at[g, rows_of(x, n), own]
+        return remote(ref, ref, e3_send.at[g, n], e3_recv.at[g, n], xn)
+
+    def to_sib(g, n, x, sem):
+        ref = acc.at[g, rows_of(x, n), own]
+        return remote(ref, ref, sem.at[g, n], acc_recv.at[g], sib)
+
+    def dw_copy(g):
+        return pltpu.make_async_copy(acc.at[g], dw_hbm.at[g], out_sem.at[g])
+
+    def exchange(g, t, t3, t4):
+        @when(t == 0)
+        def _():
+            e1(g).start()
+
+        @when(t == 1)
+        def _():
+            e1(g).wait_send()
+            pl.semaphore_signal(free_sib.at[g], inc=1, device_id={"cp": sib}, device_id_type=MESH)
+            e1(g).wait_recv()
+
+        @when(t == t3)
+        def _():
+            pl.semaphore_wait(free_sib.at[g], 1)
+
+        def chunk(t0, f):
+            n = t - t0
+            if isinstance(n, int):
+                if 0 <= n < NCH:
+                    f(n)
+            else:
+                pl.when((n >= 0) & (n < NCH))(lambda: f(n))
+
+        def reduce_core(n):
+            for x in (cx, 1 - cx):
+                acc[g, rows_of(x, n), own] += big1[rows_of(x, n), :]
+            e2(g, n).start()
+
+        def sent(n):
+            e2(g, n).wait_send()
+            pl.semaphore_signal(free_xn.at[g], inc=1, device_id={"cp": xn}, device_id_type=MESH)
+
+        def reduce_chip(n):
+            e2(g, n).wait_recv()
+            pl.semaphore_wait(free_xn.at[g], 1)
+            acc[g, rows_of(cx, n), own] += big2[g, pl.ds(pl.multiple_of(CH * n, CH), CH), :]
+            e3(g, n, cx).start()
+            to_sib(g, n, cx, e3s_send).start()
+
+        def forward(n):
+            e3(g, n, 1 - cx).wait_recv()
+            to_sib(g, n, 1 - cx, e4_send).start()
+
+        chunk(1, reduce_core)
+        chunk(t3 - 1, sent)
+        chunk(t3, reduce_chip)
+        chunk(t4, forward)
+
+        @when(t == t4 + NCH + 1)
+        def _():
+            remote(acc.at[g, :, other], acc.at[g, :, other], e1_send.at[g], acc_recv.at[g], sib).wait_recv()
+            for n in range(NCH):
+                e3(g, n, cx).wait_send()
+                to_sib(g, n, cx, e3s_send).wait_send()
+                to_sib(g, n, 1 - cx, e4_send).wait_send()
+            dw_copy(g).start()
 
     def operands(i, j, h):
         cols = pl.ds(pl.multiple_of(W * (i // NP) + 256 * h, 256), 256)
@@ -180,13 +313,13 @@
                     x = (x[0:32] + x[32:64]) + (x[64:96] + x[96:128])
                     od[slot, which, T * j:T * (j + 1), ck] = x
                     if which == 1:
-                        acc[grp, D:D + 1, ck] += jnp.sum(x, axis=0, keepdims=True)
+                        bias[me, pl.ds(grp, 1), ck] += jnp.sum(x, axis=0, keepdims=True)
                 dk = jnp.dot(gb, qb, preferred_element_type=F32)
                 dv = jnp.dot(pb, db, preferred_element_type=F32)
                 dkv[slot, rows, ck] = dk.astype(BF)
                 dkv[slot, rows, cv] = dv.astype(BF)
-                acc[grp, D:D + 1, cv] += jnp.sum(dv, axis=0, keepdims=True)
-        acc[grp, 0:D, :] += jnp.dot(mt[slot], dkv[slot], preferred_element_type=F32)
+                bias[me, pl.ds(grp, 1), cv] += jnp.sum(dv, axis=0, keepdims=True)
+        acc[grp] += jnp.dot(mt[slot], dkv[slot], preferred_element_type=F32)
 
     def part_a(i):
         m_copy(i).wait()
@@ -197,26 +330,32 @@
 
         stage_a(i)
         for k in range(1, 4):
-            stat_copy(i, k).start()
-
-    def part_b(i):
+            stat_copy(i, me, k).start()
+
+    def part_b(b):
+        exchange(0, b - NP, 9, 12)
         for k in range(1, 4):
-            stat_wait(i, k)
-            stat_copy(i, k).wait_send()
-
-        @pl.when(i >= 2)
-        def _():
-            dkv_copy(i - 2).wait()
-            od_copy(i - 2).wait()
-
-        combine(i)
-        stage_b(i)
-        dkv_copy(i).start()
-        od_copy(i).start()
+            stat_copy(b, (me + k) % 4, k).wait_recv()
+
+        @pl.when(b >= 1)
+        def _():
+            for k in range(1, 4):
+                stat_copy(b - 1, me, k).wait_send()
+
+        @pl.when(b >= 2)
+        def _():
+            dkv_copy(b - 2).wait()
+
+        od_pre(b, True)
+        combine(b)
+        stage_b(b)
+        dkv_copy(b).start()
+        od_post(b, True)
 
     m_copy(0).start()
     for g in range(2):
-        acc[g] = jnp.zeros((ACC, D), F32)
+        acc[g] = jnp.zeros((D, D), F32)
+    bias[me] = jnp.zeros((8, D), F32)
     barrier = pltpu.get_barrier_semaphore()
     for k in range(1, 4):
         pl.semaphore_signal(barrier, inc=1, device_id={"cp": (me + k) % 4}, device_id_type=MESH)
@@ -230,12 +369,80 @@
 
     lax.fori_loop(1, STEPS, step, 0)
     part_b(jnp.int32(STEPS - 1))
-    out = pltpu.make_async_copy(acc, dw_hbm, dw_sem)
-    out.start()
-    for i in (STEPS - 2, STEPS - 1):
-        dkv_copy(i).wait()
-        od_copy(i).wait()
-    out.wait()
+
+    def b_copy(k, src):
+        return remote(bias.at[src], bias.at[src], b_send.at[k - 1], b_recv.at[src], (me + k) % 4)
+
+    for k in range(1, 4):
+        b_copy(k, me).start()
+        stat_copy(STEPS - 1, me, k).wait_send()
+    dkv_copy(STEPS - 2).wait()
+    dkv_copy(STEPS - 1).wait()
+
+    bufs = (kv, dkv)
+
+    def c_load(c, s):
+        return [pltpu.make_async_copy(dkv_hbm.at[g, c], bufs[s].at[g], m_sem.at[g] if s == 0 else dkv_sem.at[g]) for g in range(2)]
+
+    def dm_copy(c, s):
+        return pltpu.make_async_copy(mbuf.at[s], dm_hbm.at[pl.ds(2 * c, 2)], dm_sem.at[s])
+
+    for cp in c_load(0, 0):
+        cp.start()
+
+    def c_step(u, carry):
+        for s in range(2):
+            c = 2 * u + s
+            for cp in c_load(c, s):
+                cp.wait()
+
+            @pl.when(c + 1 < NP)
+            def _():
+                for cp in c_load(c + 1, 1 - s):
+                    cp.start()
+
+            @pl.when(c >= 2)
+            def _():
+                dm_copy(c - 2, s).wait()
+
+            exchange(0, c + NP, 9, 12)
+            exchange(1, c, 6, 10)
+
+            @pl.when(c < 7)
+            def _():
+                od_pre(c + STEPS, False)
+
+            x = jnp.concatenate([bufs[s][0], bufs[s][1]], axis=1)
+            w = jnp.concatenate([wk[:, :W], wv[:, :W], wk[:, W:], wv[:, W:]], axis=1)
+            mbuf[s] = dotg(x, w, 1, 1).astype(BF).reshape(2, FP, D)
+            dm_copy(c, s).start()
+
+            @pl.when(c < 7)
+            def _():
+                od_post(c + STEPS, False)
+
+            @pl.when(c == 9)
+            def _():
+                pltpu.make_async_copy(res.at[0], res.at[0], res_recv).wait()
+                pltpu.make_async_copy(res, res_hbm, out_sem.at[2]).start()
+        return carry
+
+    lax.fori_loop(0, NP // 2, c_step, 0)
+    for t in range(NP, 10 + NCH + 2):
+        exchange(1, t, 6, 10)
+    for k in range(1, 4):
+        b_copy(k, (me + k) % 4).wait_recv()
+        b_copy(k, me).wait_send()
+    big1[0:8, :] = (bias[0, :, 0:W] + bias[1, :, 0:W]) + (bias[2, :, 0:W] + bias[3, :, 0:W])
+    big1[8:16, :] = (bias[0, :, W:] + bias[1, :, W:]) + (bias[2, :, W:] + bias[3, :, W:])
+    bias_out = pltpu.make_async_copy(big1.at[0:16], bias_hbm, out_sem.at[3])
+    bias_out.start()
+    dm_copy(NP - 2, 0).wait()
+    dm_copy(NP - 1, 1).wait()
+    dw_copy(0).wait()
+    dw_copy(1).wait()
+    pltpu.make_async_copy(res, res_hbm, out_sem.at[2]).wait()
+    bias_out.wait()
 
 
 def attention(m_pad, q, do, w_k, w_v, b_v):
@@ -244,16 +451,22 @@
     dma = pltpu.SemaphoreType.DMA
     return pl.pallas_call(
         attn_kernel, name="attention",
-        out_shape=(jax.ShapeDtypeStruct((2, NB * T, D), F32), jax.ShapeDtypeStruct((2, ACC, D), F32),
+        out_shape=(jax.ShapeDtypeStruct((2, NB * T, D), BF), jax.ShapeDtypeStruct((2, D, D), F32),
+                   jax.ShapeDtypeStruct((16, W), F32), jax.ShapeDtypeStruct((NB, FP, D), BF),
                    jax.ShapeDtypeStruct((2, NP, ROWS, D), BF)),
         in_specs=[hbm, vm, vm, vm, vm, vm],
-        out_specs=(hbm, hbm, hbm),
+        out_specs=(hbm,) * 5,
         scratch_shapes=[
             VMEM((2, 2, FP, D), BF), VMEM((2, ROWS, D), BF), VMEM((2, 4, FP, 128), F32), VMEM((2, 4, FP, 128), F32),
             VMEM((2, D, ROWS), BF), VMEM((4, 4, 16, 128), F32), VMEM((8, 128), F32), VMEM((2, ROWS, D), BF),
-            VMEM((2, ACC, D), F32), VMEM((2, 2, 64, W), F32),
-            dma((2,)), dma((2,)), dma((2,)), dma, dma((4, 3)), dma((4, 4))],
-        compiler_params=pltpu.CompilerParams(vmem_limit_bytes=60 << 20, collective_id=0, has_side_effects=True),
+            VMEM((2, D, D), F32), VMEM((4, 8, D), F32), VMEM((2, 2, 64, W), F32), VMEM((4, 64, W), F32),
+            VMEM((4, T, W), F32), VMEM((4, T, W), F32), VMEM((8, T, W), F32), VMEM((2, NB * T, D), BF),
+            VMEM((D, W), F32), VMEM((2, D // 2, W), F32),
+            dma((2,)), dma((2,)), dma((2,)), dma((4,)), dma((4, 3)), dma((4, 4)), dma((4,)), dma((4,)), dma((8,)), dma((8,)),
+            dma((8,)), dma((8,)), dma((4,)), dma((4,)), dma, dma((2,)), dma((2,)), dma((2, NCH)), dma((2, NCH)),
+            dma((2, NCH)), dma((2, NCH)), dma((2, NCH)), dma((2, NCH)), dma((2,)), dma((3,)), dma((4,)),
+            pltpu.SemaphoreType.REGULAR((2,)), pltpu.SemaphoreType.REGULAR((2,))],
+        compiler_params=pltpu.CompilerParams(vmem_limit_bytes=62 << 20, collective_id=0, has_side_effects=True),
     )(m_pad, q, do, w_k, w_v, b_v)
 
 
@@ -276,19 +489,16 @@
         q = (jnp.dot(x, w_q, preferred_element_type=F32) + b_q.astype(F32)).astype(BF)
         do = dotg(dy, w_o, 1, 1).astype(BF)
         m_pad = split_frames(memory.transpose(1, 0, 2))
-        od, dw, dkv = attention(m_pad, q, do, w_k, w_v, b_v.astype(F32).reshape(1, D))
-        od = lax.psum(od, "cp")
-        dw = lax.psum(dw, "cp")
-        grad_mem = join_frames(dm_product(dkv, w_k, w_v)).transpose(1, 0, 2)
-        o = od[0].astype(BF)
-        dq = od[1].astype(BF)
+        res, dw, bias, dm, _ = attention(m_pad, q, do, w_k, w_v, b_v.astype(F32).reshape(1, D))
+        grad_mem = join_frames(dm).transpose(1, 0, 2)
+        o, dq = res[0], res[1]
         out_y = (h + jnp.dot(o, w_o, preferred_element_type=F32) + b_o.astype(F32)).astype(BF)
         grad_wo = dotg(o, dy, 0, 0)
         grad_bo = jnp.sum(dy, axis=0, dtype=F32)
-        grad_wk = jnp.concatenate([dw[0, :D, :W], dw[1, :D, :W]], axis=1)
-        grad_wv = jnp.concatenate([dw[0, :D, W:], dw[1, :D, W:]], axis=1)
-        grad_bq = jnp.concatenate([dw[0, D, :W], dw[1, D, :W]])
-        grad_bv = jnp.concatenate([dw[0, D, W:], dw[1, D, W:]])
+        grad_wk = jnp.concatenate([dw[0, :, :W], dw[1, :, :W]], axis=1)
+        grad_wv = jnp.concatenate([dw[0, :, W:], dw[1, :, W:]], axis=1)
+        grad_bq = jnp.concatenate([bias[0], bias[1]])
+        grad_bv = jnp.concatenate([bias[8], bias[9]])
         grad_wq = dotg(x, dq, 0, 0)
         d_x = dotg(dq, w_q, 1, 1)
         grad_gain = jnp.sum(d_x * x_hat, axis=0)

time: 620 us -> 347 us (0.56)
  blocking collectives: 276 us -> 0 us
  between operations: 14.2 us -> 0.81 us
  Pallas kernels: 284 us -> 296 us
    psum x1 -> x0, blocking collectives: 276 us -> none  [device_step(): od = lax.psum(od, 'cp')]
    pallas_call x1, Pallas kernels: 171 us -> 244 us  [attention(): pl.pallas_call(attn_kernel, name='attention', out_shape=(jax.ShapeDtypeSt...]
    pallas_call x1 -> x0, Pallas kernels: 59.8 us -> none  [dm_product(): pl.pallas_call(dm_kernel, grid=(NP,), name='dm_product', out_shape=jax.Sh...]
  transfers between devices with their start and end apart: 1 -> 0, of which waited for: 0 -> 0; matrix products, arithmetic and copies ran while one was open for 3% -> 0% of each run, Pallas kernels for 14% -> 0%
where the time goes in v2:
time: 347 us; the launch traced here: 345 us
  Pallas kernels  296 us (85%)
  matrix products  25.5 us (7%)
  other arithmetic  15.7 us (5%)
  local copies, waits for them, and re-layouts  7.52 us (2%)
    pallas_call x1, Pallas kernels, attention(): pl.pallas_call(attn_kernel, name='attention', out_shape=(jax.ShapeDtypeSt...  244 us
    pallas_call x1, Pallas kernels, join_frames(): pl.pallas_call(join_kernel, grid=(NB // 8, D // 256), name='join_frames',...  26.2 us
    pallas_call x1, Pallas kernels, split_frames(): pl.pallas_call(split_kernel, grid=(NB // 8, D // 256), name='split_frames...  25.9 us
    dot_general x4, matrix products, dotg(): lax.dot_general(a, b, (((ca,), (cb,)), ((), ())), preferred_element_type=...  18.1 us

profile of v2, /device:TPU:0, one launch (start us, length us, event | category | flops | bytes accessed | tf_op | source)
XLA Modules:
  0.0 345.4 jit_solution(7030237819788298730)
XLA Ops:
  0.6 0.0 copy-start
  0.7 0.0 copy-start.4
  0.7 0.0 copy-start.5
  0.7 0.0 copy-start.6
  0.7 2.1 convert_reduce_fusion
  2.8 2.3 fusion.2
  5.1 0.1 rsqrt.13
  5.2 0.1 div.15
  5.2 0.0 copy-done.4
  5.2 0.0 copy-start.10
  5.2 0.0 copy-done.5
  5.3 0.0 copy-done
  5.3 0.8 fusion.12
  6.1 0.0 copy-done.6
  6.1 0.7 copy-done.10
  6.8 0.0 copy-start.2
  6.8 0.0 copy-start.12
  6.8 3.7 %add_convert_fusion.q = bf16[1024,1024]{1,0:T(8,128)(2,1)} fusion(f32[1024]{0:T(1024)S(1)} %convert_element_type.57, bf16[1024,1024]{1,0:T(8,128)(2,1)S(1)} %fusion.12, bf16[1024,1024]{1,0:T(8,128)(2,1)S(1)} %copy-done.10), kind=kOutput, calls=%fused_computation.28 | convolution fusion | flops 2149580800 | bytes 6295552 | tf_op jit(solution)/shard_map/dot_general | solution.py:489
  10.5 0.0 copy-done.2
  10.5 0.0 copy-done.12
  10.5 3.7 %convolution_convert_fusion.do = bf16[1024,1024]{1,0:T(8,128)(2,1)} fusion(bf16[1024,1024]{1,0:T(8,128)(2,1)S(1)} %bitcast.77, bf16[1024,1024]{1,0:T(8,128)(2,1)S(1)} %copy-done.12), kind=kOutput, calls=%fused_computation.42 | convolution fusion | flops 2148532224 | bytes 6291456 | tf_op jit(solution)/shard_map/dot_general | solution.py:25
  14.2 0.0 copy-start.7
  14.2 25.9 %split_frames.1.m_hbm = bf16[32,384,1024]{2,1,0:T(8,128)(2,1)} custom-call(bf16[375,32,1024]{2,1,0:T(8,128)(2,1)} %bitcast.75), custom_call_target="tpu_custom_call" | custom-call | tf_op jit(solution)/shard_map/split_frames/pallas_call | solution.py:40
  40.2 0.0 copy-done.7
  40.2 0.6 reshape.110
  40.7 243.7 %attention.1 = (bf16[2,1024,1024]{2,1,0:T(8,128)(2,1)}, f32[2,1024,1024]{2,1,0:T(8,128)}, f32[16,512]{1,0:T(8,128)}, bf16[32,384,1024]{2,1,0:T(8,128)(2,1)}, bf16[2,16,768,1024]{3,2,1,0:T(8,128)(2,1)}) custom-call(bf16[32,384,1024]{2,1,0:T(8,128)(2,1)} %split_frames.1.m_hbm, bf16[1024,1024]{1,0:T(8,128)(2,1)} %add_convert_fusion.q, ...), custom_call_target="tpu_custom_call" | custom-call | tf_op jit(solution)/shard_map/attention/pallas_call | solution.py:452
  284.5 4.5 %slice_bitcast_fusion.1 = (f32[1024,512]{1,0:T(8,128)S(1)}, f32[1024,512]{1,0:T(8,128)S(1)}, f32[1024,512]{1,0:T(8,128)S(1)}, f32[1024,512]{1,0:T(8,128)S(1)}) fusion(f32[2,1024,1024]{2,1,0:T(8,128)} %get-tuple-element.19), kind=kLoop, calls=%fused_computation.39 | loop fusion | bytes 16777216 | tf_op jit(solution)/shard_map/squeeze | solution.py:499
  288.9 0.0 copy-start.1
  288.9 0.0 copy-start.11
  288.9 4.6 %pad_maximum_fusion = (f32[1024,1024]{1,0:T(8,128)}, f32[1024,1024]{1,0:T(8,128)}) fusion(f32[1024,512]{1,0:T(8,128)S(1)} %get-tuple-element.26, f32[1024,512]{1,0:T(8,128)S(1)} %get-tuple-element.27, f32[1024,512]{1,0:T(8,128)S(1)} %get-tuple-element.25, f32[1024,512]{1,0:T(8,128)S(1)} %get-tuple-element.24), kind=kLoop, calls=%fused_computation | loop fusion | flops 2097152 | bytes 16777216 | tf_op jit(solution)/shard_map/concatenate | solution.py:498
  293.6 0.8 fusion.35
  294.4 0.6 pad_maximum_fusion.2
  295.0 0.0 copy-done.1
  295.0 0.0 copy-done.11
  295.0 0.0 copy-start.3
  295.0 5.6 %fusion.18 = (f32[1024]{0:T(1024)}, f32[1024]{0:T(1024)S(1)}, f32[1024]{0:T(1024)S(1)}, f32[1024]{0:T(1024)}, f32[1024,1024]{1,0:T(8,128)S(1)}) fusion(bf16[32,32,1024]{2,1,0:T(8,128)(2,1)S(1)} %copy-done.1, f32[1024]{0:T(1024)S(1)} %rsqrt.13, f32[1024]{0:T(1024)S(1)} %div.15, f32[1024]{0:T(1024)S(1)} %convert_element_type.54, ...), kind=kOutput, calls=%fused_computation.24 | convolution fusion | flops 2157965312 | bytes 10514432 | tf_op jit(solution)/shard_map/dot_general | solution.py:25
  300.6 0.0 copy-done.3
  300.6 2.9 fusion.17
  303.5 0.0 copy-start.9
  303.5 0.8 fusion.5
  304.4 1.4 copy-done.9
  305.7 4.4 %fusion.21 = f32[1024,1024]{1,0:T(8,128)} fusion(bf16[1024,1024]{1,0:T(8,128)(2,1)S(1)} %bitcast.80, bf16[2,1024,1024]{2,1,0:T(8,128)(2,1)S(1)} %copy-done.9), kind=kOutput, calls=%fused_computation.30 | convolution fusion | flops 2147483648 | bytes 8388608 | tf_op jit(solution)/shard_map/dot_general | solution.py:25
  310.1 0.0 copy-start.8
  310.1 0.0 copy-start.13
  310.1 4.4 %fusion.25 = f32[1024,1024]{1,0:T(8,128)} fusion(bf16[1024,1024]{1,0:T(8,128)(2,1)S(1)} %bitcast.78, bf16[2,1024,1024]{2,1,0:T(8,128)(2,1)S(1)} %copy-done.9), kind=kOutput, calls=%fused_computation.34 | convolution fusion | flops 2147483648 | bytes 8388608 | tf_op jit(solution)/shard_map/dot_general | solution.py:25
  314.5 0.0 copy-done.8
  314.5 0.0 copy-done.13
  314.5 3.7 %fusion.20 = bf16[1024,1024]{1,0:T(8,128)(2,1)} fusion(bf16[32,32,1024]{2,1,0:T(8,128)(2,1)S(1)} %copy-done.1, f32[1024]{0:T(1024)S(1)} %convert_element_type.60, bf16[1024,1024]{1,0:T(8,128)(2,1)S(1)} %copy-done.13, bf16[2,1024,1024]{2,1,0:T(8,128)(2,1)S(1)} %copy-done.9), kind=kOutput, calls=%fused_computation.26 | convolution fusion | flops 2151677952 | bytes 8392704 | tf_op jit(solution)/shard_map/dot_general | solution.py:495
  318.2 26.2 %join_frames.1 = bf16[375,32,1024]{2,1,0:T(8,128)(2,1)} custom-call(bf16[32,384,1024]{2,1,0:T(8,128)(2,1)} %get-tuple-element.17.x_ref), custom_call_target="tpu_custom_call" | custom-call | tf_op jit(solution)/shard_map/join_frames/pallas_call | solution.py:60
  344.4 1.0 convert_reduce_fusion.1
  (7 shorter events, 0.0 us)
Async XLA Ops:
  0.6 4.6 %copy-start = (bf16[32,32,1024]{2,1,0:T(8,128)(2,1)S(1)}, bf16[32,32,1024]{2,1,0:T(8,128)(2,1)}, u32[]{:S(2)}) copy-start(bf16[32,32,1024]{2,1,0:T(8,128)(2,1)} %param.12) | copy-start | bytes 6291460
  0.7 4.6 %copy-start.4 = (bf16[1024]{0:T(1024)(128)(2,1)S(1)}, bf16[1024]{0:T(1024)(128)(2,1)}, u32[]{:S(2)}) copy-start(bf16[1024]{0:T(1024)(128)(2,1)} %param.14) | copy-start | bytes 6148
  0.7 4.6 %copy-start.5 = (bf16[1024]{0:T(1024)(128)(2,1)S(1)}, bf16[1024]{0:T(1024)(128)(2,1)}, u32[]{:S(2)}) copy-start(bf16[1024]{0:T(1024)(128)(2,1)} %param.15) | copy-start | bytes 6148
  0.7 5.4 %copy-start.6 = (bf16[1024]{0:T(1024)(128)(2,1)S(1)}, bf16[1024]{0:T(1024)(128)(2,1)}, u32[]{:S(2)}) copy-start(bf16[1024]{0:T(1024)(128)(2,1)} %param.17) | copy-start | bytes 6148
  5.2 1.6 copy-start.10
  6.8 3.7 %copy-start.2 = (bf16[32,32,1024]{2,1,0:T(8,128)(2,1)S(1)}, bf16[32,32,1024]{2,1,0:T(8,128)(2,1)}, u32[]{:S(2)}) copy-start(bf16[32,32,1024]{2,1,0:T(8,128)(2,1)} %param.23) | copy-start | bytes 6291460
  6.8 3.7 %copy-start.12 = (bf16[1024,1024]{1,0:T(8,128)(2,1)S(1)}, bf16[1024,1024]{1,0:T(8,128)(2,1)}, u32[]{:S(2)}) copy-start(bf16[1024,1024]{1,0:T(8,128)(2,1)} %param.21) | copy-start | bytes 6291460
  14.2 25.9 %copy-start.7 = (bf16[1024]{0:T(1024)(128)(2,1)S(1)}, bf16[1024]{0:T(1024)(128)(2,1)}, u32[]{:S(2)}) copy-start(bf16[1024]{0:T(1024)(128)(2,1)} %param.20) | copy-start | bytes 6148
  288.9 6.1 %copy-start.1 = (bf16[32,32,1024]{2,1,0:T(8,128)(2,1)S(1)}, bf16[32,32,1024]{2,1,0:T(8,128)(2,1)}, u32[]{:S(2)}) copy-start(bf16[32,32,1024]{2,1,0:T(8,128)(2,1)} %param.12) | copy-start | bytes 6291460
  288.9 6.1 %copy-start.11 = (bf16[1024,1024]{1,0:T(8,128)(2,1)S(1)}, bf16[1024,1024]{1,0:T(8,128)(2,1)}, u32[]{:S(2)}) copy-start(bf16[1024,1024]{1,0:T(8,128)(2,1)} %param.16) | copy-start | bytes 6291460
  295.0 5.6 %copy-start.3 = (bf16[32,32,1024]{2,1,0:T(8,128)(2,1)S(1)}, bf16[32,32,1024]{2,1,0:T(8,128)(2,1)}, u32[]{:S(2)}) copy-start(bf16[32,32,1024]{2,1,0:T(8,128)(2,1)} %param.23) | copy-start | bytes 6291460
  303.5 2.2 copy-start.9
  310.1 4.4 %copy-start.8 = (bf16[1024]{0:T(1024)(128)(2,1)S(1)}, bf16[1024]{0:T(1024)(128)(2,1)}, u32[]{:S(2)}) copy-start(bf16[1024]{0:T(1024)(128)(2,1)} %param.22) | copy-start | bytes 6148
  310.1 4.4 %copy-start.13 = (bf16[1024,1024]{1,0:T(8,128)(2,1)S(1)}, bf16[1024,1024]{1,0:T(8,128)(2,1)}, u32[]{:S(2)}) copy-start(bf16[1024,1024]{1,0:T(8,128)(2,1)} %param.21) | copy-start | bytes 6291460

commit v3 on v2

--- a/solution.py
+++ b/solution.py
@@ -19,52 +19,186 @@
 LOG2 = 0.125 * math.log2(math.e)
 MESH = pl.DeviceIdType.MESH
 VMEM = pltpu.VMEM
+B2, B4, B8, LANES = 2, 4, 8, 128
+TOK = NB * T
+SDS = jax.ShapeDtypeStruct
 
 
 def dotg(a, b, ca, cb):
     return lax.dot_general(a, b, (((ca,), (cb,)), ((), ())), preferred_element_type=F32)
 
 
-def split_kernel(x_ref, o_ref, s_ref):
-    x = x_ref[...].astype(F32).reshape(8 * F, 256)
-    for t in range(2):
-        s_ref[t] = x[:, 128 * t:128 * (t + 1)]
-    for b in range(8):
-        for t in range(2):
-            y = s_ref[t, pl.ds(b, F, stride=8), :].astype(BF)
-            o_ref[b, 0:F, 128 * t:128 * (t + 1)] = y
-            o_ref[b, 368:FP, 128 * t:128 * (t + 1)] = jnp.concatenate([y[368:F], jnp.zeros((FP - F, 128), BF)], axis=0)
-
-
-def split_frames(mt):
+FC = 64
+NFC = FP // FC
+
+
+def fixed(rows):
+    return pl.BlockSpec((rows, D), lambda s: (0, 0), pipeline_mode=pl.Buffered(1))
+
+
+def lanes(t):
+    return slice(LANES * t, LANES * (t + 1))
+
+
+def norm_parts(h):
+    centered = h - jnp.mean(h, axis=-1, keepdims=True)
+    inv_std = lax.rsqrt(jnp.mean(centered * centered, axis=-1, keepdims=True) + EPS)
+    return centered * inv_std, inv_std
+
+
+def prep_kernel(m_ref, h_ref, dy_ref, gain, shift, wq, bq, wo, mp_ref, q_ref, do_ref, s_ref):
+    step = pl.program_id(0)
+
+    @pl.when(step < TOK // LANES)
+    def _():
+        x_hat, _ = norm_parts(h_ref[...].astype(F32))
+        x = (x_hat * gain[...] + shift[...]).astype(BF)
+        q_ref[...] = (jnp.dot(x, wq[...], preferred_element_type=F32) + bq[...]).astype(BF)
+        do_ref[...] = dotg(dy_ref[...], wo[...], 1, 1).astype(BF)
+
+    x = m_ref[...].astype(F32).reshape(B8 * FC, D)
+    for t in range(D // LANES):
+        s_ref[t] = x[:, lanes(t)]
+    real = lax.broadcasted_iota(jnp.int32, (FC, LANES), 0) + FC * (step % NFC) < F
+    for b in range(B8):
+        for t in range(D // LANES):
+            y = jnp.where(real, s_ref[t, pl.ds(b, FC, stride=B8), :], 0.0)
+            mp_ref[b, :, lanes(t)] = y.astype(BF)
+
+
+def prepare(mt, h, dy, gain, shift, w_q, b_q, w_o):
+    tok = pl.BlockSpec((LANES, D), lambda s: (jnp.minimum(s, TOK // LANES - 1), 0))
+    vec, mat = fixed(1), fixed(D)
     return pl.pallas_call(
-        split_kernel, grid=(NB // 8, D // 256), name="split_frames",
-        out_shape=jax.ShapeDtypeStruct((NB, FP, D), BF),
-        in_specs=[pl.BlockSpec((F, 8, 256), lambda b, c: (0, b, c))],
-        out_specs=pl.BlockSpec((8, FP, 256), lambda b, c: (b, 0, c)),
-        scratch_shapes=[VMEM((2, 8 * F, 128), F32)],
+        prep_kernel, grid=(NB // B8 * NFC,), name="prepare",
+        out_shape=(SDS((NB, FP, D), BF), SDS((TOK, D), BF), SDS((TOK, D), BF)),
+        in_specs=[pl.BlockSpec((FC, B8, D), lambda s: (s % NFC, s // NFC, 0)), tok, tok, vec, vec, mat, vec, mat],
+        out_specs=(pl.BlockSpec((B8, FC, D), lambda s: (s // NFC, s % NFC, 0)), tok, tok),
+        scratch_shapes=[VMEM((D // LANES, B8 * FC, LANES), F32)],
         compiler_params=pltpu.CompilerParams(vmem_limit_bytes=40 << 20),
-    )(mt)
-
-
-def join_kernel(x_ref, o_ref, s_ref):
-    for b in range(8):
-        x = x_ref[b, 0:F, :].astype(F32)
-        for t in range(2):
-            s_ref[t, pl.ds(b, F, stride=8), :] = x[:, 128 * t:128 * (t + 1)]
-    y = jnp.concatenate([s_ref[0], s_ref[1]], axis=1)
-    o_ref[...] = y.reshape(F, 8, 256).astype(BF)
-
-
-def join_frames(x):
+    )(mt, h, dy, gain, shift, w_q, b_q, w_o)
+
+
+JOB0, JOBS, RC = 3, 4, 256
+
+
+def finish_kernel(dm_ref, res_hbm, h_hbm, dy_hbm, wo_hbm, wq_hbm, dw_hbm, gain, shift, bo,
+                  gm_ref, y_hbm, gh_hbm, gwo_hbm, gwq_hbm, gwk_hbm, gwv_hbm, vec_ref,
+                  s_ref, res, h, dy, wo, wq, x, y, gh, gw, stage, in_sem, y_sem, gh_sem, gw_sem, ld_sem, st_sem):
+    step = pl.program_id(0)
+    loads = [pltpu.make_async_copy(a, b, in_sem.at[k]) for k, (a, b) in enumerate(
+        ((h_hbm, h), (res_hbm, res), (wo_hbm, wo), (dy_hbm, dy), (wq_hbm, wq)))]
+
+    def rows(n):
+        return pl.ds(pl.multiple_of(RC * n, RC), RC)
+
+    def out_copy(src, dst, sem, n):
+        return pltpu.make_async_copy(src.at[rows(n)], dst.at[rows(n)], sem.at[n])
+
+    def gw_copy(dst, n):
+        return pltpu.make_async_copy(gw.at[n], dst.at[rows(n)], gw_sem.at[n])
+
+    def piece_in(k):
+        g, v = k // 2, k % 2
+        return pltpu.make_async_copy(dw_hbm.at[g, :, pl.ds(W * v, W)], stage.at[k % 2], ld_sem.at[k % 2])
+
+    def piece_out(k):
+        g, v = k // 2, k % 2
+        return pltpu.make_async_copy(stage.at[k % 2], (gwk_hbm, gwv_hbm)[v].at[:, pl.ds(W * g, W)], st_sem.at[k % 2])
+
+    @pl.when(step == 0)
+    def _():
+        for cp in loads:
+            cp.start()
+        piece_in(0).start()
+        piece_in(1).start()
+        vec_ref[...] = jnp.zeros_like(vec_ref)
+
+    for k in range(4):
+        @pl.when(step == 4 + 5 * (k // 2) + k % 2)
+        def _():
+            piece_in(k).wait()
+            piece_out(k).start()
+
+        @pl.when(step == 7 + 5 * (k // 2) + k % 2)
+        def _():
+            if k < 2:
+                piece_out(k).wait()
+                piece_in(k + 2).start()
+
+    @pl.when(step == JOB0)
+    def _():
+        for cp in loads:
+            cp.wait()
+
+    job = step - JOB0
+    n = job % JOBS
+
+    @pl.when((job >= 0) & (job < JOBS))
+    def _():
+        hf = h[rows(n)].astype(F32)
+        x_hat, _ = norm_parts(hf)
+        x[rows(n)] = (x_hat * gain[...] + shift[...]).astype(BF)
+        y[rows(n)] = (hf + jnp.dot(res[0, rows(n)], wo[...], preferred_element_type=F32) + bo[...]).astype(BF)
+        out_copy(y, y_hbm, y_sem, n).start()
+
+    @pl.when((job >= JOBS) & (job < 2 * JOBS))
+    def _():
+        gw[n] = dotg(res[0, :, rows(n)], dy[...], 0, 0)
+        gw_copy(gwo_hbm, n).start()
+
+    @pl.when((job >= 2 * JOBS) & (job < 3 * JOBS))
+    def _():
+        x_hat, inv_std = norm_parts(h[rows(n)].astype(F32))
+        dyf = dy[rows(n)].astype(F32)
+        d_x = dotg(res[1, rows(n)], wq[...], 1, 1)
+        vec_ref[0:1] += jnp.sum(d_x * x_hat, axis=0, keepdims=True)
+        vec_ref[1:2] += jnp.sum(d_x, axis=0, keepdims=True)
+        vec_ref[2:3] += jnp.sum(dyf, axis=0, keepdims=True)
+        d_hat = d_x * gain[...]
+        d_h = inv_std * (d_hat - jnp.mean(d_hat, axis=-1, keepdims=True) - x_hat * jnp.mean(d_hat * x_hat, axis=-1, keepdims=True))
+        gh[rows(n)] = (dyf + d_h).astype(BF)
+        out_copy(gh, gh_hbm, gh_sem, n).start()
+
+    @pl.when((job >= 3 * JOBS) & (job < 4 * JOBS))
+    def _():
+        gw_copy(gwo_hbm, n).wait()
+        gw[n] = dotg(x[:, rows(n)], res[1], 0, 0)
+        gw_copy(gwq_hbm, n).start()
+
+    for b in range(B8):
+        z = dm_ref[b].astype(F32)
+        for t in range(D // LANES):
+            s_ref[t, pl.ds(b, FC, stride=B8), :] = z[:, lanes(t)]
+    z = jnp.concatenate([s_ref[t] for t in range(D // LANES)], axis=1)
+    gm_ref[...] = z.reshape(FC, B8, D).astype(BF)
+
+    @pl.when(step == pl.num_programs(0) - 1)
+    def _():
+        for k in range(JOBS):
+            out_copy(y, y_hbm, y_sem, k).wait()
+            out_copy(gh, gh_hbm, gh_sem, k).wait()
+            gw_copy(gwq_hbm, k).wait()
+        for k in (2, 3):
+            piece_out(k).wait()
+
+
+def finish(dm, res, h, dy, w_o, w_q, dw, gain, shift, b_o):
+    hbm = pl.BlockSpec(memory_space=pl.ANY)
+    vec = fixed(1)
+    dma = pltpu.SemaphoreType.DMA
+    mat, dj = VMEM((D, D), BF), dma((JOBS,))
     return pl.pallas_call(
-        join_kernel, grid=(NB // 8, D // 256), name="join_frames",
-        out_shape=jax.ShapeDtypeStruct((F, NB, D), BF),
-        in_specs=[pl.BlockSpec((8, FP, 256), lambda b, c: (b, 0, c))],
-        out_specs=pl.BlockSpec((F, 8, 256), lambda b, c: (0, b, c)),
-        scratch_shapes=[VMEM((2, 8 * F, 128), F32)],
-        compiler_params=pltpu.CompilerParams(vmem_limit_bytes=40 << 20),
-    )(x)
+        finish_kernel, grid=(NB // B8 * NFC,), name="finish",
+        out_shape=(SDS((F, NB, D), BF), SDS((TOK, D), BF), SDS((TOK, D), BF), SDS((D, D), F32), SDS((D, D), F32),
+                   SDS((D, D), F32), SDS((D, D), F32), SDS((B8, D), F32)),
+        in_specs=[pl.BlockSpec((B8, FC, D), lambda s: (s // NFC, s % NFC, 0))] + [hbm] * 6 + [vec] * 3,
+        out_specs=(pl.BlockSpec((FC, B8, D), lambda s: (s % NFC, s // NFC, 0)),) + (hbm,) * 6 + (pl.BlockSpec((B8, D), lambda s: (0, 0)),),
+        scratch_shapes=[
+            VMEM((D // LANES, B8 * FC, LANES), F32), VMEM((B2, TOK, D), BF), mat, mat, mat, mat, mat, mat, mat, VMEM((JOBS, RC, D), F32),
+            VMEM((B2, D, W), F32), dma((B8,)), dj, dj, dj, dma((B2,)), dma((B2,))],
+        compiler_params=pltpu.CompilerParams(vmem_limit_bytes=50 << 20),
+    )(dm, res, h, dy, w_o, w_q, dw, gain, shift, b_o)
 
 
 def block_mask():
@@ -449,23 +583,23 @@
     vm = pl.BlockSpec(memory_space=VMEM)
     hbm = pl.BlockSpec(memory_space=pl.ANY)
     dma = pltpu.SemaphoreType.DMA
+    d2, d4, d8, dn = dma((B2,)), dma((B4,)), dma((B8,)), dma((B2, NCH))
+    credit = pltpu.SemaphoreType.REGULAR((B2,))
+    probs = VMEM((B2, B4, FP, LANES), F32)
     return pl.pallas_call(
         attn_kernel, name="attention",
-        out_shape=(jax.ShapeDtypeStruct((2, NB * T, D), BF), jax.ShapeDtypeStruct((2, D, D), F32),
-                   jax.ShapeDtypeStruct((16, W), F32), jax.ShapeDtypeStruct((NB, FP, D), BF),
-                   jax.ShapeDtypeStruct((2, NP, ROWS, D), BF)),
+        out_shape=(SDS((B2, TOK, D), BF), SDS((B2, D, D), F32), SDS((2 * B8, W), F32), SDS((NB, FP, D), BF),
+                   SDS((B2, NP, ROWS, D), BF)),
         in_specs=[hbm, vm, vm, vm, vm, vm],
         out_specs=(hbm,) * 5,
         scratch_shapes=[
-            VMEM((2, 2, FP, D), BF), VMEM((2, ROWS, D), BF), VMEM((2, 4, FP, 128), F32), VMEM((2, 4, FP, 128), F32),
-            VMEM((2, D, ROWS), BF), VMEM((4, 4, 16, 128), F32), VMEM((8, 128), F32), VMEM((2, ROWS, D), BF),
-            VMEM((2, D, D), F32), VMEM((4, 8, D), F32), VMEM((2, 2, 64, W), F32), VMEM((4, 64, W), F32),
-            VMEM((4, T, W), F32), VMEM((4, T, W), F32), VMEM((8, T, W), F32), VMEM((2, NB * T, D), BF),
-            VMEM((D, W), F32), VMEM((2, D // 2, W), F32),
-            dma((2,)), dma((2,)), dma((2,)), dma((4,)), dma((4, 3)), dma((4, 4)), dma((4,)), dma((4,)), dma((8,)), dma((8,)),
-            dma((8,)), dma((8,)), dma((4,)), dma((4,)), dma, dma((2,)), dma((2,)), dma((2, NCH)), dma((2, NCH)),
-            dma((2, NCH)), dma((2, NCH)), dma((2, NCH)), dma((2, NCH)), dma((2,)), dma((3,)), dma((4,)),
-            pltpu.SemaphoreType.REGULAR((2,)), pltpu.SemaphoreType.REGULAR((2,))],
+            VMEM((B2, B2, FP, D), BF), VMEM((B2, ROWS, D), BF), probs, probs, VMEM((B2, D, ROWS), BF),
+            VMEM((B4, B4, 2 * B8, LANES), F32), VMEM((B8, LANES), F32), VMEM((B2, ROWS, D), BF),
+            VMEM((B2, D, D), F32), VMEM((B4, B8, D), F32), VMEM((B2, B2, 2 * T, W), F32), VMEM((B4, 2 * T, W), F32),
+            VMEM((B4, T, W), F32), VMEM((B4, T, W), F32), VMEM((B8, T, W), F32), VMEM((B2, TOK, D), BF),
+            VMEM((D, W), F32), VMEM((B2, D // 2, W), F32),
+            d2, d2, d2, d4, dma((B4, B4)), dma((B4, B4)), d4, d4, d8, d8, d8, d8, d4, d4, dma, d2, d2, dn, dn, dn, dn, dn, dn, d2, d4, d4,
+            credit, credit],
         compiler_params=pltpu.CompilerParams(vmem_limit_bytes=62 << 20, collective_id=0, has_side_effects=True),
     )(m_pad, q, do, w_k, w_v, b_v)
 
@@ -479,34 +613,15 @@
     out_specs = (act_spec, act_spec, mem_spec, vec_out, vec_out, mat_out, vec_out, mat_out, mat_out, vec_out, mat_out, vec_out)
 
     def device_step(hidden, memory, ln_gain, ln_bias, w_q, b_q, w_k, w_v, b_v, w_o, b_o, grad_y):
-        h = hidden.reshape(NB * T, D).astype(F32)
-        dy = grad_y.reshape(NB * T, D)
-        centered = h - jnp.mean(h, axis=-1, keepdims=True)
-        inv_std = lax.rsqrt(jnp.mean(centered * centered, axis=-1, keepdims=True) + EPS)
-        x_hat = centered * inv_std
-        gain = ln_gain.astype(F32)
-        x = (x_hat * gain + ln_bias.astype(F32)).astype(BF)
-        q = (jnp.dot(x, w_q, preferred_element_type=F32) + b_q.astype(F32)).astype(BF)
-        do = dotg(dy, w_o, 1, 1).astype(BF)
-        m_pad = split_frames(memory.transpose(1, 0, 2))
-        res, dw, bias, dm, _ = attention(m_pad, q, do, w_k, w_v, b_v.astype(F32).reshape(1, D))
-        grad_mem = join_frames(dm).transpose(1, 0, 2)
-        o, dq = res[0], res[1]
-        out_y = (h + jnp.dot(o, w_o, preferred_element_type=F32) + b_o.astype(F32)).astype(BF)
-        grad_wo = dotg(o, dy, 0, 0)
-        grad_bo = jnp.sum(dy, axis=0, dtype=F32)
-        grad_wk = jnp.concatenate([dw[0, :, :W], dw[1, :, :W]], axis=1)
-        grad_wv = jnp.concatenate([dw[0, :, W:], dw[1, :, W:]], axis=1)
-        grad_bq = jnp.concatenate([bias[0], bias[1]])
-        grad_bv = jnp.concatenate([bias[8], bias[9]])
-        grad_wq = dotg(x, dq, 0, 0)
-        d_x = dotg(dq, w_q, 1, 1)
-        grad_gain = jnp.sum(d_x * x_hat, axis=0)
-        grad_bias = jnp.sum(d_x, axis=0)
-        d_hat = d_x * gain
-        d_h = inv_std * (d_hat - jnp.mean(d_hat, axis=-1, keepdims=True) - x_hat * jnp.mean(d_hat * x_hat, axis=-1, keepdims=True))
-        grad_h = (dy.astype(F32) + d_h).astype(BF)
-        return (out_y.reshape(NB, T, D), grad_h.reshape(NB, T, D), grad_mem, grad_gain, grad_bias, grad_wq, grad_bq,
-                grad_wk, grad_wv, grad_bv, grad_wo, grad_bo)
+        h = hidden.reshape(TOK, D)
+        dy = grad_y.reshape(TOK, D)
+        gain, shift, bq, bv, bo = (a.astype(F32).reshape(1, D) for a in (ln_gain, ln_bias, b_q, b_v, b_o))
+        m_pad, q, do = prepare(memory.transpose(1, 0, 2), h, dy, gain, shift, w_q, bq, w_o)
+        res, dw, bias, dm, _ = attention(m_pad, q, do, w_k, w_v, bv)
+        gm, y, gh, gwo, gwq, gwk, gwv, vec = finish(dm, res, h, dy, w_o, w_q, dw, gain, shift, bo)
+        grad_bq = bias[0:2].reshape(D)
+        grad_bv = bias[8:10].reshape(D)
+        return (y.reshape(NB, T, D), gh.reshape(NB, T, D), gm.transpose(1, 0, 2), vec[0], vec[1], gwq, grad_bq,
+                gwk, gwv, grad_bv, gwo, vec[2])
 
     return jax.shard_map(device_step, mesh=mesh, in_specs=in_specs, out_specs=out_specs, check_vma=False)

time: 347 us -> 343 us (0.988)
  Pallas kernels: 296 us -> 325 us
  matrix products: 25.5 us -> 0 us
  other arithmetic: 15.7 us -> 2.65 us
  local copies, waits for them, and re-layouts: 7.52 us -> 13.1 us
    pallas_call x3, Pallas kernels: 296 us -> 325 us  [the longest x1 244 us: attention(): pl.pallas_call(attn_kernel, name='attention', out_shape=(SDS((B2, TOK, D)...]
    dot_general x6 -> x0, matrix products: 25.5 us -> none  [the longest x4 18.1 us: dotg(): lax.dot_general(a, b, (((ca,), (cb,)), ((), ())), preferred_element_type=...]
    unnamed x28 -> x21, local copies, waits for them, and re-layouts: 2.13 us -> 12.5 us
    reduce_sum x3 -> x0, other arithmetic: 5.32 us -> none  [the longest x1 2.29 us: device_step(): jnp.mean(centered * centered, axis=-1, keepdims=True) + EPS]
    concatenate x2 -> x0, other arithmetic: 5.24 us -> none  [the longest x1 4.64 us: device_step(): grad_wk = jnp.concatenate([dw[0, :, :W], dw[1, :, :W]], axis=1)]
    convert_element_type x7 -> x0, other arithmetic: 4.55 us -> none  [the longest x1 2.91 us: device_step(): grad_h = (dy.astype(F32) + d_h).astype(BF)]
    squeeze x1 -> x0, local copies, waits for them, and re-layouts: 4.45 us -> none  [device_step(): grad_wv = jnp.concatenate([dw[0, :, W:], dw[1, :, W:]], axis=1)]
where the time goes in v3:
time: 343 us; the launch traced here: 341 us
  Pallas kernels  325 us (95%)
  local copies, waits for them, and re-layouts  13.1 us (4%)
    pallas_call x1, Pallas kernels, attention(): pl.pallas_call(attn_kernel, name='attention', out_shape=(SDS((B2, TOK, D)...  244 us
    pallas_call x1, Pallas kernels, finish(): pl.pallas_call(finish_kernel, grid=(NB // B8 * NFC,), name='finish', out_...  43.9 us
    pallas_call x1, Pallas kernels, prepare(): pl.pallas_call(prep_kernel, grid=(NB // B8 * NFC,), name='prepare', out_s...  37.3 us
    unnamed x21, local copies, waits for them, and re-layouts  12.5 us

profile of v3, /device:TPU:0, one launch (start us, length us, event | category | flops | bytes accessed | tf_op | source)
XLA Modules:
  0.0 341.5 jit_solution(7329185920893942609)
XLA Ops:
  0.6 0.7 reshape.83
  1.3 0.7 reshape.85
  2.0 0.7 reshape.87
  2.7 0.0 copy-start
  2.7 1.6 copy-done
  4.3 0.0 copy-start.2
  4.3 1.6 copy-done.2
  5.9 0.0 copy-start.3
  5.9 1.6 copy-done.3
  7.5 0.0 copy-start.4
  7.5 1.6 copy-done.4
  9.1 0.0 copy-start.7
  9.1 37.3 %prepare.1 = (bf16[32,384,1024]{2,1,0:T(8,128)(2,1)}, bf16[1024,1024]{1,0:T(8,128)(2,1)S(1)}, bf16[1024,1024]{1,0:T(8,128)(2,1)S(1)}) custom-call(bf16[375,32,1024]{2,1,0:T(8,128)(2,1)} %bitcast.30, bf16[1024,1024]{1,0:T(8,128)(2,1)S(1)} %bitcast.20, bf16[1024,1024]{1,0:T(8,128)(2,1)S(1)} %bitcast.23, f32[1,1024]{1,0:T(1,128)S(1)} %bitcast.24, ...), custom_call_target="tpu_custom_call" | custom-call | tf_op jit(solution)/shard_map/prepare/pallas_call | solution.py:72
  46.4 0.0 copy-start.5
  46.4 1.3 copy-done.5
  47.7 0.0 copy-start.6
  47.7 1.3 copy-done.6
  49.0 0.0 copy-done.7
  49.0 0.6 reshape.89
  49.6 0.0 copy-start.8
  49.6 243.8 %attention.1 = (bf16[2,1024,1024]{2,1,0:T(8,128)(2,1)}, f32[2,1024,1024]{2,1,0:T(8,128)}, f32[16,512]{1,0:T(8,128)}, bf16[32,384,1024]{2,1,0:T(8,128)(2,1)}, bf16[2,16,768,1024]{3,2,1,0:T(8,128)(2,1)}) custom-call(bf16[32,384,1024]{2,1,0:T(8,128)(2,1)} %get-tuple-element.27.m_hbm, bf16[1024,1024]{1,0:T(8,128)(2,1)} %copy-done.5, ...), custom_call_target="tpu_custom_call" | custom-call | tf_op jit(solution)/shard_map/attention/pallas_call | solution.py:589
  293.4 0.0 copy-done.8
  293.5 0.0 copy-start.1
  293.5 1.6 copy-done.1
  295.0 43.9 %finish.1 = (bf16[375,32,1024]{2,1,0:T(8,128)(2,1)}, bf16[1024,1024]{1,0:T(8,128)(2,1)}, bf16[1024,1024]{1,0:T(8,128)(2,1)}, f32[1024,1024]{1,0:T(8,128)}, f32[1...) custom-call(bf16[32,384,1024]{2,1,0:T(8,128)(2,1)} %get-tuple-element.30.dm_ref, ...), custom_call_target="tpu_custom_call" | custom-call | tf_op jit(solution)/shard_map/finish/pallas_call | solution.py:191
  338.9 0.6 fusion
  339.5 0.7 slice_bitcast_fusion
  340.3 0.6 copy.24
  340.9 0.6 copy.25
  (1 shorter events, 0.0 us)
Async XLA Ops:
  2.7 1.6 copy-start
  4.3 1.6 copy-start.2
  5.9 1.6 copy-start.3
  7.5 1.6 copy-start.4
  9.1 40.0 %copy-start.7 = (bf16[1024]{0:T(1024)(128)(2,1)S(1)}, bf16[1024]{0:T(1024)(128)(2,1)}, u32[]{:S(2)}) copy-start(bf16[1024]{0:T(1024)(128)(2,1)} %param.20) | copy-start | bytes 6148
  46.4 1.3 copy-start.5
  47.7 1.3 copy-start.6
  49.6 243.8 %copy-start.8 = (bf16[1024]{0:T(1024)(128)(2,1)S(1)}, bf16[1024]{0:T(1024)(128)(2,1)}, u32[]{:S(2)}) copy-start(bf16[1024]{0:T(1024)(128)(2,1)} %param.22) | copy-start | bytes 6148
  293.5 1.6 copy-start.1

commit v4 on v3

--- a/solution.py
+++ b/solution.py
@@ -15,11 +15,13 @@
 STEPS = 2 * NP
 W = 512
 ROWS = 2 * FP
+QW = 256
 BF, F32 = jnp.bfloat16, jnp.float32
 LOG2 = 0.125 * math.log2(math.e)
 MESH = pl.DeviceIdType.MESH
 VMEM = pltpu.VMEM
 B2, B4, B8, LANES = 2, 4, 8, 128
+RC = 256
 TOK = NB * T
 SDS = jax.ShapeDtypeStruct
 
@@ -46,40 +48,7 @@
     return centered * inv_std, inv_std
 
 
-def prep_kernel(m_ref, h_ref, dy_ref, gain, shift, wq, bq, wo, mp_ref, q_ref, do_ref, s_ref):
-    step = pl.program_id(0)
-
-    @pl.when(step < TOK // LANES)
-    def _():
-        x_hat, _ = norm_parts(h_ref[...].astype(F32))
-        x = (x_hat * gain[...] + shift[...]).astype(BF)
-        q_ref[...] = (jnp.dot(x, wq[...], preferred_element_type=F32) + bq[...]).astype(BF)
-        do_ref[...] = dotg(dy_ref[...], wo[...], 1, 1).astype(BF)
-
-    x = m_ref[...].astype(F32).reshape(B8 * FC, D)
-    for t in range(D // LANES):
-        s_ref[t] = x[:, lanes(t)]
-    real = lax.broadcasted_iota(jnp.int32, (FC, LANES), 0) + FC * (step % NFC) < F
-    for b in range(B8):
-        for t in range(D // LANES):
-            y = jnp.where(real, s_ref[t, pl.ds(b, FC, stride=B8), :], 0.0)
-            mp_ref[b, :, lanes(t)] = y.astype(BF)
-
-
-def prepare(mt, h, dy, gain, shift, w_q, b_q, w_o):
-    tok = pl.BlockSpec((LANES, D), lambda s: (jnp.minimum(s, TOK // LANES - 1), 0))
-    vec, mat = fixed(1), fixed(D)
-    return pl.pallas_call(
-        prep_kernel, grid=(NB // B8 * NFC,), name="prepare",
-        out_shape=(SDS((NB, FP, D), BF), SDS((TOK, D), BF), SDS((TOK, D), BF)),
-        in_specs=[pl.BlockSpec((FC, B8, D), lambda s: (s % NFC, s // NFC, 0)), tok, tok, vec, vec, mat, vec, mat],
-        out_specs=(pl.BlockSpec((B8, FC, D), lambda s: (s // NFC, s % NFC, 0)), tok, tok),
-        scratch_shapes=[VMEM((D // LANES, B8 * FC, LANES), F32)],
-        compiler_params=pltpu.CompilerParams(vmem_limit_bytes=40 << 20),
-    )(mt, h, dy, gain, shift, w_q, b_q, w_o)
-
-
-JOB0, JOBS, RC = 3, 4, 256
+JOB0, JOBS = 3, 4
 
 
 def finish_kernel(dm_ref, res_hbm, h_hbm, dy_hbm, wo_hbm, wq_hbm, dw_hbm, gain, shift, bo,
@@ -219,9 +188,10 @@
 NCH = D // 2 // CH
 
 
-def attn_kernel(m_hbm, q, do, wk, wv, bv, res_hbm, dw_hbm, bias_hbm, dm_hbm, dkv_hbm,
-                mbuf, kv, e_s, dp_s, mt, stats, coef, dkv, acc, bias, od, r1, keep, x2, r2, res, big1, big2,
-                m_sem, dkv_sem, dm_sem, out_sem, st_send, st_recv, s1_send, s1_recv, s2_send, s2_recv,
+def attn_kernel(m_hbm, h_hbm, dy_hbm, wq_hbm, wo_hbm, wk_hbm, wv_hbm, gain, shift, bq, bv,
+                res_hbm, dw_hbm, bias_hbm, dm_hbm, dkv_hbm,
+                raw, fine, frames, q, do, wk, wv, kv, e_s, dp_s, mt, stats, coef, dkv, acc, bias, od, r1, keep, x2, r2, res, big1, big2,
+                raw_sem, in_sem, dkv_sem, dm_sem, out_sem, st_send, st_recv, s1_send, s1_recv, s2_send, s2_recv,
                 s3_send, s3_recv, s3s_send, s4_send, res_recv, e1_send, e1_recv, e2_send, e2_recv,
                 e3_send, e3_recv, e3s_send, e4_send, acc_recv, b_send, b_recv, free_sib, free_xn):
     me = lax.axis_index("cp")
@@ -232,14 +202,33 @@
         return pltpu.make_async_remote_copy(src_ref=src, dst_ref=dst, send_sem=ss, recv_sem=rs,
                                             device_id={"cp": dev}, device_id_type=MESH)
 
-    def m_copy(i):
-        return pltpu.make_async_copy(m_hbm.at[pl.ds(2 * (i % NP), 2)], mbuf.at[i % 2], m_sem.at[i % 2])
+    def raw_copy(c):
+        seqs = pl.ds(pl.multiple_of(B8 * (c // B4 % B4), B8), B8)
+        return pltpu.make_async_copy(m_hbm.at[:, seqs, quarter(c)], raw.at[c % 2], raw_sem.at[c % 2])
+
+    def quarter(c):
+        return pl.ds(pl.multiple_of(c % B4 * QW, QW), QW)
+
+    def sort_frames(c):
+        x = raw[c % 2].astype(F32)
+        for f in range(F):
+            for t in range(QW // LANES):
+                fine[t, 9 * f:9 * f + B8] = x[f, :, lanes(t)]
+        for b in range(B8):
+            y = jnp.concatenate([fine[t, pl.ds(b, FP, stride=9), :] for t in range(QW // LANES)], axis=1)
+            frames[c // B4 % 2, FP * b:FP * (b + 1), quarter(c)] = y.astype(BF)
 
     def dkv_copy(i):
         return pltpu.make_async_copy(dkv.at[i % 2], dkv_hbm.at[i // NP, i % NP], dkv_sem.at[i % 2])
 
-    def stat_copy(i, src, k):
-        return remote(stats.at[i % 4, src], stats.at[i % 4, src], st_send.at[i % 4, k - 1], st_recv.at[i % 4, src], (me + k) % 4)
+    def stat_send(i):
+        for k in range(1, B4):
+            remote(stats.at[i % B4, me], stats.at[i % B4, me], st_send.at[i % B4], st_recv.at[i % B4], (me + k) % B4).start()
+
+    def stat_wait(i):
+        three = stats.at[i % B4, 0:3]
+        for sem in (st_recv, st_send):
+            pltpu.make_async_copy(three, three, sem.at[i % B4]).wait()
 
     def s1(b):
         return remote(od.at[b % 2, 1 - cc], r1.at[b % 4], s1_send.at[b % 4], s1_recv.at[b % 4], sib)
@@ -396,27 +385,26 @@
 
     def stage_a(i):
         slot = i % 2
-        m = mbuf[slot].reshape(ROWS, D)
+        m = frames[i // B4 % 2, pl.ds(pl.multiple_of(i % B4 * ROWS, ROWS), ROWS), :]
         cols = pl.ds(pl.multiple_of(W * (i // NP), W), W)
+        mt[i % 3] = m.T
         kv[slot, :, 0:W] = jnp.dot(m, wk[:, cols], preferred_element_type=F32).astype(BF)
         kv[slot, :, W:] = (jnp.dot(m, wv[:, cols], preferred_element_type=F32) + bv[:, cols]).astype(BF)
-        mt[slot] = m.T
-        real = lax.broadcasted_iota(jnp.int32, (FP, 128), 0) < F
+        real = lax.broadcasted_iota(jnp.int32, (FP, LANES), 0) < F
         for j in range(2):
             rows = slice(FP * j, FP * (j + 1))
             for h in range(2):
                 n = 2 * j + h
                 qb, db, _ = operands(i, j, h)
-                s = dotg(kv[slot, rows, 256 * h:256 * (h + 1)], qb, 1, 1)
-                dp = dotg(kv[slot, rows, W + 256 * h:W + 256 * (h + 1)], db, 1, 1)
+                s = dotg(kv[slot, rows, QW * h:QW * (h + 1)], qb, 1, 1)
+                dp = dotg(kv[slot, rows, W + QW * h:W + QW * (h + 1)], db, 1, 1)
                 s = jnp.where(real, s, -1e30)
                 top = jnp.max(s, axis=0, keepdims=True)
                 e = jnp.exp2((s - top) * LOG2)
                 e_s[slot, n] = e
                 dp_s[slot, n] = dp
-                stats[i % 4, me, n:n + 1, :] = top
-                stats[i % 4, me, 4 + n:5 + n, :] = jnp.sum(e, axis=0, keepdims=True)
-                stats[i % 4, me, 8 + n:9 + n, :] = jnp.sum(e * dp, axis=0, keepdims=True)
+                for k, row in enumerate((top, jnp.sum(e, axis=0, keepdims=True), jnp.sum(e * dp, axis=0, keepdims=True))):
+                    stats[i % B4, me, B4 * k + n:B4 * k + n + 1, :] = row
 
     def combine(i):
         slot = i % 4
@@ -453,73 +441,105 @@
                 dkv[slot, rows, ck] = dk.astype(BF)
                 dkv[slot, rows, cv] = dv.astype(BF)
                 bias[me, pl.ds(grp, 1), cv] += jnp.sum(dv, axis=0, keepdims=True)
-        acc[grp] += jnp.dot(mt[slot], dkv[slot], preferred_element_type=F32)
-
-    def part_a(i):
-        m_copy(i).wait()
-
-        @pl.when(i + 1 < STEPS)
-        def _():
-            m_copy(i + 1).start()
-
-        stage_a(i)
-        for k in range(1, 4):
-            stat_copy(i, me, k).start()
-
-    def part_b(b):
-        exchange(0, b - NP, 9, 12)
-        for k in range(1, 4):
-            stat_copy(b, (me + k) % 4, k).wait_recv()
-
-        @pl.when(b >= 1)
-        def _():
-            for k in range(1, 4):
-                stat_copy(b - 1, me, k).wait_send()
-
-        @pl.when(b >= 2)
-        def _():
-            dkv_copy(b - 2).wait()
-
-        od_pre(b, True)
-        combine(b)
-        stage_b(b)
-        dkv_copy(b).start()
-        od_post(b, True)
-
-    m_copy(0).start()
-    for g in range(2):
-        acc[g] = jnp.zeros((D, D), F32)
-    bias[me] = jnp.zeros((8, D), F32)
+
+    def step(i, do_a, do_b):
+        b = i - 2
+        if do_b:
+            @pl.when(b >= NP)
+            def _():
+                exchange(0, b - NP, 9, 12)
+
+            stat_wait(b)
+
+            @pl.when(b >= 2)
+            def _():
+                dkv_copy(b - 2).wait()
+
+            od_pre(b, True)
+        if do_a:
+            @pl.when(i + B4 < STEPS)
+            def _():
+                raw_copy(i + B4).wait()
+
+            @pl.when(i + B4 + 1 < STEPS)
+            def _():
+                raw_copy(i + B4 + 1).start()
+
+        if do_b:
+            combine(b)
+            stage_b(b)
+        if do_a:
+            stage_a(i)
+            sort_frames(i + B4)
+        if do_b:
+            acc[b // NP] += jnp.dot(mt[b % 3], dkv[b % 2], preferred_element_type=F32)
+        if do_a:
+            stat_send(i)
+        if do_b:
+            dkv_copy(b).start()
+            od_post(b, True)
+
     barrier = pltpu.get_barrier_semaphore()
-    for k in range(1, 4):
-        pl.semaphore_signal(barrier, inc=1, device_id={"cp": (me + k) % 4}, device_id_type=MESH)
+    for k in range(1, B4):
+        pl.semaphore_signal(barrier, inc=1, device_id={"cp": (me + k) % B4}, device_id_type=MESH)
+    top, low = pl.ds(0, ROWS), pl.ds(ROWS, D - ROWS)
+    rest = pl.ds(0, D - ROWS)
+    loads = [pltpu.make_async_copy(x, y, in_sem.at[k]) for k, (x, y) in enumerate((
+        (h_hbm, res.at[0]), (wq_hbm.at[top], kv.at[0]), (wq_hbm.at[low], dkv.at[0, rest]), (dy_hbm, res.at[1]),
+        (wo_hbm.at[top], kv.at[1]), (wo_hbm.at[low], dkv.at[1, rest]), (wk_hbm, wk), (wv_hbm, wv)))]
+    raw_copy(0).start()
+    for cp in loads:
+        cp.start()
+    fine[...] = jnp.zeros(fine.shape, F32)
+    bias[me] = jnp.zeros((B8, D), F32)
+    for cp in loads[:-2]:
+        cp.wait()
+
+    def first(n, carry):
+        raw_copy(n).wait()
+        raw_copy(n + 1).start()
+        rows = pl.ds(pl.multiple_of(RC * n, RC), RC)
+        x_hat, _ = norm_parts(res[0, rows].astype(F32))
+        x = (x_hat * gain[...] + shift[...]).astype(BF)
+        q[rows] = (jnp.dot(x[:, :ROWS], kv[0], preferred_element_type=F32)
+                   + jnp.dot(x[:, ROWS:], dkv[0, rest], preferred_element_type=F32) + bq[...]).astype(BF)
+        do[rows, :ROWS] = dotg(res[1, rows], kv[1], 1, 1).astype(BF)
+        do[rows, ROWS:] = dotg(res[1, rows], dkv[1, rest], 1, 1).astype(BF)
+        sort_frames(n)
+        for g in range(2):
+            acc[g, rows] = jnp.zeros((RC, D), F32)
+        return carry
+
+    lax.fori_loop(0, TOK // RC, first, 0)
+    for cp in loads[-2:]:
+        cp.wait()
     pl.semaphore_wait(barrier, 3)
-    part_a(jnp.int32(0))
-
-    def step(i, carry):
-        part_a(i)
-        part_b(i - 1)
-        return carry
-
-    lax.fori_loop(1, STEPS, step, 0)
-    part_b(jnp.int32(STEPS - 1))
+
+    def run(lo, hi, do_a, do_b):
+        def body(i, carry):
+            step(i, do_a, do_b)
+            return carry
+        lax.fori_loop(lo, hi, body, 0)
+
+    run(0, 2, True, False)
+    run(2, STEPS, True, True)
+    run(STEPS, STEPS + 2, False, True)
 
     def b_copy(k, src):
         return remote(bias.at[src], bias.at[src], b_send.at[k - 1], b_recv.at[src], (me + k) % 4)
 
     for k in range(1, 4):
         b_copy(k, me).start()
-        stat_copy(STEPS - 1, me, k).wait_send()
     dkv_copy(STEPS - 2).wait()
     dkv_copy(STEPS - 1).wait()
 
     bufs = (kv, dkv)
 
     def c_load(c, s):
-        return [pltpu.make_async_copy(dkv_hbm.at[g, c], bufs[s].at[g], m_sem.at[g] if s == 0 else dkv_sem.at[g]) for g in range(2)]
+        return [pltpu.make_async_copy(dkv_hbm.at[g, c], bufs[s].at[g], raw_sem.at[g] if s == 0 else dkv_sem.at[g]) for g in range(2)]
 
     def dm_copy(c, s):
-        return pltpu.make_async_copy(mbuf.at[s], dm_hbm.at[pl.ds(2 * c, 2)], dm_sem.at[s])
+        return pltpu.make_async_copy(frames.at[0, pl.ds(ROWS * s, ROWS)], dm_hbm.at[c], dm_sem.at[s])
 
     for cp in c_load(0, 0):
         cp.start()
@@ -548,7 +568,7 @@
 
             x = jnp.concatenate([bufs[s][0], bufs[s][1]], axis=1)
             w = jnp.concatenate([wk[:, :W], wv[:, :W], wk[:, W:], wv[:, W:]], axis=1)
-            mbuf[s] = dotg(x, w, 1, 1).astype(BF).reshape(2, FP, D)
+            frames[0, pl.ds(ROWS * s, ROWS)] = dotg(x, w, 1, 1).astype(BF)
             dm_copy(c, s).start()
 
             @pl.when(c < 7)
@@ -579,29 +599,29 @@
     bias_out.wait()
 
 
-def attention(m_pad, q, do, w_k, w_v, b_v):
+def attention(mt, h, dy, w_q, w_o, w_k, w_v, gain, shift, b_q, b_v):
     vm = pl.BlockSpec(memory_space=VMEM)
     hbm = pl.BlockSpec(memory_space=pl.ANY)
     dma = pltpu.SemaphoreType.DMA
     d2, d4, d8, dn = dma((B2,)), dma((B4,)), dma((B8,)), dma((B2, NCH))
     credit = pltpu.SemaphoreType.REGULAR((B2,))
-    probs = VMEM((B2, B4, FP, LANES), F32)
+    probs, mat, rows32 = VMEM((B2, B4, FP, LANES), F32), VMEM((D, D), BF), VMEM((B4, T, W), F32)
     return pl.pallas_call(
         attn_kernel, name="attention",
-        out_shape=(SDS((B2, TOK, D), BF), SDS((B2, D, D), F32), SDS((2 * B8, W), F32), SDS((NB, FP, D), BF),
+        out_shape=(SDS((B2, TOK, D), BF), SDS((B2, D, D), F32), SDS((2 * B8, W), F32), SDS((NP, ROWS, D), BF),
                    SDS((B2, NP, ROWS, D), BF)),
-        in_specs=[hbm, vm, vm, vm, vm, vm],
+        in_specs=[hbm] * 7 + [vm] * B4,
         out_specs=(hbm,) * 5,
         scratch_shapes=[
-            VMEM((B2, B2, FP, D), BF), VMEM((B2, ROWS, D), BF), probs, probs, VMEM((B2, D, ROWS), BF),
-            VMEM((B4, B4, 2 * B8, LANES), F32), VMEM((B8, LANES), F32), VMEM((B2, ROWS, D), BF),
-            VMEM((B2, D, D), F32), VMEM((B4, B8, D), F32), VMEM((B2, B2, 2 * T, W), F32), VMEM((B4, 2 * T, W), F32),
-            VMEM((B4, T, W), F32), VMEM((B4, T, W), F32), VMEM((B8, T, W), F32), VMEM((B2, TOK, D), BF),
-            VMEM((D, W), F32), VMEM((B2, D // 2, W), F32),
-            d2, d2, d2, d4, dma((B4, B4)), dma((B4, B4)), d4, d4, d8, d8, d8, d8, d4, d4, dma, d2, d2, dn, dn, dn, dn, dn, dn, d2, d4, d4,
+            VMEM((B2, F, B8, QW), BF), VMEM((QW // LANES, 9 * FP, LANES), F32), VMEM((B2, B8 * FP, D), BF), mat, mat, mat, mat,
+            VMEM((B2, ROWS, D), BF), probs, probs, VMEM((3, D, ROWS), BF), VMEM((B4, B4, 2 * B8, LANES), F32),
+            VMEM((B8, LANES), F32), VMEM((B2, ROWS, D), BF), VMEM((B2, D, D), F32), VMEM((B4, B8, D), F32),
+            VMEM((B2, B2, 2 * T, W), F32), VMEM((B4, 2 * T, W), F32), rows32, rows32, VMEM((B8, T, W), F32),
+            VMEM((B2, TOK, D), BF), VMEM((D, W), F32), VMEM((B2, D // 2, W), F32),
+            d2, d8, d2, d2, d4, d4, d4, d4, d4, d8, d8, d8, d8, d4, d4, dma, d2, d2, dn, dn, dn, dn, dn, dn, d2, d4, d4,
             credit, credit],
-        compiler_params=pltpu.CompilerParams(vmem_limit_bytes=62 << 20, collective_id=0, has_side_effects=True),
-    )(m_pad, q, do, w_k, w_v, b_v)
+        compiler_params=pltpu.CompilerParams(vmem_limit_bytes=67043328, collective_id=0, has_side_effects=True),
+    )(mt, h, dy, w_q, w_o, w_k, w_v, gain, shift, b_q, b_v)
 
 
 def solution(mesh):
@@ -616,9 +636,8 @@
         h = hidden.reshape(TOK, D)
         dy = grad_y.reshape(TOK, D)
         gain, shift, bq, bv, bo = (a.astype(F32).reshape(1, D) for a in (ln_gain, ln_bias, b_q, b_v, b_o))
-        m_pad, q, do = prepare(memory.transpose(1, 0, 2), h, dy, gain, shift, w_q, bq, w_o)
-        res, dw, bias, dm, _ = attention(m_pad, q, do, w_k, w_v, bv)
-        gm, y, gh, gwo, gwq, gwk, gwv, vec = finish(dm, res, h, dy, w_o, w_q, dw, gain, shift, bo)
+        res, dw, bias, dm, _ = attention(memory.transpose(1, 0, 2), h, dy, w_q, w_o, w_k, w_v, gain, shift, bq, bv)
+        gm, y, gh, gwo, gwq, gwk, gwv, vec = finish(dm.reshape(NB, FP, D), res, h, dy, w_o, w_q, dw, gain, shift, bo)
         grad_bq = bias[0:2].reshape(D)
         grad_bv = bias[8:10].reshape(D)
         return (y.reshape(NB, T, D), gh.reshape(NB, T, D), gm.transpose(1, 0, 2), vec[0], vec[1], gwq, grad_bq,

time: 343 us -> 347 us (1.012)
  Pallas kernels: 325 us -> 334 us
  local copies, waits for them, and re-layouts: 13.1 us -> 5.5 us
    pallas_call x1, Pallas kernels: 244 us -> 290 us  [attention(): pl.pallas_call(attn_kernel, name='attention', out_shape=(SDS((B2, TOK, D)...]
    pallas_call x1 -> x0, Pallas kernels: 37.3 us -> none  [prepare(): pl.pallas_call(prep_kernel, grid=(NB // B8 * NFC,), name='prepare', out_s...]
    unnamed x21 -> x9, local copies, waits for them, and re-layouts: 12.5 us -> 4.89 us
where the time goes in v4:
time: 347 us; the launch traced here: 346 us
  Pallas kernels  334 us (96%)
  other arithmetic  5.79 us (2%)
  local copies, waits for them, and re-layouts  5.5 us (2%)
    pallas_call x1, Pallas kernels, attention(): pl.pallas_call(attn_kernel, name='attention', out_shape=(SDS((B2, TOK, D)...  290 us
    pallas_call x1, Pallas kernels, finish(): pl.pallas_call(finish_kernel, grid=(NB // B8 * NFC,), name='finish', out_...  43.8 us

profile of v4, /device:TPU:0, one launch (start us, length us, event | category | flops | bytes accessed | tf_op | source)
XLA Modules:
  0.0 345.7 jit_solution(11191938965534155057)
XLA Ops:
  0.6 1.3 reshape.87
  1.9 1.3 reshape.89
  3.2 1.3 reshape.91
  4.5 1.3 reshape.93
  5.7 290.0 %attention.1 = (bf16[2,1024,1024]{2,1,0:T(8,128)(2,1)}, f32[2,1024,1024]{2,1,0:T(8,128)}, f32[16,512]{1,0:T(8,128)}, bf16[16,768,1024]{2,1,0:T(8,128)(2,1)}, bf16[2,16,768,1024]{3,2,1,0:T(8,128)(2,1)}) custom-call(bf16[375,32,1024]{2,1,0:T(8,128)(2,1)} %bitcast.29, bf16[1024,1024]{1,0:T(8,128)(2,1)} %bitcast.21, bf16[1024,1024]{1,0:T(8,128)(2,1)} %bitcast.30, ...), custom_call_target="tpu_custom_call" | custom-call | tf_op jit(solution)/shard_map/attention/pallas_call | solution.py:609
  295.7 0.7 reshape.95
  296.4 0.0 copy-start
  296.4 1.6 copy-done
  298.0 0.0 copy-start.1
  298.0 0.7 copy-done.1
  298.7 0.0 copy-start.2
  298.7 0.7 copy-done.2
  299.4 43.8 %finish.1 = (bf16[375,32,1024]{2,1,0:T(8,128)(2,1)}, bf16[1024,1024]{1,0:T(8,128)(2,1)}, bf16[1024,1024]{1,0:T(8,128)(2,1)}, f32[1024,1024]{1,0:T(8,128)}, f32[1...) custom-call(bf16[32,384,1024]{2,1,0:T(8,128)(2,1)} %bitcast.28, ...), custom_call_target="tpu_custom_call" | custom-call | tf_op jit(solution)/shard_map/finish/pallas_call | solution.py:160
  343.2 0.6 fusion
  343.8 0.7 slice_bitcast_fusion
  344.6 0.6 copy.24
  345.2 0.6 copy.25
Async XLA Ops:
  296.4 1.6 copy-start
  298.0 0.7 copy-start.1
  298.7 0.7 copy-start.2

commit v5 on v4

--- a/solution.py
+++ b/solution.py
@@ -30,7 +30,7 @@
     return lax.dot_general(a, b, (((ca,), (cb,)), ((), ())), preferred_element_type=F32)
 
 
-FC = 64
+FC = 32
 NFC = FP // FC
 
 
@@ -40,6 +40,12 @@
 
 def lanes(t):
     return slice(LANES * t, LANES * (t + 1))
+
+
+def permutation(axis):
+    r = lax.broadcasted_iota(jnp.int32, (QW, QW), axis)
+    k = lax.broadcasted_iota(jnp.int32, (QW, QW), 1 - axis)
+    return (k == r % FC * B8 + r // FC).astype(F32).astype(BF)
 
 
 def norm_parts(h):
@@ -49,11 +55,13 @@
 
 
 JOB0, JOBS = 3, 4
+FB = 64
+NFB = FP // FB
 
 
 def finish_kernel(dm_ref, res_hbm, h_hbm, dy_hbm, wo_hbm, wq_hbm, dw_hbm, gain, shift, bo,
                   gm_ref, y_hbm, gh_hbm, gwo_hbm, gwq_hbm, gwk_hbm, gwv_hbm, vec_ref,
-                  s_ref, res, h, dy, wo, wq, x, y, gh, gw, stage, in_sem, y_sem, gh_sem, gw_sem, ld_sem, st_sem):
+                  perm, res, h, dy, wo, wq, x, y, gh, gw, stage, in_sem, y_sem, gh_sem, gw_sem, ld_sem, st_sem):
     step = pl.program_id(0)
     loads = [pltpu.make_async_copy(a, b, in_sem.at[k]) for k, (a, b) in enumerate(
         ((h_hbm, h), (res_hbm, res), (wo_hbm, wo), (dy_hbm, dy), (wq_hbm, wq)))]
@@ -82,6 +90,7 @@
         piece_in(0).start()
         piece_in(1).start()
         vec_ref[...] = jnp.zeros_like(vec_ref)
+        perm[...] = permutation(1)
 
     for k in range(4):
         @pl.when(step == 4 + 5 * (k // 2) + k % 2)
@@ -135,12 +144,10 @@
         gw[n] = dotg(x[:, rows(n)], res[1], 0, 0)
         gw_copy(gwq_hbm, n).start()
 
-    for b in range(B8):
-        z = dm_ref[b].astype(F32)
-        for t in range(D // LANES):
-            s_ref[t, pl.ds(b, FC, stride=B8), :] = z[:, lanes(t)]
-    z = jnp.concatenate([s_ref[t] for t in range(D // LANES)], axis=1)
-    gm_ref[...] = z.reshape(FC, B8, D).astype(BF)
+    for k in range(FB // FC):
+        z = dm_ref[:, FC * k:FC * (k + 1), :].reshape(QW, D)
+        z = jnp.dot(perm[...], z, preferred_element_type=F32)
+        gm_ref[FC * k:FC * (k + 1)] = z.astype(BF).reshape(FC, B8, D)
 
     @pl.when(step == pl.num_programs(0) - 1)
     def _():
@@ -158,13 +165,13 @@
     dma = pltpu.SemaphoreType.DMA
     mat, dj = VMEM((D, D), BF), dma((JOBS,))
     return pl.pallas_call(
-        finish_kernel, grid=(NB // B8 * NFC,), name="finish",
+        finish_kernel, grid=(NB // B8 * NFB,), name="finish",
         out_shape=(SDS((F, NB, D), BF), SDS((TOK, D), BF), SDS((TOK, D), BF), SDS((D, D), F32), SDS((D, D), F32),
                    SDS((D, D), F32), SDS((D, D), F32), SDS((B8, D), F32)),
-        in_specs=[pl.BlockSpec((B8, FC, D), lambda s: (s // NFC, s % NFC, 0))] + [hbm] * 6 + [vec] * 3,
-        out_specs=(pl.BlockSpec((FC, B8, D), lambda s: (s % NFC, s // NFC, 0)),) + (hbm,) * 6 + (pl.BlockSpec((B8, D), lambda s: (0, 0)),),
+        in_specs=[pl.BlockSpec((B8, FB, D), lambda s: (s // NFB, s % NFB, 0))] + [hbm] * 6 + [vec] * 3,
+        out_specs=(pl.BlockSpec((FB, B8, D), lambda s: (s % NFB, s // NFB, 0)),) + (hbm,) * 6 + (pl.BlockSpec((B8, D), lambda s: (0, 0)),),
         scratch_shapes=[
-            VMEM((D // LANES, B8 * FC, LANES), F32), VMEM((B2, TOK, D), BF), mat, mat, mat, mat, mat, mat, mat, VMEM((JOBS, RC, D), F32),
+            VMEM((QW, QW), BF), VMEM((B2, TOK, D), BF), mat, mat, mat, mat, mat, mat, mat, VMEM((JOBS, RC, D), F32),
             VMEM((B2, D, W), F32), dma((B8,)), dj, dj, dj, dma((B2,)), dma((B2,))],
         compiler_params=pltpu.CompilerParams(vmem_limit_bytes=50 << 20),
     )(dm, res, h, dy, w_o, w_q, dw, gain, shift, b_o)
@@ -190,7 +197,7 @@
 
 def attn_kernel(m_hbm, h_hbm, dy_hbm, wq_hbm, wo_hbm, wk_hbm, wv_hbm, gain, shift, bq, bv,
                 res_hbm, dw_hbm, bias_hbm, dm_hbm, dkv_hbm,
-                raw, fine, frames, q, do, wk, wv, kv, e_s, dp_s, mt, stats, coef, dkv, acc, bias, od, r1, keep, x2, r2, res, big1, big2,
+                raw, perm, frames, q, do, wk, wv, kv, e_s, dp_s, mt, stats, coef, dkv, acc, bias, od, r1, keep, x2, r2, res, big1, big2,
                 raw_sem, in_sem, dkv_sem, dm_sem, out_sem, st_send, st_recv, s1_send, s1_recv, s2_send, s2_recv,
                 s3_send, s3_recv, s3s_send, s4_send, res_recv, e1_send, e1_recv, e2_send, e2_recv,
                 e3_send, e3_recv, e3s_send, e4_send, acc_recv, b_send, b_recv, free_sib, free_xn):
@@ -204,19 +211,17 @@
 
     def raw_copy(c):
         seqs = pl.ds(pl.multiple_of(B8 * (c // B4 % B4), B8), B8)
-        return pltpu.make_async_copy(m_hbm.at[:, seqs, quarter(c)], raw.at[c % 2], raw_sem.at[c % 2])
+        return pltpu.make_async_copy(m_hbm.at[:, seqs, quarter(c)], raw.at[c % 2, 0:F], raw_sem.at[c % 2])
 
     def quarter(c):
         return pl.ds(pl.multiple_of(c % B4 * QW, QW), QW)
 
     def sort_frames(c):
-        x = raw[c % 2].astype(F32)
-        for f in range(F):
-            for t in range(QW // LANES):
-                fine[t, 9 * f:9 * f + B8] = x[f, :, lanes(t)]
-        for b in range(B8):
-            y = jnp.concatenate([fine[t, pl.ds(b, FP, stride=9), :] for t in range(QW // LANES)], axis=1)
-            frames[c // B4 % 2, FP * b:FP * (b + 1), quarter(c)] = y.astype(BF)
+        for n in range(NFC):
+            x = raw[c % 2, FC * n:FC * (n + 1)].reshape(QW, QW)
+            y = jnp.dot(perm[...], x, preferred_element_type=F32).astype(BF)
+            for b in range(B8):
+                frames[c // B4 % 2, FP * b + FC * n:FP * b + FC * (n + 1), quarter(c)] = y[FC * b:FC * (b + 1)]
 
     def dkv_copy(i):
         return pltpu.make_async_copy(dkv.at[i % 2], dkv_hbm.at[i // NP, i % NP], dkv_sem.at[i % 2])
@@ -490,7 +495,8 @@
     raw_copy(0).start()
     for cp in loads:
         cp.start()
-    fine[...] = jnp.zeros(fine.shape, F32)
+    raw[:, F:] = jnp.zeros((B2, FP - F, B8, QW), BF)
+    perm[...] = permutation(0)
     bias[me] = jnp.zeros((B8, D), F32)
     for cp in loads[:-2]:
         cp.wait()
@@ -613,7 +619,7 @@
         in_specs=[hbm] * 7 + [vm] * B4,
         out_specs=(hbm,) * 5,
         scratch_shapes=[
-            VMEM((B2, F, B8, QW), BF), VMEM((QW // LANES, 9 * FP, LANES), F32), VMEM((B2, B8 * FP, D), BF), mat, mat, mat, mat,
+            VMEM((B2, FP, B8, QW), BF), VMEM((QW, QW), BF), VMEM((B2, B8 * FP, D), BF), mat, mat, mat, mat,
             VMEM((B2, ROWS, D), BF), probs, probs, VMEM((3, D, ROWS), BF), VMEM((B4, B4, 2 * B8, LANES), F32),
             VMEM((B8, LANES), F32), VMEM((B2, ROWS, D), BF), VMEM((B2, D, D), F32), VMEM((B4, B8, D), F32),
             VMEM((B2, B2, 2 * T, W), F32), VMEM((B4, 2 * T, W), F32), rows32, rows32, VMEM((B8, T, W), F32),

time: 347 us -> 342 us (0.986)
  Pallas kernels: 334 us -> 329 us
where the time goes in v5:
time: 342 us; the launch traced here: 341 us
  Pallas kernels  329 us (96%)
  other arithmetic  5.79 us (2%)
  local copies, waits for them, and re-layouts  5.5 us (2%)
    pallas_call x1, Pallas kernels, attention(): pl.pallas_call(attn_kernel, name='attention', out_shape=(SDS((B2, TOK, D)...  288 us
    pallas_call x1, Pallas kernels, finish(): pl.pallas_call(finish_kernel, grid=(NB // B8 * NFB,), name='finish', out_...  41.5 us

profile of v5, /device:TPU:0, one launch (start us, length us, event | category | flops | bytes accessed | tf_op | source)
XLA Modules:
  0.0 341.3 jit_solution(10171759947734053197)
XLA Ops:
  0.6 1.3 reshape.87
  1.9 1.3 reshape.89
  3.2 1.3 reshape.91
  4.5 1.3 reshape.93
  5.7 287.9 %attention.1 = (bf16[2,1024,1024]{2,1,0:T(8,128)(2,1)}, f32[2,1024,1024]{2,1,0:T(8,128)}, f32[16,512]{1,0:T(8,128)}, bf16[16,768,1024]{2,1,0:T(8,128)(2,1)}, bf16[2,16,768,1024]{3,2,1,0:T(8,128)(2,1)}) custom-call(bf16[375,32,1024]{2,1,0:T(8,128)(2,1)} %bitcast.29, bf16[1024,1024]{1,0:T(8,128)(2,1)} %bitcast.21, bf16[1024,1024]{1,0:T(8,128)(2,1)} %bitcast.30, ...), custom_call_target="tpu_custom_call" | custom-call | tf_op jit(solution)/shard_map/attention/pallas_call | solution.py:615
  293.6 0.7 reshape.95
  294.3 0.0 copy-start
  294.3 1.6 copy-done
  295.9 0.0 copy-start.1
  295.9 0.7 copy-done.1
  296.6 0.0 copy-start.2
  296.6 0.7 copy-done.2
  297.3 41.5 %finish.1 = (bf16[375,32,1024]{2,1,0:T(8,128)(2,1)}, bf16[1024,1024]{1,0:T(8,128)(2,1)}, bf16[1024,1024]{1,0:T(8,128)(2,1)}, f32[1024,1024]{1,0:T(8,128)}, f32[1...) custom-call(bf16[32,384,1024]{2,1,0:T(8,128)(2,1)} %bitcast.28, ...), custom_call_target="tpu_custom_call" | custom-call | tf_op jit(solution)/shard_map/finish/pallas_call | solution.py:167
  338.7 0.6 fusion
  339.4 0.7 slice_bitcast_fusion
  340.1 0.6 copy.24
  340.7 0.6 copy.25
Async XLA Ops:
  294.3 1.6 copy-start
  295.9 0.7 copy-start.1
  296.6 0.7 copy-start.2

commit v6 on v5

--- a/solution.py
+++ b/solution.py
@@ -42,10 +42,10 @@
     return slice(LANES * t, LANES * (t + 1))
 
 
-def permutation(axis):
-    r = lax.broadcasted_iota(jnp.int32, (QW, QW), axis)
-    k = lax.broadcasted_iota(jnp.int32, (QW, QW), 1 - axis)
-    return (k == r % FC * B8 + r // FC).astype(F32).astype(BF)
+def permutation(n):
+    r = lax.broadcasted_iota(jnp.int32, (QW, QW), 0)
+    k = lax.broadcasted_iota(jnp.int32, (QW, QW), 1)
+    return (k == r % n * (QW // n) + r // n).astype(F32).astype(BF)
 
 
 def norm_parts(h):
@@ -55,8 +55,7 @@
 
 
 JOB0, JOBS = 3, 4
-FB = 64
-NFB = FP // FB
+FB = 16
 
 
 def finish_kernel(dm_ref, res_hbm, h_hbm, dy_hbm, wo_hbm, wq_hbm, dw_hbm, gain, shift, bo,
@@ -90,7 +89,7 @@
         piece_in(0).start()
         piece_in(1).start()
         vec_ref[...] = jnp.zeros_like(vec_ref)
-        perm[...] = permutation(1)
+        perm[...] = permutation(FB)
 
     for k in range(4):
         @pl.when(step == 4 + 5 * (k // 2) + k % 2)
@@ -144,10 +143,10 @@
         gw[n] = dotg(x[:, rows(n)], res[1], 0, 0)
         gw_copy(gwq_hbm, n).start()
 
-    for k in range(FB // FC):
-        z = dm_ref[:, FC * k:FC * (k + 1), :].reshape(QW, D)
+    for k in range(NB // FB):
+        z = dm_ref[FB * k:FB * (k + 1)].reshape(QW, D)
         z = jnp.dot(perm[...], z, preferred_element_type=F32)
-        gm_ref[FC * k:FC * (k + 1)] = z.astype(BF).reshape(FC, B8, D)
+        gm_ref[:, FB * k:FB * (k + 1), :] = z.astype(BF).reshape(FB, FB, D)
 
     @pl.when(step == pl.num_programs(0) - 1)
     def _():
@@ -165,11 +164,11 @@
     dma = pltpu.SemaphoreType.DMA
     mat, dj = VMEM((D, D), BF), dma((JOBS,))
     return pl.pallas_call(
-        finish_kernel, grid=(NB // B8 * NFB,), name="finish",
+        finish_kernel, grid=(FP // FB,), name="finish",
         out_shape=(SDS((F, NB, D), BF), SDS((TOK, D), BF), SDS((TOK, D), BF), SDS((D, D), F32), SDS((D, D), F32),
                    SDS((D, D), F32), SDS((D, D), F32), SDS((B8, D), F32)),
-        in_specs=[pl.BlockSpec((B8, FB, D), lambda s: (s // NFB, s % NFB, 0))] + [hbm] * 6 + [vec] * 3,
-        out_specs=(pl.BlockSpec((FB, B8, D), lambda s: (s % NFB, s // NFB, 0)),) + (hbm,) * 6 + (pl.BlockSpec((B8, D), lambda s: (0, 0)),),
+        in_specs=[pl.BlockSpec((NB, FB, D), lambda s: (0, s, 0))] + [hbm] * 6 + [vec] * 3,
+        out_specs=(pl.BlockSpec((FB, NB, D), lambda s: (s, 0, 0)),) + (hbm,) * 6 + (pl.BlockSpec((B8, D), lambda s: (0, 0)),),
         scratch_shapes=[
             VMEM((QW, QW), BF), VMEM((B2, TOK, D), BF), mat, mat, mat, mat, mat, mat, mat, VMEM((JOBS, RC, D), F32),
             VMEM((B2, D, W), F32), dma((B8,)), dj, dj, dj, dma((B2,)), dma((B2,))],
@@ -257,33 +256,30 @@
         def on(k):
             return (b >= k) if inside else (b - k < STEPS)
 
-        @when(on(7))
-        def _():
-            s4(b - 7).wait_send()
-
-        @when(on(5))
-        def _():
-            s3(b - 5, 1 - cx).wait_recv()
-            s4(b - 5).start()
-            s3(b - 5, cx).wait_send()
-            s3s(b - 5).wait_send()
-
-        @when(on(3))
-        def _():
-            s2(b - 3).wait_recv()
-            s2(b - 3).wait_send()
-            res_at(b - 3, cx)[...] = (keep[(b - 3) % 4] + r2[(b - 3) % 8]).astype(BF)
+        @when(on(8))
+        def _():
+            s4(b - 8).wait_send()
+
+        @when(on(6))
+        def _():
+            s3(b - 6, 1 - cx).wait_recv()
+            s4(b - 6).start()
+            s3(b - 6, cx).wait_send()
+            s3s(b - 6).wait_send()
+
+        @when(on(4))
+        def _():
+            s2(b - 4).wait_recv()
+            s2(b - 4).wait_send()
+            res_at(b - 4, cx)[...] = (keep[b % B4] + r2[(b - 4) % B8]).astype(BF)
 
         @when(on(2))
         def _():
             s1(b - 2).wait_send()
-
-        @when(on(1))
-        def _():
-            s1(b - 1).wait_recv()
+            s1(b - 2).wait_recv()
             for ref, x in ((keep, cx), (x2, 1 - cx)):
                 rows = pl.ds(pl.multiple_of(T * x, T), T)
-                ref[(b - 1) % 4] = od[(b - 1) % 2, cc, rows, :] + r1[(b - 1) % 4, rows, :]
+                ref[(b - 2) % B4] = od[b % 2, cc, rows, :] + r1[(b - 2) % B4, rows, :]
 
     def od_post(b, inside):
         def on(k):
@@ -292,14 +288,14 @@
         if inside:
             s1(b).start()
 
-        @when(on(1))
-        def _():
-            s2(b - 1).start()
-
-        @when(on(3))
-        def _():
-            s3(b - 3, cx).start()
-            s3s(b - 3).start()
+        @when(on(2))
+        def _():
+            s2(b - 2).start()
+
+        @when(on(4))
+        def _():
+            s3(b - 4, cx).start()
+            s3s(b - 4).start()
 
     own = pl.ds(pl.multiple_of(W * cc, W), W)
     other = pl.ds(pl.multiple_of(W * (1 - cc), W), W)
@@ -496,7 +492,7 @@
     for cp in loads:
         cp.start()
     raw[:, F:] = jnp.zeros((B2, FP - F, B8, QW), BF)
-    perm[...] = permutation(0)
+    perm[...] = permutation(FC)
     bias[me] = jnp.zeros((B8, D), F32)
     for cp in loads[:-2]:
         cp.wait()
@@ -568,7 +564,7 @@
             exchange(0, c + NP, 9, 12)
             exchange(1, c, 6, 10)
 
-            @pl.when(c < 7)
+            @pl.when(c < B8)
             def _():
                 od_pre(c + STEPS, False)
 
@@ -577,7 +573,7 @@
             frames[0, pl.ds(ROWS * s, ROWS)] = dotg(x, w, 1, 1).astype(BF)
             dm_copy(c, s).start()
 
-            @pl.when(c < 7)
+            @pl.when(c < B8)
             def _():
                 od_post(c + STEPS, False)
 

time: 342 us -> 316 us (0.924)
  Pallas kernels: 329 us -> 303 us
    pallas_call x1, Pallas kernels: 288 us -> 262 us  [attention(): pl.pallas_call(attn_kernel, name='attention', out_shape=(SDS((B2, TOK, D)...]
where the time goes in v6:
time: 316 us; the launch traced here: 315 us
  Pallas kernels  303 us (96%)
  other arithmetic  5.79 us (2%)
  local copies, waits for them, and re-layouts  5.5 us (2%)
    pallas_call x1, Pallas kernels, attention(): pl.pallas_call(attn_kernel, name='attention', out_shape=(SDS((B2, TOK, D)...  262 us
    pallas_call x1, Pallas kernels, finish(): pl.pallas_call(finish_kernel, grid=(FP // FB,), name='finish', out_shape=...  41 us

profile of v6, /device:TPU:0, one launch (start us, length us, event | category | flops | bytes accessed | tf_op | source)
XLA Modules:
  0.0 315.0 jit_solution(15000844788843660144)
XLA Ops:
  0.6 1.3 reshape.87
  1.9 1.3 reshape.89
  3.2 1.3 reshape.91
  4.5 1.3 reshape.93
  5.7 262.0 %attention.1 = (bf16[2,1024,1024]{2,1,0:T(8,128)(2,1)}, f32[2,1024,1024]{2,1,0:T(8,128)}, f32[16,512]{1,0:T(8,128)}, bf16[16,768,1024]{2,1,0:T(8,128)(2,1)}, bf16[2,16,768,1024]{3,2,1,0:T(8,128)(2,1)}) custom-call(bf16[375,32,1024]{2,1,0:T(8,128)(2,1)} %bitcast.29, bf16[1024,1024]{1,0:T(8,128)(2,1)} %bitcast.21, bf16[1024,1024]{1,0:T(8,128)(2,1)} %bitcast.30, ...), custom_call_target="tpu_custom_call" | custom-call | tf_op jit(solution)/shard_map/attention/pallas_call | solution.py:611
  267.8 0.7 reshape.95
  268.5 0.0 copy-start
  268.5 1.6 copy-done
  270.1 0.0 copy-start.1
  270.1 0.7 copy-done.1
  270.8 0.0 copy-start.2
  270.8 0.7 copy-done.2
  271.4 41.0 %finish.1 = (bf16[375,32,1024]{2,1,0:T(8,128)(2,1)}, bf16[1024,1024]{1,0:T(8,128)(2,1)}, bf16[1024,1024]{1,0:T(8,128)(2,1)}, f32[1024,1024]{1,0:T(8,128)}, f32[1...) custom-call(bf16[32,384,1024]{2,1,0:T(8,128)(2,1)} %bitcast.28, ...), custom_call_target="tpu_custom_call" | custom-call | tf_op jit(solution)/shard_map/finish/pallas_call | solution.py:166
  312.5 0.6 fusion
  313.1 0.7 slice_bitcast_fusion
  313.8 0.6 copy.24
  314.4 0.6 copy.25
Async XLA Ops:
  268.5 1.6 copy-start
  270.1 0.7 copy-start.1
  270.8 0.7 copy-start.2

commit v7 on v6

v7 whole, which is shorter than its diff:
```python
import functools
import math
import jax
import jax.numpy as jnp
from jax import lax
from jax.experimental import pallas as pl
from jax.experimental.pallas import tpu as pltpu
from jax.sharding import PartitionSpec as P

EPS = 1e-5
HEAD = 64
F, FP, D, T = 375, 384, 1024, 32
NB = 32
NP = NB // 2
STEPS = 2 * NP
W = 512
ROWS = 2 * FP
QW = 256
BF, F32 = jnp.bfloat16, jnp.float32
LOG2 = 0.125 * math.log2(math.e)
MESH = pl.DeviceIdType.MESH
VMEM = pltpu.VMEM
B2, B4, B8, LANES = 2, 4, 8, 128
RC = 256
TOK = NB * T
SDS = jax.ShapeDtypeStruct


def dotg(a, b, ca, cb):
    return lax.dot_general(a, b, (((ca,), (cb,)), ((), ())), preferred_element_type=F32)


FC = 32
NFC = FP // FC


def fixed(rows):
    return pl.BlockSpec((rows, D), lambda s: (0, 0), pipeline_mode=pl.Buffered(1))


def lanes(t):
    return slice(LANES * t, LANES * (t + 1))


def permutation(n):
    r = lax.broadcasted_iota(jnp.int32, (QW, QW), 0)
    k = lax.broadcasted_iota(jnp.int32, (QW, QW), 1)
    return (k == r % n * (QW // n) + r // n).astype(F32).astype(BF)


def norm_parts(h):
    centered = h - jnp.mean(h, axis=-1, keepdims=True)
    inv_std = lax.rsqrt(jnp.mean(centered * centered, axis=-1, keepdims=True) + EPS)
    return centered * inv_std, inv_std


JOB0, JOBS = 2, 4
FB = 16
NFB = FP // FB


def finish_kernel(dm_hbm, res_hbm, h_hbm, dy_hbm, wo_hbm, wq_hbm, dw_hbm, bias, gain, shift, bo,
                  gm_hbm, y_hbm, gh_hbm, gwo_hbm, gwq_hbm, gwk_hbm, gwv_hbm, dg, db, dbq, dbv, dbo,
                  src, dst, perm, res, h, dy, wo, wq, x, y, gh, gw, stage, sums,
                  src_sem, dst_sem, in_sem, y_sem, gh_sem, gw_sem, ld_sem, st_sem):
    loads = [pltpu.make_async_copy(a, b, in_sem.at[k]) for k, (a, b) in enumerate(
        ((h_hbm, h), (res_hbm, res), (wo_hbm, wo), (dy_hbm, dy), (wq_hbm, wq)))]

    def src_copy(s):
        return pltpu.make_async_copy(dm_hbm.at[:, pl.ds(pl.multiple_of(FB * s, FB), FB)], src.at[s % B4], src_sem.at[s % B4])

    def dst_copy(s):
        return pltpu.make_async_copy(dst.at[s % B4], gm_hbm.at[pl.ds(FB * s, FB)], dst_sem.at[s % B4])

    def last_copy():
        s = NFB - 1
        return pltpu.make_async_copy(dst.at[s % B4, 0:F - FB * s], gm_hbm.at[FB * s:F], dst_sem.at[s % B4])

    def rows(n):
        return pl.ds(pl.multiple_of(RC * n, RC), RC)

    def out_copy(a, b, sem, n):
        return pltpu.make_async_copy(a.at[rows(n)], b.at[rows(n)], sem.at[n])

    def gw_copy(b, n):
        return pltpu.make_async_copy(gw.at[n], b.at[rows(n)], gw_sem.at[n])

    def piece_in(k):
        g, v = k // 2, k % 2
        return pltpu.make_async_copy(dw_hbm.at[g, :, pl.ds(W * v, W)], stage.at[v], ld_sem.at[v])

    def piece_out(k):
        g, v = k // 2, k % 2
        return pltpu.make_async_copy(stage.at[v], (gwk_hbm, gwv_hbm)[v].at[:, pl.ds(W * g, W)], st_sem.at[v])

    def vec(ref):
        return ref[...].astype(F32).reshape(1, D)

    def move(s):
        for k in range(NB // FB):
            z = src[s % B4, FB * k:FB * (k + 1)].reshape(QW, D)
            z = jnp.dot(perm[...], z, preferred_element_type=F32)
            dst[s % B4, :, FB * k:FB * (k + 1), :] = z.astype(BF).reshape(FB, FB, D)

    def job_y(n):
        hf = h[rows(n)].astype(F32)
        x_hat, _ = norm_parts(hf)
        x[rows(n)] = (x_hat * vec(gain) + vec(shift)).astype(BF)
        y[rows(n)] = (hf + jnp.dot(res[0, rows(n)], wo[...], preferred_element_type=F32) + vec(bo)).astype(BF)

    def job_wo(n):
        gw[n] = dotg(res[0, :, rows(n)], dy[...], 0, 0)

    def job_h(n):
        x_hat, inv_std = norm_parts(h[rows(n)].astype(F32))
        dyf = dy[rows(n)].astype(F32)
        d_x = dotg(res[1, rows(n)], wq[...], 1, 1)
        for k, a in enumerate((d_x * x_hat, d_x, dyf)):
            sums[k:k + 1] += jnp.sum(a, axis=0, keepdims=True)
        d_hat = d_x * vec(gain)
        d_h = inv_std * (d_hat - jnp.mean(d_hat, axis=-1, keepdims=True) - x_hat * jnp.mean(d_hat * x_hat, axis=-1, keepdims=True))
        gh[rows(n)] = (dyf + d_h).astype(BF)

    def job_wq(n):
        gw[n] = dotg(x[:, rows(n)], res[1], 0, 0)

    for k in range(B4 - 1):
        src_copy(k).start()
    for cp in loads:
        cp.start()
    piece_in(0).start()
    piece_in(1).start()
    sums[...] = jnp.zeros_like(sums)
    perm[...] = permutation(FB)
    for ref, k in ((dbq, 0), (dbv, B8)):
        ref[...] = jnp.concatenate([bias[k:k + 1], bias[k + 1:k + 2]], axis=1).reshape(D)
    outs = ((job_y, lambda n: out_copy(y, y_hbm, y_sem, n)), (job_wo, lambda n: gw_copy(gwo_hbm, n)),
            (job_h, lambda n: out_copy(gh, gh_hbm, gh_sem, n)), (job_wq, lambda n: gw_copy(gwq_hbm, n)))
    needs = (loads[:3], loads[3:4], loads[4:], ())

    def step(s, carry):
        src_copy(s).wait()

        @pl.when(s + B4 - 1 < NFB)
        def _():
            src_copy(s + B4 - 1).start()

        @pl.when(s >= B4)
        def _():
            dst_copy(s - B4).wait()

        job = s - JOB0
        n = job % JOBS
        for kind, (f, copy) in enumerate(outs):
            @pl.when((job >= kind * JOBS) & (job < (kind + 1) * JOBS))
            def _():
                if needs[kind]:
                    @pl.when(n == 0)
                    def _():
                        for cp in needs[kind]:
                            cp.wait()
                if kind == 3:
                    gw_copy(gwo_hbm, n).wait()
                move(s)
                f(n)
                copy(n).start()

        @pl.when((job < 0) | (job >= JOBS * JOBS))
        def _():
            move(s)

        @pl.when(s < NFB - 1)
        def _():
            dst_copy(s).start()

        for v in range(2):
            @pl.when(s == JOBS + v)
            def _():
                piece_in(v).wait()
                piece_out(v).start()

            @pl.when(s == B8 + v)
            def _():
                piece_out(v).wait()
                piece_in(v + 2).start()

            @pl.when(s == B8 + JOBS + v)
            def _():
                piece_in(v + 2).wait()
                piece_out(v + 2).start()
        return carry

    lax.fori_loop(0, NFB, step, 0)
    last_copy().start()
    for k, ref in enumerate((dg, db, dbo)):
        ref[...] = sums[k:k + 1].reshape(D)
    for k in range(JOBS):
        out_copy(y, y_hbm, y_sem, k).wait()
        out_copy(gh, gh_hbm, gh_sem, k).wait()
        gw_copy(gwq_hbm, k).wait()
    piece_out(2).wait()
    piece_out(3).wait()
    for k in range(2, JOBS + 1):
        dst_copy(NFB - k).wait()
    last_copy().wait()


def finish(dm, res, h, dy, w_o, w_q, dw, bias, gain, shift, b_o):
    hbm, vm = pl.BlockSpec(memory_space=pl.ANY), pl.BlockSpec(memory_space=VMEM)
    dma = pltpu.SemaphoreType.DMA
    mat, dj, d2, vec = VMEM((D, D), BF), dma((JOBS,)), dma((B2,)), SDS((D,), F32)
    return pl.pallas_call(
        finish_kernel, name="finish",
        out_shape=(SDS((F, NB, D), BF), SDS((TOK, D), BF), SDS((TOK, D), BF)) + (SDS((D, D), F32),) * B4 + (vec,) * (B4 + 1),
        in_specs=[hbm] * (B8 - 1) + [vm] * B4,
        out_specs=(hbm,) * (B8 - 1) + (vm,) * (B4 + 1),
        scratch_shapes=[
            VMEM((B4, NB, FB, D), BF), VMEM((B4, FB, NB, D), BF), VMEM((QW, QW), BF), VMEM((B2, TOK, D), BF), mat, mat, mat, mat, mat,
            mat, mat, VMEM((JOBS, RC, D), F32), VMEM((B2, D, W), F32), VMEM((B8, D), F32), dj, dj, dma((B8,)), dj, dj, dj, d2, d2],
        compiler_params=pltpu.CompilerParams(vmem_limit_bytes=50 << 20),
    )(dm, res, h, dy, w_o, w_q, dw, bias, gain, shift, b_o)


def block_mask():
    return lax.broadcasted_iota(jnp.int32, (128, 256), 0) // T == lax.broadcasted_iota(jnp.int32, (128, 256), 1) // HEAD


def block_diag(x, mask):
    return jnp.where(mask, jnp.concatenate([x] * 4, axis=0), jnp.zeros((), BF))


def when(cond):
    if isinstance(cond, bool):
        return (lambda f: f()) if cond else (lambda f: None)
    return pl.when(cond)


CH = (64, 128)
NCH = tuple(D // 2 // rows for rows in CH)
T3, T4 = (8, 4), (11, 6)


def attn_kernel(m_hbm, h_hbm, dy_hbm, wq_hbm, wo_hbm, wk_hbm, wv_hbm, gain, shift, bq, bv,
                res_hbm, dw_hbm, bias_hbm, dm_hbm, dkv_hbm,
                raw, perm, bv32, frames, q, do, wk, wv, kv, e_s, dp_s, mt, stats, coef, dkv, acc, bias, od, r1, keep, x2, r2, res, big1, big2,
                raw_sem, in_sem, dkv_sem, dm_sem, out_sem, st_send, st_recv, s1_send, s1_recv, s2_send, s2_recv,
                s3_send, s3_recv, s3s_send, s4_send, res_recv, e1_send, e1_recv, e2_send, e2_recv,
                e3_send, e3_recv, e3s_send, e4_send, acc_recv, b_send, b_recv, free_sib, free_xn):
    me = lax.axis_index("cp")
    cx, cc = me // 2, me % 2
    sib, xn = 2 * cx + 1 - cc, 2 * (1 - cx) + cc

    def vec(ref):
        return ref[...].astype(F32).reshape(1, D)

    def remote(src, dst, ss, rs, dev):
        return pltpu.make_async_remote_copy(src_ref=src, dst_ref=dst, send_sem=ss, recv_sem=rs,
                                            device_id={"cp": dev}, device_id_type=MESH)

    def raw_copy(c):
        seqs = pl.ds(pl.multiple_of(B8 * (c // B4 % B4), B8), B8)
        return pltpu.make_async_copy(m_hbm.at[:, seqs, quarter(c)], raw.at[c % 2, 0:F], raw_sem.at[c % 2])

    def quarter(c):
        return pl.ds(pl.multiple_of(c % B4 * QW, QW), QW)

    def sort_frames(c):
        for n in range(NFC):
            x = raw[c % 2, FC * n:FC * (n + 1)].reshape(QW, QW)
            y = jnp.dot(perm[...], x, preferred_element_type=F32).astype(BF)
            for b in range(B8):
                frames[c // B4 % 2, FP * b + FC * n:FP * b + FC * (n + 1), quarter(c)] = y[FC * b:FC * (b + 1)]

    def dkv_copy(i):
        return pltpu.make_async_copy(dkv.at[i % 2], dkv_hbm.at[i // NP, i % NP], dkv_sem.at[i % 2])

    def stat_send(i):
        for k in range(1, B4):
            remote(stats.at[i % B4, me], stats.at[i % B4, me], st_send.at[i % B4], st_recv.at[i % B4], (me + k) % B4).start()

    def stat_wait(i):
        three = stats.at[i % B4, 0:3]
        for sem in (st_recv, st_send):
            pltpu.make_async_copy(three, three, sem.at[i % B4]).wait()

    def s1(b):
        return remote(od.at[b % 2, 1 - cc], r1.at[b % 4], s1_send.at[b % 4], s1_recv.at[b % 4], sib)

    def s2(b):
        return remote(x2.at[b % 4], r2.at[b % 8], s2_send.at[b % 8], s2_recv.at[b % 8], xn)

    def res_at(b, x):
        return res.at[cc, pl.ds(pl.multiple_of(64 * (b % NP) + T * x, T), T), pl.ds(pl.multiple_of(W * (b // NP), W), W)]

    def s3(b, x):
        return remote(res_at(b, x), res_at(b, x), s3_send, s3_recv.at[b % (2 * B8)], xn)

    def s3s(b):
        return remote(res_at(b, cx), res_at(b, cx), s3s_send, res_recv, sib)

    def s4(b):
        return remote(res_at(b, 1 - cx), res_at(b, 1 - cx), s4_send, res_recv, sib)

    def od_pre(b, inside):
        def on(k):
            return (b >= k) if inside else (b - k < STEPS)

        @when(on(8))
        def _():
            s3(b - 8, 1 - cx).wait_recv()
            s4(b - 8).start()

        @when(on(5))
        def _():
            s2(b - 5).wait_recv()
            s2(b - 5).wait_send()
            res_at(b - 5, cx)[...] = (keep[(b - 5) % B4] + r2[(b - 5) % B8]).astype(BF)

        @when(on(2))
        def _():
            s1(b - 2).wait_send()
            s1(b - 2).wait_recv()
            for ref, x in ((keep, cx), (x2, 1 - cx)):
                rows = pl.ds(pl.multiple_of(T * x, T), T)
                ref[(b - 2) % B4] = od[b % 2, cc, rows, :] + r1[(b - 2) % B4, rows, :]

    def od_post(b, inside):
        def on(k):
            return (b >= k) if inside else (b - k < STEPS)

        if inside:
            s1(b).start()

        @when(on(2))
        def _():
            s2(b - 2).start()

        @when(on(5))
        def _():
            s3(b - 5, cx).start()
            s3s(b - 5).start()

    own = pl.ds(pl.multiple_of(W * cc, W), W)
    other = pl.ds(pl.multiple_of(W * (1 - cc), W), W)

    def rows_of(g, x, n):
        return pl.ds(pl.multiple_of(x * (D // 2) + CH[g] * n, CH[g]), CH[g])

    def chunk_of(g, n):
        return big2.at[g, pl.ds(pl.multiple_of(CH[g] * n, CH[g]), CH[g])]

    def e1(g):
        return remote(acc.at[g, :, other], big1, e1_send.at[g], e1_recv.at[g], sib)

    def e2(g, n):
        return remote(acc.at[g, rows_of(g, 1 - cx, n), own], chunk_of(g, n), e2_send.at[g, n], e2_recv.at[g, n], xn)

    def e3(g, n, x):
        ref = acc.at[g, rows_of(g, x, n), own]
        return remote(ref, ref, e3_send.at[g, n], e3_recv.at[g, n], xn)

    def to_sib(g, n, x, sem):
        ref = acc.at[g, rows_of(g, x, n), own]
        return remote(ref, ref, sem.at[g, n], acc_recv.at[g], sib)

    def dw_copy(g):
        return pltpu.make_async_copy(acc.at[g], dw_hbm.at[g], out_sem.at[g])

    def reduce_core(g, n):
        for x in (cx, 1 - cx):
            acc[g, rows_of(g, x, n), own] += big1[rows_of(g, x, n), :]
        e2(g, n).start()

    def sent(g, n):
        e2(g, n).wait_send()
        pl.semaphore_signal(free_xn.at[g], inc=1, device_id={"cp": xn}, device_id_type=MESH)

    def reduce_chip(g, n):
        e2(g, n).wait_recv()
        pl.semaphore_wait(free_xn.at[g], 1)
        acc[g, rows_of(g, cx, n), own] += chunk_of(g, n)[...]
        e3(g, n, cx).start()
        to_sib(g, n, cx, e3s_send).start()

    def forward(g, n):
        e3(g, n, 1 - cx).wait_recv()
        to_sib(g, n, 1 - cx, e4_send).start()

    def gathered(g):
        half = acc.at[g, :, other]
        remote(half, half, e1_send.at[g], acc_recv.at[g], sib).wait_recv()
        for n in range(NCH[g]):
            e3(g, n, cx).wait_send()
            to_sib(g, n, cx, e3s_send).wait_send()
            to_sib(g, n, 1 - cx, e4_send).wait_send()
        dw_copy(g).start()

    def exchange(g, t, t3, t4):
        def chunk(t0, f):
            n = t - t0
            if isinstance(n, int):
                if 0 <= n < NCH[g]:
                    f(g, n)
            else:
                pl.when((n >= 0) & (n < NCH[g]))(lambda: f(g, n))

        @when(t == 0)
        def _():
            e1(g).start()

        @when(t == 1)
        def _():
            e1(g).wait_send()
            pl.semaphore_signal(free_sib.at[g], inc=1, device_id={"cp": sib}, device_id_type=MESH)
            e1(g).wait_recv()

        @when(t == t3)
        def _():
            pl.semaphore_wait(free_sib.at[g], 1)

        chunk(1, reduce_core)
        chunk(t3 - 1, sent)
        chunk(t3, reduce_chip)
        chunk(t4, forward)

    def operands(i, j, h):
        cols = pl.ds(pl.multiple_of(W * (i // NP) + 256 * h, 256), 256)
        rows = pl.ds(pl.multiple_of(64 * (i % NP) + T * j, T), T)
        mask = block_mask()
        return block_diag(q[rows, cols], mask), block_diag(do[rows, cols], mask), mask

    def stage_a(i):
        slot = i % 2
        m = frames[i // B4 % 2, pl.ds(pl.multiple_of(i % B4 * ROWS, ROWS), ROWS), :]
        cols = pl.ds(pl.multiple_of(W * (i // NP), W), W)
        mt[i % 3] = m.T
        kv[slot, :, 0:W] = jnp.dot(m, wk[:, cols], preferred_element_type=F32).astype(BF)
        kv[slot, :, W:] = (jnp.dot(m, wv[:, cols], preferred_element_type=F32) + bv32[:, cols]).astype(BF)
        real = lax.broadcasted_iota(jnp.int32, (FP, LANES), 0) < F
        for j in range(2):
            rows = slice(FP * j, FP * (j + 1))
            for h in range(2):
                n = 2 * j + h
                qb, db, _ = operands(i, j, h)
                s = dotg(kv[slot, rows, QW * h:QW * (h + 1)], qb, 1, 1)
                dp = dotg(kv[slot, rows, W + QW * h:W + QW * (h + 1)], db, 1, 1)
                s = jnp.where(real, s, -1e30)
                top = jnp.max(s, axis=0, keepdims=True)
                e = jnp.exp2((s - top) * LOG2)
                e_s[slot, n] = e
                dp_s[slot, n] = dp
                for k, row in enumerate((top, jnp.sum(e, axis=0, keepdims=True), jnp.sum(e * dp, axis=0, keepdims=True))):
                    stats[i % B4, me, B4 * k + n:B4 * k + n + 1, :] = row

    def combine(i):
        slot = i % 4
        tops = [stats[slot, d, 0:4, :] for d in range(4)]
        top = jnp.maximum(jnp.maximum(tops[0], tops[1]), jnp.maximum(tops[2], tops[3]))
        ws = [jnp.exp2((t - top) * LOG2) for t in tops]
        total = sum(stats[slot, d, 4:8, :] * ws[d] for d in range(4))
        dots = sum(stats[slot, d, 8:12, :] * ws[d] for d in range(4))
        coef[0:4, :] = jnp.exp2((stats[slot, me, 0:4, :] - top) * LOG2) / total
        coef[4:8, :] = dots / total

    def stage_b(i):
        slot = i % 2
        grp = i // NP
        for j in range(2):
            rows = slice(FP * j, FP * (j + 1))
            for h in range(2):
                n = 2 * j + h
                qb, db, mask = operands(i, j, h)
                ck, cv = slice(256 * h, 256 * (h + 1)), slice(W + 256 * h, W + 256 * (h + 1))
                p = e_s[slot, n] * coef[n:n + 1, :]
                pb = p.astype(BF)
                gb = (p * (dp_s[slot, n] - coef[4 + n:5 + n, :]) * 0.125).astype(BF)
                o = dotg(pb, kv[slot, rows, cv], 0, 0)
                dq = dotg(gb, kv[slot, rows, ck], 0, 0)
                for which, x in ((0, o), (1, dq)):
                    x = jnp.where(mask, x, 0.0)
                    x = (x[0:32] + x[32:64]) + (x[64:96] + x[96:128])
                    od[slot, which, T * j:T * (j + 1), ck] = x
                    if which == 1:
                        bias[me, pl.ds(grp, 1), ck] += jnp.sum(x, axis=0, keepdims=True)
                dk = jnp.dot(gb, qb, preferred_element_type=F32)
                dv = jnp.dot(pb, db, preferred_element_type=F32)
                dkv[slot, rows, ck] = dk.astype(BF)
                dkv[slot, rows, cv] = dv.astype(BF)
                bias[me, pl.ds(grp, 1), cv] += jnp.sum(dv, axis=0, keepdims=True)

    def step(i, do_a, do_b):
        b = i - 2
        if do_b:
            @pl.when(b >= NP)
            def _():
                exchange(0, b - NP, T3[0], T4[0])

            stat_wait(b)

            @pl.when(b >= 2)
            def _():
                dkv_copy(b - 2).wait()

            od_pre(b, True)
        if do_a:
            @pl.when(i + B4 < STEPS)
            def _():
                raw_copy(i + B4).wait()

            @pl.when(i + B4 + 1 < STEPS)
            def _():
                raw_copy(i + B4 + 1).start()

        if do_b:
            combine(b)
            stage_b(b)
        if do_a:
            stage_a(i)
            sort_frames(i + B4)
        if do_b:
            acc[b // NP] += jnp.dot(mt[b % 3], dkv[b % 2], preferred_element_type=F32)
        if do_a:
            stat_send(i)
        if do_b:
            dkv_copy(b).start()
            od_post(b, True)

    barrier = pltpu.get_barrier_semaphore()
    for k in range(1, B4):
        pl.semaphore_signal(barrier, inc=1, device_id={"cp": (me + k) % B4}, device_id_type=MESH)
    top, low = pl.ds(0, ROWS), pl.ds(ROWS, D - ROWS)
    rest = pl.ds(0, D - ROWS)
    loads = [pltpu.make_async_copy(x, y, in_sem.at[k]) for k, (x, y) in enumerate((
        (h_hbm, res.at[0]), (wq_hbm.at[top], kv.at[0]), (wq_hbm.at[low], dkv.at[0, rest]), (dy_hbm, res.at[1]),
        (wo_hbm.at[top], kv.at[1]), (wo_hbm.at[low], dkv.at[1, rest]), (wk_hbm, wk), (wv_hbm, wv)))]
    raw_copy(0).start()
    for cp in loads:
        cp.start()
    raw[:, F:] = jnp.zeros((B2, FP - F, B8, QW), BF)
    perm[...] = permutation(FC)
    bv32[...] = vec(bv)
    bias[me] = jnp.zeros((B8, D), F32)
    for cp in loads[:-2]:
        cp.wait()

    def first(n, carry):
        raw_copy(n).wait()
        raw_copy(n + 1).start()
        rows = pl.ds(pl.multiple_of(RC * n, RC), RC)
        x_hat, _ = norm_parts(res[0, rows].astype(F32))
        x = (x_hat * vec(gain) + vec(shift)).astype(BF)
        q[rows] = (jnp.dot(x[:, :ROWS], kv[0], preferred_element_type=F32)
                   + jnp.dot(x[:, ROWS:], dkv[0, rest], preferred_element_type=F32) + vec(bq)).astype(BF)
        do[rows, :ROWS] = dotg(res[1, rows], kv[1], 1, 1).astype(BF)
        do[rows, ROWS:] = dotg(res[1, rows], dkv[1, rest], 1, 1).astype(BF)
        sort_frames(n)
        for g in range(2):
            acc[g, rows] = jnp.zeros((RC, D), F32)
        return carry

    lax.fori_loop(0, TOK // RC, first, 0)
    for cp in loads[-2:]:
        cp.wait()
    pl.semaphore_wait(barrier, 3)

    def run(lo, hi, do_a, do_b):
        def body(i, carry):
            step(i, do_a, do_b)
            return carry
        lax.fori_loop(lo, hi, body, 0)

    run(0, 2, True, False)
    run(2, STEPS, True, True)
    run(STEPS, STEPS + 2, False, True)

    def b_copy(k, src):
        return remote(bias.at[src], bias.at[src], b_send.at[k - 1], b_recv.at[src], (me + k) % 4)

    for k in range(1, 4):
        b_copy(k, me).start()
    dkv_copy(STEPS - 2).wait()
    dkv_copy(STEPS - 1).wait()

    def part(u, k):
        return frames.at[u % 2, pl.ds(ROWS * k, ROWS)]

    def c_load(u, k):
        return pltpu.make_async_copy(dkv_hbm.at[k % 2, 2 * u + k // 2], part(u, k), in_sem.at[k])

    def dm_copy(u, k):
        return pltpu.make_async_copy((kv, dkv)[k].at[u % 2], dm_hbm.at[2 * u + k], dm_sem.at[k, u % 2])

    for k in range(B4):
        c_load(0, k).start()
    exchange(1, 0, T3[1], T4[1])

    def c_step(u, carry):
        for k in range(B4):
            c_load(u, k).wait()

        @pl.when(u + 1 < NP // 2)
        def _():
            for k in range(B4):
                c_load(u + 1, k).start()

        @pl.when(u >= 2)
        def _():
            for k in range(2):
                dm_copy(u - 2, k).wait()

        @pl.when(u < B4)
        def _():
            for k in range(2):
                od_pre(STEPS + 2 * u + k, False)
                od_post(STEPS + 2 * u + k, False)

        exchange(1, u + 1, T3[1], T4[1])

        @pl.when(u == 1)
        def _():
            for n in range(NP - T4[0], NCH[0]):
                forward(0, n)

        @pl.when(u == 3)
        def _():
            gathered(0)

        @pl.when(u == 6)
        def _():
            rows = res.at[0, 0:TOK // 2]
            for sem in (s3_send, s3s_send, s4_send):
                pltpu.make_async_copy(rows, rows, sem).wait()
            pltpu.make_async_copy(res.at[0], res.at[0], res_recv).wait()
            pltpu.make_async_copy(res, res_hbm, out_sem.at[2]).start()

        w = jnp.concatenate([wk[:, :W], wv[:, :W], wk[:, W:], wv[:, W:]], axis=1)
        for k in range(2):
            x = jnp.concatenate([part(u, 2 * k)[...], part(u, 2 * k + 1)[...]], axis=1)
            (kv, dkv)[k][u % 2] = dotg(x, w, 1, 1).astype(BF)
        for k in range(2):
            dm_copy(u, k).start()
        return carry

    lax.fori_loop(0, NP // 2, c_step, 0)
    for t in range(NP // 2 + 1, T4[1] + NCH[1]):
        exchange(1, t, T3[1], T4[1])
    gathered(1)
    for k in range(1, 4):
        b_copy(k, (me + k) % 4).wait_recv()
        b_copy(k, me).wait_send()
    big1[0:8, :] = (bias[0, :, 0:W] + bias[1, :, 0:W]) + (bias[2, :, 0:W] + bias[3, :, 0:W])
    big1[8:16, :] = (bias[0, :, W:] + bias[1, :, W:]) + (bias[2, :, W:] + bias[3, :, W:])
    bias_out = pltpu.make_async_copy(big1.at[0:16], bias_hbm, out_sem.at[3])
    bias_out.start()
    for u in (NP // 2 - 2, NP // 2 - 1):
        for k in range(2):
            dm_copy(u, k).wait()
    dw_copy(0).wait()
    dw_copy(1).wait()
    pltpu.make_async_copy(res, res_hbm, out_sem.at[2]).wait()
    bias_out.wait()


def attention(mt, h, dy, w_q, w_o, w_k, w_v, gain, shift, b_q, b_v):
    vm = pl.BlockSpec(memory_space=VMEM)
    hbm = pl.BlockSpec(memory_space=pl.ANY)
    dma = pltpu.SemaphoreType.DMA
    d2, d4, d8, dn = dma((B2,)), dma((B4,)), dma((B8,)), dma((B2, B8))
    credit = pltpu.SemaphoreType.REGULAR((B2,))
    probs, mat, rows32 = VMEM((B2, B4, FP, LANES), F32), VMEM((D, D), BF), VMEM((B4, T, W), F32)
    return pl.pallas_call(
        attn_kernel, name="attention",
        out_shape=(SDS((B2, TOK, D), BF), SDS((B2, D, D), F32), SDS((2 * B8, W), F32), SDS((NP, ROWS, D), BF),
                   SDS((B2, NP, ROWS, D), BF)),
        in_specs=[hbm] * 7 + [vm] * B4,
        out_specs=(hbm,) * 5,
        scratch_shapes=[
            VMEM((B2, FP, B8, QW), BF), VMEM((QW, QW), BF), VMEM((1, D), F32), VMEM((B2, B8 * FP, D), BF), mat, mat, mat, mat,
            VMEM((B2, ROWS, D), BF), probs, probs, VMEM((3, D, ROWS), BF), VMEM((B4, B4, 2 * B8, LANES), F32),
            VMEM((B8, LANES), F32), VMEM((B2, ROWS, D), BF), VMEM((B2, D, D), F32), VMEM((B4, B8, D), F32),
            VMEM((B2, B2, 2 * T, W), F32), VMEM((B4, 2 * T, W), F32), rows32, rows32, VMEM((B8, T, W), F32),
            VMEM((B2, TOK, D), BF), VMEM((D, W), F32), VMEM((B2, D // 2, W), F32),
            d2, d8, d2, dma((B2, B2)), d4, d4, d4, d4, d4, d8, d8, dma, dma((2 * B8,)), dma, dma, dma, d2, d2, dn, dn, dn, dn, dn, dn, d2, d4, d4,
            credit, credit],
        compiler_params=pltpu.CompilerParams(vmem_limit_bytes=67043328, collective_id=0, has_side_effects=True),
    )(mt, h, dy, w_q, w_o, w_k, w_v, gain, shift, b_q, b_v)


def solution(mesh):
    act_spec = P("dp", None, None)
    mem_spec = P("dp", "cp", None)
    vec_out = P("dp")
    mat_out = P("dp", None)
    in_specs = (act_spec, mem_spec, P(), P(), P(), P(), P(), P(), P(), P(), P(), act_spec)
    out_specs = (act_spec, act_spec, mem_spec, vec_out, vec_out, mat_out, vec_out, mat_out, mat_out, vec_out, mat_out, vec_out)

    def device_step(hidden, memory, ln_gain, ln_bias, w_q, b_q, w_k, w_v, b_v, w_o, b_o, grad_y):
        h = hidden.reshape(TOK, D)
        dy = grad_y.reshape(TOK, D)
        res, dw, bias, dm, _ = attention(memory.transpose(1, 0, 2), h, dy, w_q, w_o, w_k, w_v, ln_gain, ln_bias, b_q, b_v)
        gm, y, gh, gwo, gwq, gwk, gwv, dg, db, dbq, dbv, dbo = finish(
            dm.reshape(NB, FP, D), res, h, dy, w_o, w_q, dw, bias, ln_gain, ln_bias, b_o)
        return (y.reshape(NB, T, D), gh.reshape(NB, T, D), gm.transpose(1, 0, 2), dg, db, gwq, dbq, gwk, gwv, dbv, gwo, dbo)

    return jax.shard_map(device_step, mesh=mesh, in_specs=in_specs, out_specs=out_specs, check_vma=False)
```

time: 316 us -> 299 us (0.946)
  Pallas kernels: 303 us -> 293 us
  other arithmetic: 5.79 us -> 0 us
    pallas_call x1, Pallas kernels: 41 us -> 32.7 us  [finish(): pl.pallas_call(finish_kernel, name='finish', out_shape=(SDS((F, NB, D), B...]
    reshape x5 -> x0, other arithmetic: 5.79 us -> none  [device_step(): a.astype(F32).reshape(1, D)]
where the time goes in v7:
time: 299 us; the launch traced here: 298 us
  Pallas kernels  293 us (98%)
  local copies, waits for them, and re-layouts  4.39 us (1%)
    pallas_call x1, Pallas kernels, attention(): pl.pallas_call(attn_kernel, name='attention', out_shape=(SDS((B2, TOK, D)...  260 us
    pallas_call x1, Pallas kernels, finish(): pl.pallas_call(finish_kernel, name='finish', out_shape=(SDS((F, NB, D), B...  32.7 us

profile of v7, /device:TPU:0, one launch (start us, length us, event | category | flops | bytes accessed | tf_op | source)
XLA Modules:
  0.0 298.4 jit_solution(1453493962769538306)
XLA Ops:
  0.6 260.4 %attention.1 = (bf16[2,1024,1024]{2,1,0:T(8,128)(2,1)}, f32[2,1024,1024]{2,1,0:T(8,128)}, f32[16,512]{1,0:T(8,128)}, bf16[16,768,1024]{2,1,0:T(8,128)(2,1)}, bf16[2,16,768,1024]{3,2,1,0:T(8,128)(2,1)}) custom-call(bf16[375,32,1024]{2,1,0:T(8,128)(2,1)} %bitcast.10, bf16[1024,1024]{1,0:T(8,128)(2,1)} %bitcast.7, bf16[1024,1024]{1,0:T(8,128)(2,1)} %bitcast.11, ...), custom_call_target="tpu_custom_call" | custom-call | tf_op jit(solution)/shard_map/attention/pallas_call | solution.py:671
  261.1 0.0 copy-start
  261.1 1.6 copy-done
  262.7 0.0 copy-start.1
  262.7 0.8 copy-done.1
  263.4 0.0 copy-start.2
  263.4 0.7 copy-done.2
  264.1 0.0 copy-start.3
  264.1 0.7 copy-done.3
  264.8 0.0 copy-start.4
  264.8 0.7 copy-done.4
  265.5 32.7 %finish.1 = (bf16[375,32,1024]{2,1,0:T(8,128)(2,1)}, bf16[1024,1024]{1,0:T(8,128)(2,1)}, bf16[1024,1024]{1,0:T(8,128)(2,1)}, f32[1024,1024]{1,0:T(8,128)}, f32[1...) custom-call(bf16[32,384,1024]{2,1,0:T(8,128)(2,1)} %bitcast.9, ...), custom_call_target="tpu_custom_call" | custom-call | tf_op jit(solution)/shard_map/finish/pallas_call | solution.py:212
Async XLA Ops:
  261.1 1.6 copy-start
  262.7 0.8 copy-start.1
  263.4 0.7 copy-start.2
  264.1 0.7 copy-start.3
  264.8 0.7 copy-start.4

commit v8 on v7

--- a/solution.py
+++ b/solution.py
@@ -240,12 +240,15 @@
 T3, T4 = (8, 4), (11, 6)
 
 
+ALL, FILL, DRAIN = range(3)
+
+
 def attn_kernel(m_hbm, h_hbm, dy_hbm, wq_hbm, wo_hbm, wk_hbm, wv_hbm, gain, shift, bq, bv,
-                res_hbm, dw_hbm, bias_hbm, dm_hbm, dkv_hbm,
+                res_hbm, dw_hbm, bias_hbm, dm_hbm, dkv_hbm, mp_hbm,
                 raw, perm, bv32, frames, q, do, wk, wv, kv, e_s, dp_s, mt, stats, coef, dkv, acc, bias, od, r1, keep, x2, r2, res, big1, big2,
                 raw_sem, in_sem, dkv_sem, dm_sem, out_sem, st_send, st_recv, s1_send, s1_recv, s2_send, s2_recv,
                 s3_send, s3_recv, s3s_send, s4_send, res_recv, e1_send, e1_recv, e2_send, e2_recv,
-                e3_send, e3_recv, e3s_send, e4_send, acc_recv, b_send, b_recv, free_sib, free_xn):
+                e3_send, e3_recv, e3s_send, e4_send, acc_recv, b_send, b_recv, keep_sem, load_sem, free_sib, free_xn):
     me = lax.axis_index("cp")
     cx, cc = me // 2, me % 2
     sib, xn = 2 * cx + 1 - cc, 2 * (1 - cx) + cc
@@ -301,44 +304,48 @@
     def s4(b):
         return remote(res_at(b, 1 - cx), res_at(b, 1 - cx), s4_send, res_recv, sib)
 
-    def od_pre(b, inside):
-        def on(k):
-            return (b >= k) if inside else (b - k < STEPS)
-
-        @when(on(8))
+    def on(mode, b, k):
+        return True if mode == ALL else b >= k if mode == FILL else b - k < STEPS
+
+    def od_wait(b, mode):
+        @when(on(mode, b, 8))
         def _():
             s3(b - 8, 1 - cx).wait_recv()
-            s4(b - 8).start()
-
-        @when(on(5))
+
+        @when(on(mode, b, 5))
         def _():
             s2(b - 5).wait_recv()
             s2(b - 5).wait_send()
-            res_at(b - 5, cx)[...] = (keep[(b - 5) % B4] + r2[(b - 5) % B8]).astype(BF)
-
-        @when(on(2))
+
+        @when(on(mode, b, 2))
         def _():
             s1(b - 2).wait_send()
             s1(b - 2).wait_recv()
+
+    def od_sum(b, mode):
+        @when(on(mode, b, 5))
+        def _():
+            res_at(b - 5, cx)[...] = (keep[(b - 5) % B4] + r2[(b - 5) % B8]).astype(BF)
+
+        @when(on(mode, b, 2))
+        def _():
             for ref, x in ((keep, cx), (x2, 1 - cx)):
                 rows = pl.ds(pl.multiple_of(T * x, T), T)
                 ref[(b - 2) % B4] = od[b % 2, cc, rows, :] + r1[(b - 2) % B4, rows, :]
 
-    def od_post(b, inside):
-        def on(k):
-            return (b >= k) if inside else (b - k < STEPS)
-
-        if inside:
-            s1(b).start()
-
-        @when(on(2))
+    def od_send(b, mode):
+        @when(on(mode, b, 2))
         def _():
             s2(b - 2).start()
 
-        @when(on(5))
+        @when(on(mode, b, 5))
         def _():
             s3(b - 5, cx).start()
             s3s(b - 5).start()
+
+        @when(on(mode, b, 8))
+        def _():
+            s4(b - 8).start()
 
     own = pl.ds(pl.multiple_of(W * cc, W), W)
     other = pl.ds(pl.multiple_of(W * (1 - cc), W), W)
@@ -429,21 +436,26 @@
         mask = block_mask()
         return block_diag(q[rows, cols], mask), block_diag(do[rows, cols], mask), mask
 
-    def stage_a(i):
+    def rows_of_pair(i):
+        return frames[i // B4 % 2, pl.ds(pl.multiple_of(i % B4 * ROWS, ROWS), ROWS), :]
+
+    def project(i):
+        cols = pl.ds(pl.multiple_of(W * (i // NP), W), W)
+        m = rows_of_pair(i)
+        kv[i % 3, :, 0:W] = jnp.dot(m, wk[:, cols], preferred_element_type=F32).astype(BF)
+        kv[i % 3, :, W:] = (jnp.dot(m, wv[:, cols], preferred_element_type=F32) + bv32[:, cols]).astype(BF)
+        mt[i % 3] = m.T
+
+    def scores(i):
         slot = i % 2
-        m = frames[i // B4 % 2, pl.ds(pl.multiple_of(i % B4 * ROWS, ROWS), ROWS), :]
-        cols = pl.ds(pl.multiple_of(W * (i // NP), W), W)
-        mt[i % 3] = m.T
-        kv[slot, :, 0:W] = jnp.dot(m, wk[:, cols], preferred_element_type=F32).astype(BF)
-        kv[slot, :, W:] = (jnp.dot(m, wv[:, cols], preferred_element_type=F32) + bv32[:, cols]).astype(BF)
         real = lax.broadcasted_iota(jnp.int32, (FP, LANES), 0) < F
         for j in range(2):
             rows = slice(FP * j, FP * (j + 1))
             for h in range(2):
                 n = 2 * j + h
                 qb, db, _ = operands(i, j, h)
-                s = dotg(kv[slot, rows, QW * h:QW * (h + 1)], qb, 1, 1)
-                dp = dotg(kv[slot, rows, W + QW * h:W + QW * (h + 1)], db, 1, 1)
+                s = dotg(kv[i % 3, rows, QW * h:QW * (h + 1)], qb, 1, 1)
+                dp = dotg(kv[i % 3, rows, W + QW * h:W + QW * (h + 1)], db, 1, 1)
                 s = jnp.where(real, s, -1e30)
                 top = jnp.max(s, axis=0, keepdims=True)
                 e = jnp.exp2((s - top) * LOG2)
@@ -462,33 +474,73 @@
         coef[0:4, :] = jnp.exp2((stats[slot, me, 0:4, :] - top) * LOG2) / total
         coef[4:8, :] = dots / total
 
-    def stage_b(i):
-        slot = i % 2
-        grp = i // NP
+    def grads(i):
+        slot, grp = i % 2, i // NP
+        blocks = []
         for j in range(2):
             rows = slice(FP * j, FP * (j + 1))
             for h in range(2):
                 n = 2 * j + h
-                qb, db, mask = operands(i, j, h)
-                ck, cv = slice(256 * h, 256 * (h + 1)), slice(W + 256 * h, W + 256 * (h + 1))
+                qb, db, _ = operands(i, j, h)
+                ck, cv = slice(QW * h, QW * (h + 1)), slice(W + QW * h, W + QW * (h + 1))
                 p = e_s[slot, n] * coef[n:n + 1, :]
                 pb = p.astype(BF)
-                gb = (p * (dp_s[slot, n] - coef[4 + n:5 + n, :]) * 0.125).astype(BF)
-                o = dotg(pb, kv[slot, rows, cv], 0, 0)
-                dq = dotg(gb, kv[slot, rows, ck], 0, 0)
-                for which, x in ((0, o), (1, dq)):
-                    x = jnp.where(mask, x, 0.0)
-                    x = (x[0:32] + x[32:64]) + (x[64:96] + x[96:128])
-                    od[slot, which, T * j:T * (j + 1), ck] = x
-                    if which == 1:
-                        bias[me, pl.ds(grp, 1), ck] += jnp.sum(x, axis=0, keepdims=True)
+                gb = (p * (dp_s[slot, n] - coef[B4 + n:B4 + n + 1, :]) * 0.125).astype(BF)
                 dk = jnp.dot(gb, qb, preferred_element_type=F32)
                 dv = jnp.dot(pb, db, preferred_element_type=F32)
                 dkv[slot, rows, ck] = dk.astype(BF)
                 dkv[slot, rows, cv] = dv.astype(BF)
                 bias[me, pl.ds(grp, 1), cv] += jnp.sum(dv, axis=0, keepdims=True)
-
-    def step(i, do_a, do_b):
+                blocks.append((j, h, pb, gb))
+        return blocks
+
+    def sums(i, blocks):
+        mask = block_mask()
+        for j, h, pb, gb in blocks:
+            rows = slice(FP * j, FP * (j + 1))
+            ck, cv = slice(QW * h, QW * (h + 1)), slice(W + QW * h, W + QW * (h + 1))
+            for which, x in ((0, dotg(pb, kv[i % 3, rows, cv], 0, 0)), (1, dotg(gb, kv[i % 3, rows, ck], 0, 0))):
+                x = jnp.where(mask, x, 0.0)
+                x = (x[0:32] + x[32:64]) + (x[64:96] + x[96:128])
+                od[i % 2, which, T * j:T * (j + 1), ck] = x
+                if which == 1:
+                    bias[me, pl.ds(i // NP, 1), ck] += jnp.sum(x, axis=0, keepdims=True)
+
+    def keep_copy(n):
+        return pltpu.make_async_copy(frames.at[n % 2], mp_hbm.at[n % B4], keep_sem)
+
+    def load_copy(n):
+        return pltpu.make_async_copy(mp_hbm.at[n % B4], frames.at[n % 2], load_sem)
+
+    def tiles(i, do_sort):
+        n = i // B4
+        if do_sort:
+            raw_copy(i + B4).wait()
+
+            @pl.when(i + B4 + 1 < NP)
+            def _():
+                raw_copy(i + B4 + 1).start()
+
+        @pl.when(i % B4 == 0)
+        def _():
+            @pl.when((n >= 1) & (n <= B4))
+            def _():
+                keep_copy(n - 1).wait()
+
+            @pl.when(n < B4)
+            def _():
+                keep_copy(n).start()
+
+            if not do_sort:
+                @pl.when(n >= B4)
+                def _():
+                    load_copy(n).wait()
+
+                @pl.when((n >= B4 - 1) & (n < B8 - 1))
+                def _():
+                    load_copy(n + 1).start()
+
+    def step(i, do_a, do_b, do_sort, mode):
         b = i - 2
         if do_b:
             @pl.when(b >= NP)
@@ -497,33 +549,33 @@
 
             stat_wait(b)
 
-            @pl.when(b >= 2)
+            @when(on(mode, b, 2))
             def _():
                 dkv_copy(b - 2).wait()
 
-            od_pre(b, True)
+            od_wait(b, mode)
         if do_a:
-            @pl.when(i + B4 < STEPS)
-            def _():
-                raw_copy(i + B4).wait()
-
-            @pl.when(i + B4 + 1 < STEPS)
-            def _():
-                raw_copy(i + B4 + 1).start()
-
+            tiles(i, do_sort)
         if do_b:
+            od_sum(b, mode)
             combine(b)
-            stage_b(b)
         if do_a:
-            stage_a(i)
-            sort_frames(i + B4)
+            project(i)
+        if do_b:
+            blocks = grads(b)
+        if do_a:
+            scores(i)
+            if do_sort:
+                sort_frames(i + B4)
         if do_b:
             acc[b // NP] += jnp.dot(mt[b % 3], dkv[b % 2], preferred_element_type=F32)
+            sums(b, blocks)
         if do_a:
             stat_send(i)
         if do_b:
             dkv_copy(b).start()
-            od_post(b, True)
+            s1(b).start()
+            od_send(b, mode)
 
     barrier = pltpu.get_barrier_semaphore()
     for k in range(1, B4):
@@ -540,38 +592,46 @@
     perm[...] = permutation(FC)
     bv32[...] = vec(bv)
     bias[me] = jnp.zeros((B8, D), F32)
-    for cp in loads[:-2]:
+    for cp in loads[:3]:
         cp.wait()
 
     def first(n, carry):
-        raw_copy(n).wait()
-        raw_copy(n + 1).start()
         rows = pl.ds(pl.multiple_of(RC * n, RC), RC)
         x_hat, _ = norm_parts(res[0, rows].astype(F32))
         x = (x_hat * vec(gain) + vec(shift)).astype(BF)
         q[rows] = (jnp.dot(x[:, :ROWS], kv[0], preferred_element_type=F32)
                    + jnp.dot(x[:, ROWS:], dkv[0, rest], preferred_element_type=F32) + vec(bq)).astype(BF)
-        do[rows, :ROWS] = dotg(res[1, rows], kv[1], 1, 1).astype(BF)
-        do[rows, ROWS:] = dotg(res[1, rows], dkv[1, rest], 1, 1).astype(BF)
-        sort_frames(n)
         for g in range(2):
             acc[g, rows] = jnp.zeros((RC, D), F32)
         return carry
 
+    def second(n, carry):
+        raw_copy(n).wait()
+        raw_copy(n + 1).start()
+        rows = pl.ds(pl.multiple_of(RC * n, RC), RC)
+        sort_frames(n)
+        do[rows, :ROWS] = dotg(res[1, rows], kv[1], 1, 1).astype(BF)
+        do[rows, ROWS:] = dotg(res[1, rows], dkv[1, rest], 1, 1).astype(BF)
+        return carry
+
     lax.fori_loop(0, TOK // RC, first, 0)
+    for cp in loads[3:-2]:
+        cp.wait()
+    lax.fori_loop(0, TOK // RC, second, 0)
     for cp in loads[-2:]:
         cp.wait()
     pl.semaphore_wait(barrier, 3)
 
-    def run(lo, hi, do_a, do_b):
+    def run(lo, hi, *what):
         def body(i, carry):
-            step(i, do_a, do_b)
+            step(i, *what)
             return carry
         lax.fori_loop(lo, hi, body, 0)
 
-    run(0, 2, True, False)
-    run(2, STEPS, True, True)
-    run(STEPS, STEPS + 2, False, True)
+    run(0, 2, True, False, True, FILL)
+    run(2, NP - B4, True, True, True, FILL)
+    run(NP - B4, STEPS, True, True, False, ALL)
+    run(STEPS, STEPS + 2, False, True, False, ALL)
 
     def b_copy(k, src):
         return remote(bias.at[src], bias.at[src], b_send.at[k - 1], b_recv.at[src], (me + k) % 4)
@@ -611,8 +671,9 @@
         @pl.when(u < B4)
         def _():
             for k in range(2):
-                od_pre(STEPS + 2 * u + k, False)
-                od_post(STEPS + 2 * u + k, False)
+                od_wait(STEPS + 2 * u + k, DRAIN)
+                od_sum(STEPS + 2 * u + k, DRAIN)
+                od_send(STEPS + 2 * u + k, DRAIN)
 
         exchange(1, u + 1, T3[1], T4[1])
 
@@ -635,8 +696,10 @@
 
         w = jnp.concatenate([wk[:, :W], wv[:, :W], wk[:, W:], wv[:, W:]], axis=1)
         for k in range(2):
-            x = jnp.concatenate([part(u, 2 * k)[...], part(u, 2 * k + 1)[...]], axis=1)
-            (kv, dkv)[k][u % 2] = dotg(x, w, 1, 1).astype(BF)
+            for j in range(2):
+                rows = slice(FP * j, FP * (j + 1))
+                x = jnp.concatenate([part(u, 2 * k)[rows], part(u, 2 * k + 1)[rows]], axis=1)
+                (kv, dkv)[k][u % 2, rows] = dotg(x, w, 1, 1).astype(BF)
         for k in range(2):
             dm_copy(u, k).start()
         return carry
@@ -671,17 +734,17 @@
     return pl.pallas_call(
         attn_kernel, name="attention",
         out_shape=(SDS((B2, TOK, D), BF), SDS((B2, D, D), F32), SDS((2 * B8, W), F32), SDS((NP, ROWS, D), BF),
-                   SDS((B2, NP, ROWS, D), BF)),
+                   SDS((B2, NP, ROWS, D), BF), SDS((B4, B8 * FP, D), BF)),
         in_specs=[hbm] * 7 + [vm] * B4,
-        out_specs=(hbm,) * 5,
+        out_specs=(hbm,) * 6,
         scratch_shapes=[
             VMEM((B2, FP, B8, QW), BF), VMEM((QW, QW), BF), VMEM((1, D), F32), VMEM((B2, B8 * FP, D), BF), mat, mat, mat, mat,
-            VMEM((B2, ROWS, D), BF), probs, probs, VMEM((3, D, ROWS), BF), VMEM((B4, B4, 2 * B8, LANES), F32),
+            VMEM((3, ROWS, D), BF), probs, probs, VMEM((3, D, ROWS), BF), VMEM((B4, B4, 2 * B8, LANES), F32),
             VMEM((B8, LANES), F32), VMEM((B2, ROWS, D), BF), VMEM((B2, D, D), F32), VMEM((B4, B8, D), F32),
             VMEM((B2, B2, 2 * T, W), F32), VMEM((B4, 2 * T, W), F32), rows32, rows32, VMEM((B8, T, W), F32),
             VMEM((B2, TOK, D), BF), VMEM((D, W), F32), VMEM((B2, D // 2, W), F32),
             d2, d8, d2, dma((B2, B2)), d4, d4, d4, d4, d4, d8, d8, dma, dma((2 * B8,)), dma, dma, dma, d2, d2, dn, dn, dn, dn, dn, dn, d2, d4, d4,
-            credit, credit],
+            dma, dma, credit, credit],
         compiler_params=pltpu.CompilerParams(vmem_limit_bytes=67043328, collective_id=0, has_side_effects=True),
     )(mt, h, dy, w_q, w_o, w_k, w_v, gain, shift, b_q, b_v)
 
@@ -697,7 +760,7 @@
     def device_step(hidden, memory, ln_gain, ln_bias, w_q, b_q, w_k, w_v, b_v, w_o, b_o, grad_y):
         h = hidden.reshape(TOK, D)
         dy = grad_y.reshape(TOK, D)
-        res, dw, bias, dm, _ = attention(memory.transpose(1, 0, 2), h, dy, w_q, w_o, w_k, w_v, ln_gain, ln_bias, b_q, b_v)
+        res, dw, bias, dm, _, _ = attention(memory.transpose(1, 0, 2), h, dy, w_q, w_o, w_k, w_v, ln_gain, ln_bias, b_q, b_v)
         gm, y, gh, gwo, gwq, gwk, gwv, dg, db, dbq, dbv, dbo = finish(
             dm.reshape(NB, FP, D), res, h, dy, w_o, w_q, dw, bias, ln_gain, ln_bias, b_o)
         return (y.reshape(NB, T, D), gh.reshape(NB, T, D), gm.transpose(1, 0, 2), dg, db, gwq, dbq, gwk, gwv, dbv, gwo, dbo)

time: 299 us -> 292 us (0.977)
  Pallas kernels: 293 us -> 286 us
    pallas_call x1, Pallas kernels: 260 us -> 254 us  [attention(): pl.pallas_call(attn_kernel, name='attention', out_shape=(SDS((B2, TOK, D)...]
where the time goes in v8:
time: 292 us; the launch traced here: 291 us
  Pallas kernels  286 us (98%)
  local copies, waits for them, and re-layouts  4.39 us (2%)
    pallas_call x1, Pallas kernels, attention(): pl.pallas_call(attn_kernel, name='attention', out_shape=(SDS((B2, TOK, D)...  254 us
    pallas_call x1, Pallas kernels, finish(): pl.pallas_call(finish_kernel, name='finish', out_shape=(SDS((F, NB, D), B...  32.7 us

profile of v8, /device:TPU:0, one launch (start us, length us, event | category | flops | bytes accessed | tf_op | source)
XLA Modules:
  0.0 291.5 jit_solution(8655599839865764080)
XLA Ops:
  0.6 253.5 %attention.1 = (bf16[2,1024,1024]{2,1,0:T(8,128)(2,1)}, f32[2,1024,1024]{2,1,0:T(8,128)}, f32[16,512]{1,0:T(8,128)}, bf16[16,768,1024]{2,1,0:T(8,128)(2,1)}, bf1...) custom-call(bf16[375,32,1024]{2,1,0:T(8,128)(2,1)} %bitcast.10, bf16[1024,1024]{1,0:T(8,128)(2,1)} %bitcast.7, ...), custom_call_target="tpu_custom_call" | custom-call | tf_op jit(solution)/shard_map/attention/pallas_call | solution.py:734
  254.2 0.0 copy-start
  254.2 1.6 copy-done
  255.8 0.0 copy-start.1
  255.8 0.8 copy-done.1
  256.5 0.0 copy-start.2
  256.6 0.7 copy-done.2
  257.2 0.0 copy-start.3
  257.2 0.7 copy-done.3
  257.9 0.0 copy-start.4
  257.9 0.7 copy-done.4
  258.6 32.7 %finish.1 = (bf16[375,32,1024]{2,1,0:T(8,128)(2,1)}, bf16[1024,1024]{1,0:T(8,128)(2,1)}, bf16[1024,1024]{1,0:T(8,128)(2,1)}, f32[1024,1024]{1,0:T(8,128)}, f32[1...) custom-call(bf16[32,384,1024]{2,1,0:T(8,128)(2,1)} %bitcast.9, ...), custom_call_target="tpu_custom_call" | custom-call | tf_op jit(solution)/shard_map/finish/pallas_call | solution.py:212
Async XLA Ops:
  254.2 1.6 copy-start
  255.8 0.8 copy-start.1
  256.5 0.7 copy-start.2
  257.2 0.7 copy-start.3
  257.9 0.7 copy-start.4

commit v9 on v8

--- a/solution.py
+++ b/solution.py
@@ -217,7 +217,7 @@
         scratch_shapes=[
             VMEM((B4, NB, FB, D), BF), VMEM((B4, FB, NB, D), BF), VMEM((QW, QW), BF), VMEM((B2, TOK, D), BF), mat, mat, mat, mat, mat,
             mat, mat, VMEM((JOBS, RC, D), F32), VMEM((B2, D, W), F32), VMEM((B8, D), F32), dj, dj, dma((B8,)), dj, dj, dj, d2, d2],
-        compiler_params=pltpu.CompilerParams(vmem_limit_bytes=50 << 20),
+        compiler_params=pltpu.CompilerParams(vmem_limit_bytes=67043328),
     )(dm, res, h, dy, w_o, w_q, dw, bias, gain, shift, b_o)
 
 
@@ -237,7 +237,7 @@
 
 CH = (64, 128)
 NCH = tuple(D // 2 // rows for rows in CH)
-T3, T4 = (8, 4), (11, 6)
+T3, T4 = 4, 8
 
 
 ALL, FILL, DRAIN = range(3)
@@ -429,6 +429,32 @@
         chunk(t3 - 1, sent)
         chunk(t3, reduce_chip)
         chunk(t4, forward)
+
+    def exchange_first(t):
+        @pl.when(t == 0)
+        def _():
+            e1(0).start()
+
+        @pl.when(t == 1)
+        def _():
+            e1(0).wait_send()
+            pl.semaphore_signal(free_sib.at[0], inc=1, device_id={"cp": sib}, device_id_type=MESH)
+            e1(0).wait_recv()
+
+        @pl.when((t >= 1) & (t < 12) & (t % 3 != 0))
+        def _():
+            reduce_core(0, t - 1 - t // 3)
+
+        @pl.when((t >= 5) & (t < 13))
+        def _():
+            sent(0, t - 5)
+
+        @pl.when(t >= 12)
+        def _():
+            @pl.when(t == 12)
+            def _():
+                pl.semaphore_wait(free_sib.at[0], 1)
+            reduce_chip(0, t - 12)
 
     def operands(i, j, h):
         cols = pl.ds(pl.multiple_of(W * (i // NP) + 256 * h, 256), 256)
@@ -545,7 +571,7 @@
         if do_b:
             @pl.when(b >= NP)
             def _():
-                exchange(0, b - NP, T3[0], T4[0])
+                exchange_first(b - NP)
 
             stat_wait(b)
 
@@ -652,7 +678,7 @@
 
     for k in range(B4):
         c_load(0, k).start()
-    exchange(1, 0, T3[1], T4[1])
+    exchange(1, 0, T3, T4)
 
     def c_step(u, carry):
         for k in range(B4):
@@ -675,16 +701,22 @@
                 od_sum(STEPS + 2 * u + k, DRAIN)
                 od_send(STEPS + 2 * u + k, DRAIN)
 
-        exchange(1, u + 1, T3[1], T4[1])
-
-        @pl.when(u == 1)
-        def _():
-            for n in range(NP - T4[0], NCH[0]):
-                forward(0, n)
-
-        @pl.when(u == 3)
+        for v in range(2):
+            @pl.when(u == v)
+            def _():
+                for k in range(2):
+                    reduce_chip(0, B4 + 2 * v + k)
+
+            @pl.when(u == 1 + 2 * v)
+            def _():
+                for n in range(B4):
+                    forward(0, B4 * v + n)
+
+        @pl.when(u == 5)
         def _():
             gathered(0)
+
+        exchange(1, u + 1, T3, T4)
 
         @pl.when(u == 6)
         def _():
@@ -705,8 +737,8 @@
         return carry
 
     lax.fori_loop(0, NP // 2, c_step, 0)
-    for t in range(NP // 2 + 1, T4[1] + NCH[1]):
-        exchange(1, t, T3[1], T4[1])
+    for t in range(NP // 2 + 1, T4 + NCH[1]):
+        exchange(1, t, T3, T4)
     gathered(1)
     for k in range(1, 4):
         b_copy(k, (me + k) % 4).wait_recv()

time: 292 us -> 291 us (level)
  local copies, waits for them, and re-layouts: 4.39 us -> 0 us
  Pallas kernels: 286 us -> 290 us
    unnamed x10 -> x0, local copies, waits for them, and re-layouts: 4.39 us -> none
where the time goes in v9:
time: 291 us
  Pallas kernels  290 us (100%)
    pallas_call x1, Pallas kernels, attention(): pl.pallas_call(attn_kernel, name='attention', out_shape=(SDS((B2, TOK, D)...  256 us
    pallas_call x1, Pallas kernels, finish(): pl.pallas_call(finish_kernel, name='finish', out_shape=(SDS((F, NB, D), B...  33.6 us

profile of v9, /device:TPU:0, one launch (start us, length us, event | category | flops | bytes accessed | tf_op | source)
XLA Modules:
  0.0 290.7 jit_solution(9979090519099536891)
XLA Ops:
  0.6 256.2 %attention.1 = (bf16[2,1024,1024]{2,1,0:T(8,128)(2,1)}, f32[2,1024,1024]{2,1,0:T(8,128)}, f32[16,512]{1,0:T(8,128)}, bf16[16,768,1024]{2,1,0:T(8,128)(2,1)}, bf1...) custom-call(bf16[375,32,1024]{2,1,0:T(8,128)(2,1)} %bitcast.8, bf16[1024,1024]{1,0:T(8,128)(2,1)} %bitcast.9, ...), custom_call_target="tpu_custom_call" | custom-call | tf_op jit(solution)/shard_map/attention/pallas_call | solution.py:766
  256.9 33.6 %finish.1 = (bf16[375,32,1024]{2,1,0:T(8,128)(2,1)}, bf16[1024,1024]{1,0:T(8,128)(2,1)}, bf16[1024,1024]{1,0:T(8,128)(2,1)}, f32[1024,1024]{1,0:T(8,128)}, f32[1...) custom-call(bf16[32,384,1024]{2,1,0:T(8,128)(2,1)} %bitcast.7, ...), custom_call_target="tpu_custom_call" | custom-call | tf_op jit(solution)/shard_map/finish/pallas_call | solution.py:212

commit v10 on v8

--- a/solution.py
+++ b/solution.py
@@ -54,7 +54,7 @@
     return centered * inv_std, inv_std
 
 
-JOB0, JOBS = 2, 4
+JOB0, JOBS = 6, 4
 FB = 16
 NFB = FP // FB
 
@@ -126,8 +126,6 @@
 
     for k in range(B4 - 1):
         src_copy(k).start()
-    for cp in loads:
-        cp.start()
     piece_in(0).start()
     piece_in(1).start()
     sums[...] = jnp.zeros_like(sums)
@@ -148,6 +146,11 @@
         @pl.when(s >= B4)
         def _():
             dst_copy(s - B4).wait()
+
+        @pl.when(s == 1)
+        def _():
+            for cp in loads:
+                cp.start()
 
         job = s - JOB0
         n = job % JOBS
@@ -174,17 +177,17 @@
             dst_copy(s).start()
 
         for v in range(2):
-            @pl.when(s == JOBS + v)
+            @pl.when(s == 2 + v)
             def _():
                 piece_in(v).wait()
                 piece_out(v).start()
 
-            @pl.when(s == B8 + v)
+            @pl.when(s == JOB0 + v)
             def _():
                 piece_out(v).wait()
                 piece_in(v + 2).start()
 
-            @pl.when(s == B8 + JOBS + v)
+            @pl.when(s == JOB0 + JOBS + v)
             def _():
                 piece_in(v + 2).wait()
                 piece_out(v + 2).start()
@@ -217,7 +220,7 @@
         scratch_shapes=[
             VMEM((B4, NB, FB, D), BF), VMEM((B4, FB, NB, D), BF), VMEM((QW, QW), BF), VMEM((B2, TOK, D), BF), mat, mat, mat, mat, mat,
             mat, mat, VMEM((JOBS, RC, D), F32), VMEM((B2, D, W), F32), VMEM((B8, D), F32), dj, dj, dma((B8,)), dj, dj, dj, d2, d2],
-        compiler_params=pltpu.CompilerParams(vmem_limit_bytes=50 << 20),
+        compiler_params=pltpu.CompilerParams(vmem_limit_bytes=67043328),
     )(dm, res, h, dy, w_o, w_q, dw, bias, gain, shift, b_o)
 
 
@@ -585,8 +588,7 @@
     loads = [pltpu.make_async_copy(x, y, in_sem.at[k]) for k, (x, y) in enumerate((
         (h_hbm, res.at[0]), (wq_hbm.at[top], kv.at[0]), (wq_hbm.at[low], dkv.at[0, rest]), (dy_hbm, res.at[1]),
         (wo_hbm.at[top], kv.at[1]), (wo_hbm.at[low], dkv.at[1, rest]), (wk_hbm, wk), (wv_hbm, wv)))]
-    raw_copy(0).start()
-    for cp in loads:
+    for cp in loads[:3]:
         cp.start()
     raw[:, F:] = jnp.zeros((B2, FP - F, B8, QW), BF)
     perm[...] = permutation(FC)
@@ -594,6 +596,9 @@
     bias[me] = jnp.zeros((B8, D), F32)
     for cp in loads[:3]:
         cp.wait()
+    for cp in loads[3:]:
+        cp.start()
+    raw_copy(0).start()
 
     def first(n, carry):
         rows = pl.ds(pl.multiple_of(RC * n, RC), RC)
@@ -739,7 +744,7 @@
         out_specs=(hbm,) * 6,
         scratch_shapes=[
             VMEM((B2, FP, B8, QW), BF), VMEM((QW, QW), BF), VMEM((1, D), F32), VMEM((B2, B8 * FP, D), BF), mat, mat, mat, mat,
-            VMEM((3, ROWS, D), BF), probs, probs, VMEM((3, D, ROWS), BF), VMEM((B4, B4, 2 * B8, LANES), F32),
+            VMEM((3, ROWS, D), BF), probs, probs, VMEM((3, D, ROWS), BF), VMEM((B4, B4, 3 * B4, LANES), F32),
             VMEM((B8, LANES), F32), VMEM((B2, ROWS, D), BF), VMEM((B2, D, D), F32), VMEM((B4, B8, D), F32),
             VMEM((B2, B2, 2 * T, W), F32), VMEM((B4, 2 * T, W), F32), rows32, rows32, VMEM((B8, T, W), F32),
             VMEM((B2, TOK, D), BF), VMEM((D, W), F32), VMEM((B2, D // 2, W), F32),

time: 292 us -> 288 us (0.986)
  local copies, waits for them, and re-layouts: 4.39 us -> 0 us
    unnamed x10 -> x0, local copies, waits for them, and re-layouts: 4.39 us -> none
where the time goes in v10:
time: 288 us
  Pallas kernels  287 us (100%)
    pallas_call x1, Pallas kernels, attention(): pl.pallas_call(attn_kernel, name='attention', out_shape=(SDS((B2, TOK, D)...  252 us
    pallas_call x1, Pallas kernels, finish(): pl.pallas_call(finish_kernel, name='finish', out_shape=(SDS((F, NB, D), B...  34.5 us

profile of v10, /device:TPU:0, one launch (start us, length us, event | category | flops | bytes accessed | tf_op | source)
XLA Modules:
  0.0 287.7 jit_solution(6317439215371225696)
XLA Ops:
  0.6 252.4 %attention.1 = (bf16[2,1024,1024]{2,1,0:T(8,128)(2,1)}, f32[2,1024,1024]{2,1,0:T(8,128)}, f32[16,512]{1,0:T(8,128)}, bf16[16,768,1024]{2,1,0:T(8,128)(2,1)}, bf1...) custom-call(bf16[375,32,1024]{2,1,0:T(8,128)(2,1)} %bitcast.8, bf16[1024,1024]{1,0:T(8,128)(2,1)} %bitcast.9, ...), custom_call_target="tpu_custom_call" | custom-call | tf_op jit(solution)/shard_map/attention/pallas_call | solution.py:739
  253.0 34.5 %finish.1 = (bf16[375,32,1024]{2,1,0:T(8,128)(2,1)}, bf16[1024,1024]{1,0:T(8,128)(2,1)}, bf16[1024,1024]{1,0:T(8,128)(2,1)}, f32[1024,1024]{1,0:T(8,128)}, f32[1...) custom-call(bf16[32,384,1024]{2,1,0:T(8,128)(2,1)} %bitcast.7, ...), custom_call_target="tpu_custom_call" | custom-call | tf_op jit(solution)/shard_map/finish/pallas_call | solution.py:215

commit v11 on v8

--- a/solution.py
+++ b/solution.py
@@ -67,14 +67,14 @@
         ((h_hbm, h), (res_hbm, res), (wo_hbm, wo), (dy_hbm, dy), (wq_hbm, wq)))]
 
     def src_copy(s):
-        return pltpu.make_async_copy(dm_hbm.at[:, pl.ds(pl.multiple_of(FB * s, FB), FB)], src.at[s % B4], src_sem.at[s % B4])
+        return pltpu.make_async_copy(dm_hbm.at[:, pl.ds(pl.multiple_of(FB * s, FB), FB)], src.at[s % B8], src_sem.at[s % B8])
 
     def dst_copy(s):
-        return pltpu.make_async_copy(dst.at[s % B4], gm_hbm.at[pl.ds(FB * s, FB)], dst_sem.at[s % B4])
+        return pltpu.make_async_copy(dst.at[s % B8], gm_hbm.at[pl.ds(FB * s, FB)], dst_sem.at[s % B8])
 
     def last_copy():
         s = NFB - 1
-        return pltpu.make_async_copy(dst.at[s % B4, 0:F - FB * s], gm_hbm.at[FB * s:F], dst_sem.at[s % B4])
+        return pltpu.make_async_copy(dst.at[s % B8, 0:F - FB * s], gm_hbm.at[FB * s:F], dst_sem.at[s % B8])
 
     def rows(n):
         return pl.ds(pl.multiple_of(RC * n, RC), RC)
@@ -98,9 +98,9 @@
 
     def move(s):
         for k in range(NB // FB):
-            z = src[s % B4, FB * k:FB * (k + 1)].reshape(QW, D)
+            z = src[s % B8, FB * k:FB * (k + 1)].reshape(QW, D)
             z = jnp.dot(perm[...], z, preferred_element_type=F32)
-            dst[s % B4, :, FB * k:FB * (k + 1), :] = z.astype(BF).reshape(FB, FB, D)
+            dst[s % B8, :, FB * k:FB * (k + 1), :] = z.astype(BF).reshape(FB, FB, D)
 
     def job_y(n):
         hf = h[rows(n)].astype(F32)
@@ -124,7 +124,7 @@
     def job_wq(n):
         gw[n] = dotg(x[:, rows(n)], res[1], 0, 0)
 
-    for k in range(B4 - 1):
+    for k in range(B8 - 1):
         src_copy(k).start()
     for cp in loads:
         cp.start()
@@ -141,13 +141,13 @@
     def step(s, carry):
         src_copy(s).wait()
 
-        @pl.when(s + B4 - 1 < NFB)
-        def _():
-            src_copy(s + B4 - 1).start()
-
-        @pl.when(s >= B4)
-        def _():
-            dst_copy(s - B4).wait()
+        @pl.when(s + B8 - 1 < NFB)
+        def _():
+            src_copy(s + B8 - 1).start()
+
+        @pl.when(s >= B8)
+        def _():
+            dst_copy(s - B8).wait()
 
         job = s - JOB0
         n = job % JOBS
@@ -200,7 +200,7 @@
         gw_copy(gwq_hbm, k).wait()
     piece_out(2).wait()
     piece_out(3).wait()
-    for k in range(2, JOBS + 1):
+    for k in range(2, B8 + 1):
         dst_copy(NFB - k).wait()
     last_copy().wait()
 
@@ -208,16 +208,16 @@
 def finish(dm, res, h, dy, w_o, w_q, dw, bias, gain, shift, b_o):
     hbm, vm = pl.BlockSpec(memory_space=pl.ANY), pl.BlockSpec(memory_space=VMEM)
     dma = pltpu.SemaphoreType.DMA
-    mat, dj, d2, vec = VMEM((D, D), BF), dma((JOBS,)), dma((B2,)), SDS((D,), F32)
+    mat, dj, d2, d8, vec = VMEM((D, D), BF), dma((JOBS,)), dma((B2,)), dma((B8,)), SDS((D,), F32)
     return pl.pallas_call(
         finish_kernel, name="finish",
         out_shape=(SDS((F, NB, D), BF), SDS((TOK, D), BF), SDS((TOK, D), BF)) + (SDS((D, D), F32),) * B4 + (vec,) * (B4 + 1),
         in_specs=[hbm] * (B8 - 1) + [vm] * B4,
         out_specs=(hbm,) * (B8 - 1) + (vm,) * (B4 + 1),
         scratch_shapes=[
-            VMEM((B4, NB, FB, D), BF), VMEM((B4, FB, NB, D), BF), VMEM((QW, QW), BF), VMEM((B2, TOK, D), BF), mat, mat, mat, mat, mat,
-            mat, mat, VMEM((JOBS, RC, D), F32), VMEM((B2, D, W), F32), VMEM((B8, D), F32), dj, dj, dma((B8,)), dj, dj, dj, d2, d2],
-        compiler_params=pltpu.CompilerParams(vmem_limit_bytes=50 << 20),
+            VMEM((B8, NB, FB, D), BF), VMEM((B8, FB, NB, D), BF), VMEM((QW, QW), BF), VMEM((B2, TOK, D), BF), mat, mat, mat, mat, mat,
+            mat, mat, VMEM((JOBS, RC, D), F32), VMEM((B2, D, W), F32), VMEM((B8, D), F32), d8, d8, d8, dj, dj, dj, d2, d2],
+        compiler_params=pltpu.CompilerParams(vmem_limit_bytes=67043328),
     )(dm, res, h, dy, w_o, w_q, dw, bias, gain, shift, b_o)
 
 
@@ -237,7 +237,8 @@
 
 CH = (64, 128)
 NCH = tuple(D // 2 // rows for rows in CH)
-T3, T4 = (8, 4), (11, 6)
+TS = (7, 3)
+T3, T4 = (10, 4), (13, 6)
 
 
 ALL, FILL, DRAIN = range(3)
@@ -248,7 +249,7 @@
                 raw, perm, bv32, frames, q, do, wk, wv, kv, e_s, dp_s, mt, stats, coef, dkv, acc, bias, od, r1, keep, x2, r2, res, big1, big2,
                 raw_sem, in_sem, dkv_sem, dm_sem, out_sem, st_send, st_recv, s1_send, s1_recv, s2_send, s2_recv,
                 s3_send, s3_recv, s3s_send, s4_send, res_recv, e1_send, e1_recv, e2_send, e2_recv,
-                e3_send, e3_recv, e3s_send, e4_send, acc_recv, b_send, b_recv, keep_sem, load_sem, free_sib, free_xn):
+                e3_send, e3_recv, e3s_send, e4_send, acc_recv, b_send, b_recv, keep_sem, load_sem, e1p_send, e1p_recv, free_sib, free_xn):
     me = lax.axis_index("cp")
     cx, cc = me // 2, me % 2
     sib, xn = 2 * cx + 1 - cc, 2 * (1 - cx) + cc
@@ -359,6 +360,14 @@
     def e1(g):
         return remote(acc.at[g, :, other], big1, e1_send.at[g], e1_recv.at[g], sib)
 
+    def e1_part(n, x):
+        rows = rows_of(1, x, n)
+        return remote(acc.at[1, rows, other], big1.at[rows], e1p_send.at[n], e1p_recv.at[n], sib)
+
+    def e1_wait(n, sem):
+        both = big1.at[0:2 * CH[1]]
+        pltpu.make_async_copy(both, both, sem.at[n]).wait()
+
     def e2(g, n):
         return remote(acc.at[g, rows_of(g, 1 - cx, n), own], chunk_of(g, n), e2_send.at[g, n], e2_recv.at[g, n], xn)
 
@@ -374,6 +383,8 @@
         return pltpu.make_async_copy(acc.at[g], dw_hbm.at[g], out_sem.at[g])
 
     def reduce_core(g, n):
+        if g == 1:
+            e1_wait(n, e1p_recv)
         for x in (cx, 1 - cx):
             acc[g, rows_of(g, x, n), own] += big1[rows_of(g, x, n), :]
         e2(g, n).start()
@@ -413,20 +424,29 @@
 
         @when(t == 0)
         def _():
-            e1(g).start()
-
-        @when(t == 1)
-        def _():
-            e1(g).wait_send()
+            if g == 0:
+                e1(g).start()
+            else:
+                for n in range(NCH[1]):
+                    e1_part(n, 0).start()
+                    e1_part(n, 1).start()
+
+        @when(t == 1 + g)
+        def _():
+            if g == 0:
+                e1(g).wait_send()
+                e1(g).wait_recv()
+            else:
+                for n in range(NCH[1]):
+                    e1_wait(n, e1p_send)
             pl.semaphore_signal(free_sib.at[g], inc=1, device_id={"cp": sib}, device_id_type=MESH)
-            e1(g).wait_recv()
 
         @when(t == t3)
         def _():
             pl.semaphore_wait(free_sib.at[g], 1)
 
         chunk(1, reduce_core)
-        chunk(t3 - 1, sent)
+        chunk(TS[g], sent)
         chunk(t3, reduce_chip)
         chunk(t4, forward)
 
@@ -585,8 +605,7 @@
     loads = [pltpu.make_async_copy(x, y, in_sem.at[k]) for k, (x, y) in enumerate((
         (h_hbm, res.at[0]), (wq_hbm.at[top], kv.at[0]), (wq_hbm.at[low], dkv.at[0, rest]), (dy_hbm, res.at[1]),
         (wo_hbm.at[top], kv.at[1]), (wo_hbm.at[low], dkv.at[1, rest]), (wk_hbm, wk), (wv_hbm, wv)))]
-    raw_copy(0).start()
-    for cp in loads:
+    for cp in loads[:3]:
         cp.start()
     raw[:, F:] = jnp.zeros((B2, FP - F, B8, QW), BF)
     perm[...] = permutation(FC)
@@ -594,6 +613,9 @@
     bias[me] = jnp.zeros((B8, D), F32)
     for cp in loads[:3]:
         cp.wait()
+    for cp in loads[3:]:
+        cp.start()
+    raw_copy(0).start()
 
     def first(n, carry):
         rows = pl.ds(pl.multiple_of(RC * n, RC), RC)
@@ -677,12 +699,17 @@
 
         exchange(1, u + 1, T3[1], T4[1])
 
-        @pl.when(u == 1)
+        @pl.when(u == 0)
+        def _():
+            for n in range(NP - T3[0], NCH[0]):
+                reduce_chip(0, n)
+
+        @pl.when(u == 2)
         def _():
             for n in range(NP - T4[0], NCH[0]):
                 forward(0, n)
 
-        @pl.when(u == 3)
+        @pl.when(u == 4)
         def _():
             gathered(0)
 
@@ -739,12 +766,12 @@
         out_specs=(hbm,) * 6,
         scratch_shapes=[
             VMEM((B2, FP, B8, QW), BF), VMEM((QW, QW), BF), VMEM((1, D), F32), VMEM((B2, B8 * FP, D), BF), mat, mat, mat, mat,
-            VMEM((3, ROWS, D), BF), probs, probs, VMEM((3, D, ROWS), BF), VMEM((B4, B4, 2 * B8, LANES), F32),
+            VMEM((3, ROWS, D), BF), probs, probs, VMEM((3, D, ROWS), BF), VMEM((B4, B4, 3 * B4, LANES), F32),
             VMEM((B8, LANES), F32), VMEM((B2, ROWS, D), BF), VMEM((B2, D, D), F32), VMEM((B4, B8, D), F32),
             VMEM((B2, B2, 2 * T, W), F32), VMEM((B4, 2 * T, W), F32), rows32, rows32, VMEM((B8, T, W), F32),
             VMEM((B2, TOK, D), BF), VMEM((D, W), F32), VMEM((B2, D // 2, W), F32),
             d2, d8, d2, dma((B2, B2)), d4, d4, d4, d4, d4, d8, d8, dma, dma((2 * B8,)), dma, dma, dma, d2, d2, dn, dn, dn, dn, dn, dn, d2, d4, d4,
-            dma, dma, credit, credit],
+            dma, dma, d4, d4, credit, credit],
         compiler_params=pltpu.CompilerParams(vmem_limit_bytes=67043328, collective_id=0, has_side_effects=True),
     )(mt, h, dy, w_q, w_o, w_k, w_v, gain, shift, b_q, b_v)
 

time: 292 us -> 284 us (0.973)
  local copies, waits for them, and re-layouts: 4.39 us -> 0 us
  Pallas kernels: 286 us -> 283 us
    unnamed x10 -> x0, local copies, waits for them, and re-layouts: 4.39 us -> none
where the time goes in v11:
time: 284 us
  Pallas kernels  283 us (100%)
    pallas_call x1, Pallas kernels, attention(): pl.pallas_call(attn_kernel, name='attention', out_shape=(SDS((B2, TOK, D)...  252 us
    pallas_call x1, Pallas kernels, finish(): pl.pallas_call(finish_kernel, name='finish', out_shape=(SDS((F, NB, D), B...  30.8 us

profile of v11, /device:TPU:0, one launch (start us, length us, event | category | flops | bytes accessed | tf_op | source)
XLA Modules:
  0.0 284.1 jit_solution(14608093267462029815)
XLA Ops:
  0.6 252.4 %attention.1 = (bf16[2,1024,1024]{2,1,0:T(8,128)(2,1)}, f32[2,1024,1024]{2,1,0:T(8,128)}, f32[16,512]{1,0:T(8,128)}, bf16[16,768,1024]{2,1,0:T(8,128)(2,1)}, bf1...) custom-call(bf16[375,32,1024]{2,1,0:T(8,128)(2,1)} %bitcast.8, bf16[1024,1024]{1,0:T(8,128)(2,1)} %bitcast.9, ...), custom_call_target="tpu_custom_call" | custom-call | tf_op jit(solution)/shard_map/attention/pallas_call | solution.py:761
  253.1 30.8 %finish.1 = (bf16[375,32,1024]{2,1,0:T(8,128)(2,1)}, bf16[1024,1024]{1,0:T(8,128)(2,1)}, bf16[1024,1024]{1,0:T(8,128)(2,1)}, f32[1024,1024]{1,0:T(8,128)}, f32[1...) custom-call(bf16[32,384,1024]{2,1,0:T(8,128)(2,1)} %bitcast.7, ...), custom_call_target="tpu_custom_call" | custom-call | tf_op jit(solution)/shard_map/finish/pallas_call | solution.py:212
